TPU v7x, 32 devices: a whole 2x2x4 slice. The times are simulated.
32 devices in a mesh: tm: 4 (over z), space: 8 (over y, x, core).
Axes of the slice: x: 2, y: 2, z: 4, core: 2. Of those that a mesh axis runs over, the one named last changes fastest.
Arguments:
- eigvecs: bfloat16 [4, 128, 2, 3, 32, 512], P('tm', None, None, None, 'space'), may hold values from -0.29882812 to 0.29882812
- gauge_links: float32 [4, 3, 2, 3, 3, 32, 512], P('tm', None, None, None, None, 'space'), may hold values from -1 to 1, as said below
- perambulator: bfloat16 [8, 4, 2, 128, 128], P('tm'), may hold values from -0.375 to 0.375
- job_owner: int32 [96, 1], replicated, may hold values from 0 to 3; in each aligned block of 24 rows (0 to 23, 24 to 47, ...) at most 18 rows name the same one
- job_elemental: int32 [96], replicated, may hold values from 0 to 3
- job_source: int32 [96], replicated, may hold values from 0 to 1
- job_spin: int32 [96], replicated, may hold values from 0 to 3
Outputs:
- dressed: bfloat16 [4, 4, 18, 2, 128, 128], P('tm', None, None, None, 'space')
Inputs may be any that keep to these rules, and one draw needn't show every extreme that they name: `gauge_links`: each site's and direction's 3x3 complex matrix is special unitary. `job_owner`: jobs come in aligned blocks of 24 rows, block s holding the jobs of timeslice group s (timeslice s); within one block no owner is named by more than 18 rows, a bound that some block reaches. `job_elemental`: the job's timeslice within its group times 4 plus its operator (0 the momentum-projected plain elemental, 1 to 3 the derivatives along x1, x2, x3). `job_source`: the job's source time among its owner's 2 source times.
All inputs are finite; a program needn't handle non-finite values.
Results may differ from a plain program's by a relative error of at most 0.0057.
Values may be sent and summed in bfloat16 or wider, within the bound.
No kernel may reach another device: no remote copies, remote signals or barrier semaphores. Data moves between devices by JAX's collectives and lax.ppermute only.
A program may use at most 128 MiB of HBM per device.

v0:
```python
import math
from functools import partial

import numpy as np
import jax
import jax.numpy as jnp
from jax import lax
from jax.experimental import pallas as pl
from jax.experimental.pallas import tpu as pltpu
from jax.sharding import PartitionSpec as P

LY = 16
LZ = 32
OPS = 4
SPIN = 4
JOB_DEV = 24
LANES = 128
GROUP = 16
F32 = jnp.float32
BF16 = jnp.bfloat16
VMEM = pltpu.VMEM
SMEM = pltpu.SMEM


def vspec():
    return pl.BlockSpec(memory_space=VMEM)


def sspec():
    return pl.BlockSpec(memory_space=SMEM)


def cost(flops, moved):
    return pl.CostEstimate(flops=flops, bytes_accessed=moved, transcendentals=0)


def pick_matrix(rows, cols, source_of):
    row = lax.broadcasted_iota(jnp.int32, (rows, cols), 0)
    col = lax.broadcasted_iota(jnp.int32, (rows, cols), 1)
    return jnp.where(col == source_of(row), 1.0, 0.0).astype(BF16)


def nt_dot(left, right):
    return lax.dot_general(left, right, (((1,), (1,)), ((), ())), preferred_element_type=F32)


def rim_kernel(tiles, planes, x_ref, out_ref):
    spots = tiles * planes

    def source(row):
        return (row % GROUP) * spots + (row // GROUP) * planes

    chosen = pick_matrix(tiles * GROUP, GROUP * spots, source)
    block = x_ref[...].reshape(GROUP, 6, spots, LANES)
    for part in range(6):
        rows = block[:, part].reshape(GROUP * spots, LANES)
        taken = jnp.dot(chosen, rows, preferred_element_type=F32).astype(BF16)
        for tile in range(tiles):
            out_ref[part * tiles + tile] = taken[tile * GROUP : (tile + 1) * GROUP]


def rim_plane(x, count, tiles, planes):
    spots = tiles * planes
    return pl.pallas_call(
        partial(rim_kernel, tiles, planes),
        grid=(count // GROUP,),
        in_specs=[pl.BlockSpec((GROUP * 6 * spots, LANES), lambda g: (g, 0))],
        out_specs=pl.BlockSpec((6 * tiles, GROUP, LANES), lambda g: (0, g, 0)),
        out_shape=jax.ShapeDtypeStruct((6 * tiles, count, LANES), BF16),
        cost_estimate=cost(10**8, 4 * 10**6),
        name="rim",
    )(x)


def link_product(links, vec):
    outs_re, outs_im = [], []
    for row in range(3):
        total_re = None
        for col in range(3):
            link_re, link_im = links[0][row][col], links[1][row][col]
            part_re = link_re * vec[0][col] - link_im * vec[1][col]
            part_im = link_re * vec[1][col] + link_im * vec[0][col]
            if total_re is None:
                total_re, total_im = part_re, part_im
            else:
                total_re, total_im = total_re + part_re, total_im + part_im
        outs_re.append(total_re)
        outs_im.append(total_im)
    return outs_re, outs_im


def load_links(u_ref, direction, spot, spots):
    def one(part, row, col):
        at = (((direction * 2 + part) * 3 + row) * 3 + col) * spots + spot
        return jnp.broadcast_to(u_ref[pl.ds(at, 1), :], (8, LANES))

    return [[[one(part, row, col) for col in range(3)] for row in range(3)] for part in range(2)]


def paired(grid, count):
    real = grid[:count, :count] + grid[count:, count:]
    imag = grid[:count, count:] - grid[count:, :count]
    return real, imag


def anti(real, imag):
    return 0.5 * (real - real.T), 0.5 * (imag + imag.T)


def gram_kernel(
    count, tiles, planes, lx, x_ref, u_ref, phase_ref, sums_ref, rim_lhs_ref, v_ref, lhs_ref, op_ref, acc_ref, g_ref
):
    spots = tiles * planes
    groups = count // GROUP
    blocks = count // 8
    pair = 2
    steps = planes * (tiles // pair)

    def source(row):
        spot = row // GROUP
        return (row % GROUP) * spots + (spot % tiles) * planes + spot // tiles

    chosen = pick_matrix(GROUP * spots, GROUP * spots, source)

    def regroup(group, carry):
        start = pl.multiple_of(group * GROUP * 6 * spots, GROUP * 6 * spots)
        block = x_ref[pl.ds(start, GROUP * 6 * spots), :].reshape(GROUP, 6, spots, LANES)
        at = pl.multiple_of(group * GROUP, GROUP)
        for part in range(6):
            rows = block[:, part].reshape(GROUP * spots, LANES)
            taken = jnp.dot(chosen, rows, preferred_element_type=F32)
            half, colour = part // 3, part % 3
            for spot in range(spots):
                piece = taken[spot * GROUP : (spot + 1) * GROUP]
                v_ref[spot * 6 + part, pl.ds(at, GROUP), :] = piece
                plane, tile = spot // tiles, spot % tiles
                lhs_ref[
                    plane * (tiles // pair) + tile // pair,
                    pl.ds(half * count + at, GROUP),
                    ((tile % pair) * 3 + colour) * LANES : ((tile % pair) * 3 + colour + 1) * LANES,
                ] = piece.astype(BF16)
        return carry

    lax.fori_loop(0, groups, regroup, 0)
    for k in range(tiles * 6):
        v_ref[spots * 6 + k] = jnp.zeros((count, LANES), F32)
    acc_ref[...] = jnp.zeros_like(acc_ref)
    g_ref[...] = jnp.zeros_like(g_ref)

    lane = lax.broadcasted_iota(jnp.int32, (8, LANES), 1)
    wraps = (lane % LZ) == LZ - 1
    spills = lane < LZ

    def elementwise(step, slot):
        plane = step // (tiles // pair)
        half_tile = step % (tiles // pair)
        for sub in range(pair):
            tile = half_tile * pair + sub
            spot = plane * tiles + tile
            next_tile = plane * tiles + lax.rem(tile + 1, tiles)
            for direction in range(3):
                links = load_links(u_ref, direction, tile * planes + plane, spots)
                for block in range(blocks):
                    at = block * 8
                    if direction == 0:
                        base = (spot + tiles) * 6
                        parts = [v_ref[base + k, at : at + 8, :] for k in range(6)]
                    elif direction == 1:
                        parts = []
                        for k in range(6):
                            here = v_ref[spot * 6 + k, at : at + 8, :]
                            there = v_ref[next_tile * 6 + k, at : at + 8, :]
                            parts.append(pltpu.roll(jnp.where(spills, there, here), LANES - LZ, 1))
                    else:
                        parts = []
                        for k in range(6):
                            here = v_ref[spot * 6 + k, at : at + 8, :]
                            parts.append(
                                jnp.where(wraps, pltpu.roll(here, LZ - 1, 1), pltpu.roll(here, LANES - 1, 1))
                            )
                    outs = link_product(links, (parts[:3], parts[3:]))
                    for half in range(2):
                        for colour in range(3):
                            op_ref[
                                slot,
                                direction,
                                half * count + at : half * count + at + 8,
                                (sub * 3 + colour) * LANES : (sub * 3 + colour + 1) * LANES,
                            ] = outs[half][colour].astype(BF16)

    def multiply(step, slot):
        left = lhs_ref[step]
        plane = step // (tiles // pair)
        g_ref[plane] += nt_dot(left, left)
        for direction in range(3):
            acc_ref[direction] += nt_dot(left, op_ref[slot, direction])

    elementwise(0, 0)

    def body(step, carry):
        slot = lax.rem(step, 2)
        multiply(step - 1, 1 - slot)
        elementwise(step, slot)
        return carry

    lax.fori_loop(1, steps, body, 0)
    multiply(steps - 1, (steps - 1) % 2)

    first = lax.axis_index("space") * planes
    total_re = jnp.zeros((count, count), F32)
    total_im = jnp.zeros((count, count), F32)
    for plane in range(planes):
        real, imag = paired(g_ref[plane], count)
        cosine = phase_ref[first + plane]
        sine = phase_ref[lx + first + plane]
        total_re += cosine * real + sine * imag
        total_im += cosine * imag - sine * real
    sums_ref[0, 0] = total_re
    sums_ref[0, 1] = total_im
    for direction in range(3):
        real, imag = anti(*paired(acc_ref[direction], count))
        sums_ref[direction + 1, 0] = real
        sums_ref[direction + 1, 1] = imag
    for half in range(tiles // pair):
        rim_lhs_ref[half] = lhs_ref[(planes - 1) * (tiles // pair) + half]


def gram(x, u, phases, count, tiles, planes, lx):
    spots = tiles * planes
    pair = 2
    steps = planes * (tiles // pair)
    return pl.pallas_call(
        partial(gram_kernel, count, tiles, planes, lx),
        in_specs=[vspec(), vspec(), sspec()],
        out_specs=[vspec(), vspec()],
        out_shape=[
            jax.ShapeDtypeStruct((OPS, 2, count, count), F32),
            jax.ShapeDtypeStruct((tiles // pair, 2 * count, pair * 3 * LANES), BF16),
        ],
        scratch_shapes=[
            VMEM(((spots + tiles) * 6, count, LANES), F32),
            VMEM((steps, 2 * count, pair * 3 * LANES), BF16),
            VMEM((2, 3, 2 * count, pair * 3 * LANES), BF16),
            VMEM((3, 2 * count, 2 * count), F32),
            VMEM((planes, 2 * count, 2 * count), F32),
        ],
        compiler_params=pltpu.CompilerParams(vmem_limit_bytes=40 * 2**20),
        cost_estimate=cost(8 * 10**9, 5 * 10**6),
        name="gram",
    )(x, u, phases)


def edge_kernel(
    count, tiles, planes, rows, cores, halo_ref, lhs_ref, u_ref, sums_ref, keep_ref, send_ref, op_ref, tot_ref
):
    spots = tiles * planes
    blocks = count // GROUP
    pair = 2
    total = None
    for half_tile in range(tiles // pair):
        for sub in range(pair):
            tile = half_tile * pair + sub
            links = load_links(u_ref, 0, tile * planes + planes - 1, spots)

            for block in range(blocks):
                at = block * GROUP
                parts = [
                    halo_ref[k * tiles + tile, at : at + GROUP, :].astype(F32) for k in range(6)
                ]
                for eight in range(2):
                    vecs = [piece[eight * 8 : eight * 8 + 8] for piece in parts]
                    outs = link_product(links, (vecs[:3], vecs[3:]))
                    for half in range(2):
                        for colour in range(3):
                            start = half * count + at + eight * 8
                            op_ref[
                                half_tile,
                                start : start + 8,
                                (sub * 3 + colour) * LANES : (sub * 3 + colour + 1) * LANES,
                            ] = outs[half][colour].astype(BF16)
        got = nt_dot(lhs_ref[half_tile], op_ref[half_tile])
        total = got if total is None else total + got
    real, imag = anti(*paired(total, count))
    tot_ref[0] = real
    tot_ref[1] = imag
    mine = lax.rem(lax.axis_index("space"), cores)
    for chip in range(count // (rows * cores)):
        for which, ref in ((mine, keep_ref), (1 - mine, send_ref)):
            at = pl.multiple_of((chip * cores + which) * rows, rows)
            for op in range(OPS):
                for half in range(2):
                    piece = sums_ref[op, half, pl.ds(at, rows), :]
                    if op == 1:
                        piece = piece + tot_ref[half, pl.ds(at, rows), :]
                    ref[chip, op, half] = piece


def edge(halo, rim_lhs, u, sums, count, tiles, planes, rows, cores):
    pair = 2
    shape = jax.ShapeDtypeStruct((count // (rows * cores), OPS, 2, rows, count), F32)
    return pl.pallas_call(
        partial(edge_kernel, count, tiles, planes, rows, cores),
        in_specs=[vspec()] * 4,
        out_specs=[vspec(), vspec()],
        out_shape=[shape, shape],
        scratch_shapes=[
            VMEM((tiles // pair, 2 * count, pair * 3 * LANES), BF16),
            VMEM((2, count, count), F32),
        ],
        cost_estimate=cost(10**9, 3 * 10**6),
        name="edge",
    )(halo, rim_lhs, u, sums)


def fold_kernel(chips, keep_ref, got_ref, own_ref, *out_refs):
    me = lax.axis_index("space") // 2
    own_ref[...] = keep_ref[me] + got_ref[me]
    for step in range(1, chips):
        to = me ^ step
        out_refs[step - 1][...] = keep_ref[to] + got_ref[to]


def fold(keep, got):
    chips = keep.shape[0]
    shape = jax.ShapeDtypeStruct(keep.shape[1:], F32)
    return pl.pallas_call(
        partial(fold_kernel, chips),
        in_specs=[vspec()] * 2,
        out_specs=[vspec()] * chips,
        out_shape=[shape] * chips,
        cost_estimate=cost(10**6, 10**6),
        name="fold",
    )(keep, got)


def total_kernel(*refs):
    total = refs[0][...]
    for ref in refs[1:-1]:
        total = total + ref[...]
    refs[-1][...] = total.astype(BF16)


def total_rows(parts):
    return pl.pallas_call(
        total_kernel,
        in_specs=[vspec()] * len(parts),
        out_specs=vspec(),
        out_shape=jax.ShapeDtypeStruct(parts[0].shape, BF16),
        cost_estimate=cost(10**6, 10**6),
        name="total",
    )(*parts)


def table_kernel(groups, jobs, slots, empty, owner_ref, elem_ref, source_ref, spin_ref, out_ref):
    me = lax.axis_index("tm")

    def clear(at, carry):
        out_ref[at] = empty
        return carry

    lax.fori_loop(0, groups * slots + 1, clear, 0)
    for group in range(groups):

        def place(job, used):
            at = group * jobs + job
            mine = owner_ref[at] == me
            product = (source_ref[at] * SPIN + spin_ref[at]) * (groups * OPS) + group * OPS + elem_ref[at]
            spot = jnp.where(mine, group * slots + used, groups * slots)
            out_ref[spot] = product
            return used + mine.astype(jnp.int32)

        lax.fori_loop(0, jobs, place, jnp.int32(0))


def job_table(owner, elem, source, spin, groups, slots, empty):
    jobs = owner.shape[0] // groups
    return pl.pallas_call(
        partial(table_kernel, groups, jobs, slots, empty),
        in_specs=[sspec()] * 4,
        out_specs=sspec(),
        out_shape=jax.ShapeDtypeStruct((groups * slots + 1,), jnp.int32),
        cost_estimate=cost(10**5, 10**4),
        name="table",
    )(owner, elem, source, spin)


def dress_kernel(groups, slots, taus, rows, count, table_ref, per_ref, *refs):
    slab_refs = refs[:groups]
    out_ref, lhs_ref, prod_ref = refs[groups:]
    me = lax.axis_index("tm")
    for step in range(groups):
        group = me ^ step
        for op in range(OPS):
            at = pl.multiple_of((group * OPS + op) * rows, rows)
            lhs_ref[pl.ds(at, rows), 0:count] = slab_refs[step][op, 0]
            lhs_ref[pl.ds(at, rows), count : 2 * count] = slab_refs[step][op, 1]
    left = lhs_ref[...]
    for tau in range(taus):
        real, imag = per_ref[tau, 0], per_ref[tau, 1]
        right = jnp.concatenate(
            [jnp.concatenate([real, imag], axis=1), jnp.concatenate([-imag, real], axis=1)], axis=0
        )
        got = jnp.dot(left, right, preferred_element_type=F32).astype(BF16)
        for piece in range(groups * OPS):
            prod_ref[tau * groups * OPS + piece] = got[piece * rows : (piece + 1) * rows]
    prod_ref[taus * groups * OPS] = jnp.zeros((rows, 2 * count), BF16)
    for group in range(groups):
        for slot in range(slots):
            piece = prod_ref[table_ref[group * slots + slot]]
            out_ref[group, slot, 0] = piece[:, :count]
            out_ref[group, slot, 1] = piece[:, count:]


def dress(table, per, slabs, groups, slots, rows, count):
    taus = per.shape[0]
    return pl.pallas_call(
        partial(dress_kernel, groups, slots, taus, rows, count),
        in_specs=[sspec(), vspec()] + [vspec()] * groups,
        out_specs=vspec(),
        out_shape=jax.ShapeDtypeStruct((groups, slots, 2, rows, count), BF16),
        scratch_shapes=[
            VMEM((groups * OPS * rows, 2 * count), BF16),
            VMEM((taus * groups * OPS + 1, rows, 2 * count), BF16),
        ],
        cost_estimate=cost(10**9, 2 * 10**6),
        name="dress",
    )(table, per, *slabs)


def fast_shards(eigvecs, gauge_links, perambulator, job_owner, job_elemental, job_source, job_spin):
    count = eigvecs.shape[1]
    planes, sites = eigvecs.shape[4], eigvecs.shape[5]
    tiles = sites // LANES
    space_size = lax.axis_size("space")
    groups = lax.axis_size("tm")
    lx = planes * space_size
    rows = count // space_size
    slots = 3 * ((JOB_DEV + groups - 1) // groups)
    cores = 2

    def tiled(field):
        head = field.shape[:-2]
        order = tuple(range(len(head))) + (len(head) + 1, len(head), len(head) + 2)
        split = field.reshape(head + (planes, tiles, LANES))
        return split.transpose(order).reshape(-1, LANES)

    x = tiled(eigvecs)
    u = tiled(gauge_links)
    angle = 2.0 * math.pi / lx * np.arange(lx)
    phases = jnp.asarray(np.concatenate([np.cos(angle), np.sin(angle)]).astype(np.float32))

    rim = rim_plane(x, count, tiles, planes)
    halo = lax.ppermute(rim, "space", [(i, (i - 1) % space_size) for i in range(space_size)])
    sums, rim_lhs = gram(x, u, phases, count, tiles, planes, lx)
    per = perambulator.reshape(-1, 2, count, count)
    table = job_table(
        job_owner.reshape(-1), job_elemental, job_source, job_spin, groups, slots, per.shape[0] * groups * OPS
    )
    keep, send = edge(halo, rim_lhs, u, sums, count, tiles, planes, rows, cores)
    got = lax.ppermute(send, "space", [(i, i ^ 1) for i in range(space_size)])
    parts = fold(keep, got)
    summed = [parts[0]]
    for step in range(1, space_size // cores):
        summed.append(
            lax.ppermute(parts[step], "space", [(i, i ^ (step * cores)) for i in range(space_size)])
        )
    own = total_rows(summed)
    slabs = [own]
    for step in range(1, groups):
        slabs.append(lax.ppermute(own, "tm", [(i, i ^ step) for i in range(groups)]))
    return dress(table, per, slabs, groups, slots, rows, count)[None]


def passed_along(shard, axis, by):
    count = lax.axis_size(axis)
    return lax.ppermute(shard, axis, [(i, (i + by) % count) for i in range(count)])


def shifted_sites(lattice_field, direction, offset):
    shaped = lattice_field.reshape(lattice_field.shape[:-1] + (LY, LZ))
    rolled = jnp.roll(shaped, -offset, axis=direction - 4)
    return rolled.reshape(lattice_field.shape)


def apply_link(link_field, vectors):
    total_re = None
    total_im = None
    for colour in range(3):
        link_re = link_field[0, :, colour][None]
        link_im = link_field[1, :, colour][None]
        vector_re = vectors[:, 0, colour][:, None]
        vector_im = vectors[:, 1, colour][:, None]
        part_re = link_re * vector_re - link_im * vector_im
        part_im = link_re * vector_im + link_im * vector_re
        if colour == 0:
            total_re, total_im = (part_re, part_im)
        else:
            total_re = total_re + part_re
            total_im = total_im + part_im
    return jnp.stack([total_re, total_im], axis=1)


def stacked_form(vectors):
    vector_count = vectors.shape[0]
    swapped = jnp.concatenate([-vectors[:, 1:2], vectors[:, 0:1]], axis=1)
    return jnp.concatenate(
        [vectors.reshape(vector_count, -1), swapped.reshape(vector_count, -1)], axis=0
    )


def paired_gram(stacked, lattice_field):
    vector_count = lattice_field.shape[0]
    flat_field = lattice_field.astype(jnp.bfloat16).reshape(vector_count, -1)
    product = lax.dot_general(
        stacked, flat_field, (((1,), (1,)), ((), ())), preferred_element_type=jnp.float32
    )
    return product.reshape(2, vector_count, vector_count)


def twisted_field(vectors, xcoord):
    phase_angle = 2.0 * math.pi / (vectors.shape[3] * lax.axis_size("space")) * xcoord
    cosine = jnp.cos(phase_angle)[:, None]
    sine_part = jnp.sin(phase_angle)[:, None]
    real_part = cosine * vectors[:, 0] + sine_part * vectors[:, 1]
    imag_part = cosine * vectors[:, 1] - sine_part * vectors[:, 0]
    return jnp.stack([real_part, imag_part], axis=1)


def antihermitian(paired):
    return 0.5 * jnp.stack([paired[0] - paired[0].T, paired[1] + paired[1].T], axis=0)


def plain_shards(eigvecs, gauge_links, perambulator, job_owner, job_elemental, job_source, job_spin):
    slice_count = eigvecs.shape[0]
    vector_count = eigvecs.shape[1]
    planes = eigvecs.shape[4]
    space_size = lax.axis_size("space")
    group_count = lax.axis_size("tm")
    row_count = vector_count // space_size
    capacity = 3 * ((JOB_DEV + group_count - 1) // group_count)
    xcoord = (lax.axis_index("space") * planes + jnp.arange(planes, dtype=jnp.int32)).astype(
        jnp.float32
    )
    upper_plane = passed_along(eigvecs[:, :, :, :, 0:1], "space", -1)
    low_vectors = eigvecs[0]
    vectors = low_vectors.astype(jnp.float32)
    stacked = stacked_form(low_vectors)
    results = [paired_gram(stacked, twisted_field(vectors, xcoord))]
    for direction in (1, 2, 3):
        link_field = gauge_links[0, direction - 1]
        if direction == 1:
            upper_rim = upper_plane[0].astype(jnp.float32)
            above_field = jnp.concatenate([vectors[:, :, :, 1:], upper_rim], axis=3)
        else:
            above_field = shifted_sites(vectors, direction, 1)
        forward = apply_link(link_field, above_field)
        results.append(antihermitian(paired_gram(stacked, forward)))
    partial_list = [jnp.stack(results, axis=0)]
    partial_value = jnp.stack(partial_list, axis=0)
    summed = lax.psum(partial_value, "space")
    own_rows = lax.dynamic_slice_in_dim(summed, lax.axis_index("space") * row_count, row_count, 3)
    slab_table = own_rows.astype(jnp.bfloat16).reshape(
        slice_count * OPS, 2 * row_count * vector_count
    )
    owners = job_owner[:, 0].reshape(group_count, -1)
    elements = job_elemental.reshape(group_count, -1)
    position = jnp.arange(owners.shape[1], dtype=jnp.int32)
    earlier = position[None, :] < position[:, None]
    same_owner = owners[:, :, None] == owners[:, None, :]
    slot_rank = jnp.sum(jnp.where(same_owner & earlier[None], 1, 0), axis=2).astype(jnp.int32)
    own_group = lax.axis_index("tm")
    slot_count = group_count * capacity
    live_jobs = owners == own_group
    slot_match = live_jobs[:, None, :] & (
        slot_rank[:, None, :] == jnp.arange(capacity, dtype=jnp.int32)[None, :, None]
    )
    sender_owners = lax.dynamic_index_in_dim(owners, own_group, 0, keepdims=False)
    sender_ranks = lax.dynamic_index_in_dim(slot_rank, own_group, 0, keepdims=False)
    sender_elements = lax.dynamic_index_in_dim(elements, own_group, 0, keepdims=False)
    slot_ids = sender_owners * capacity + sender_ranks
    slot_hot = (jnp.arange(slot_count, dtype=jnp.int32)[:, None] == slot_ids[None, :]).astype(
        jnp.float32
    )
    elem_hot = (
        sender_elements[:, None] == jnp.arange(slice_count * OPS, dtype=jnp.int32)[None, :]
    ).astype(jnp.float32)
    picker = jnp.dot(slot_hot, elem_hot, precision=lax.Precision.HIGHEST).astype(jnp.bfloat16)
    outgoing = jnp.dot(picker, slab_table, preferred_element_type=jnp.float32).astype(jnp.bfloat16)
    outgoing = outgoing.reshape(group_count, capacity, 2, row_count, vector_count)
    received = lax.all_to_all(outgoing, "tm", split_axis=0, concat_axis=0, tiled=True)
    block_index = job_source.reshape(group_count, -1) * SPIN + job_spin.reshape(group_count, -1)
    tau_index = jnp.sum(jnp.where(slot_match, block_index[:, None, :], 0), axis=2)
    blocks = perambulator.reshape(-1, 2 * vector_count, vector_count)
    chosen = jnp.take(blocks, tau_index.reshape(-1), axis=0)
    slab_rows = received.reshape(slot_count, 2, row_count, vector_count)
    real_rows = jnp.concatenate([slab_rows[:, 0], -slab_rows[:, 1]], axis=-1)
    imag_rows = jnp.concatenate([slab_rows[:, 1], slab_rows[:, 0]], axis=-1)
    left_side = jnp.stack([real_rows, imag_rows], axis=1).reshape(
        slot_count, 2 * row_count, 2 * vector_count
    )
    dressed = lax.dot_general(
        left_side, chosen, (((2,), (1,)), ((0,), (0,))), preferred_element_type=jnp.float32
    )
    return dressed.astype(jnp.bfloat16).reshape(
        1, group_count, capacity, 2, row_count, vector_count
    )


def shards(*args):
    eigvecs = args[0]
    count, planes, sites = eigvecs.shape[1], eigvecs.shape[4], eigvecs.shape[5]
    space_size, groups = lax.axis_size("space"), lax.axis_size("tm")
    whole_tiles = sites % (2 * LANES) == 0 and count == LANES and planes * (sites // LANES) == GROUP
    powers = space_size & (space_size - 1) == 0 and groups & (groups - 1) == 0
    small = space_size * GROUP == count and groups <= 8
    if whole_tiles and powers and small and eigvecs.shape[0] == 1:
        return fast_shards(*args)
    return plain_shards(*args)


def solution(mesh):
    return jax.shard_map(
        shards,
        mesh=mesh,
        in_specs=(
            P("tm", None, None, None, "space", None),
            P("tm", None, None, None, None, "space", None),
            P("tm", None, None, None, None),
            P(),
            P(),
            P(),
            P(),
        ),
        out_specs=P("tm", None, None, None, "space", None),
        check_vma=False,
    )
```

profile of v0, /device:TPU:0, one launch (start us, length us, event | category | flops | bytes accessed | tf_op | source)
XLA Modules:
  0.0 56.2 jit_solution(8273667162447797012)
XLA Ops:
  0.0 6.5 %rim.1 = bf16[24,128,128]{2,1,0:T(8,128)(2,1)} custom-call(bf16[12288,128]{1,0:T(8,128)(2,1)} %bitcast.13), custom_call_target="tpu_custom_call" | custom-call | flops 100000000 | bytes 4000000 | tf_op jit(solution)/shard_map/rim/pallas_call | solution.py:64
  6.5 3.4 %collective-permute-start = (bf16[24,128,128]{2,1,0:T(8,128)(2,1)}, bf16[24,128,128]{2,1,0:T(8,128)(2,1)}, u32[]{:S(2)}, u32[]{:S(2)}) collective-permute-start(bf16[24,128,128]{2,1,0:T(8,128)(2,1)} %rim.1), channel_id=1, source_target_pairs={{0,7},{1,0},{2,1},{3,2},{4,3},{5,4},{6,5},{7,6},{8,15},{9,8},{10,9... | collective-permute-start | bytes 2359304 | tf_op jit(solution)/shard_map/ppermute | solution.py:453
  9.8 0.0 copy-done.2
  9.8 1.0 %copy-done.1 = f32[1,3,2,3,3,4,512]{6,5,4,3,2,1,0:T(4,128)S(1)} copy-done((f32[1,3,2,3,3,4,512]{6,5,4,3,2,1,0:T(4,128)S(1)}, f32[1,3,2,3,3,4,512]{6,5,4,3,2,1,0:T(4,128)}, u32[]{:S(2)}) %copy-start.1) | copy-done | bytes 442392
  10.9 15.4 %gram.1 = (f32[4,2,128,128]{3,2,1,0:T(8,128)S(1)}, bf16[2,256,768]{2,1,0:T(8,128)(2,1)S(1)}) custom-call(bf16[12288,128]{1,0:T(8,128)(2,1)S(1)} %bitcast.14, f32[864,128]{1,0:T(8,128)S(1)} %bitcast.16, f32[64]{0:T(128)S(1)} %copy-done.2), custom_call_target="tpu_custom_call" | custom-call | flops 8000000000 | bytes 5000000 | tf_op jit(solution)/shard_map/gram/pallas_call | solution.py:232
  26.3 0.9 %copy-done.3 = bf16[2,256,768]{2,1,0:T(8,128)(2,1)} copy-done((bf16[2,256,768]{2,1,0:T(8,128)(2,1)}, bf16[2,256,768]{2,1,0:T(8,128)(2,1)S(1)}, u32[]{:S(2)}) %copy-start.3) | copy-done | bytes 786456
  27.2 0.8 %copy-done.4 = f32[4,2,128,128]{3,2,1,0:T(8,128)} copy-done((f32[4,2,128,128]{3,2,1,0:T(8,128)}, f32[4,2,128,128]{3,2,1,0:T(8,128)S(1)}, u32[]{:S(2)}) %copy-start.4) | copy-done | bytes 524312
  28.0 0.0 collective-permute-done.halo_ref
  28.0 3.5 %edge.1 = (f32[4,4,2,16,128]{4,3,2,1,0:T(8,128)}, f32[4,4,2,16,128]{4,3,2,1,0:T(8,128)}) custom-call(bf16[24,128,128]{2,1,0:T(8,128)(2,1)} %collective-permute-done.halo_ref, bf16[2,256,768]{2,1,0:T(8,128)(2,1)} %copy-done.3, f32[864,128]{1,0:T(8,128)} %bitcast.15, f32[4,2,128,128]{3,2,1,0:T(8,128)} %copy-done.4), custom_call_target="tpu_custom_call" | custom-call | flops 1000000000 | bytes 3000000 | tf_op jit(solution)/shard_map/edge/pallas_call | solution.py:301
  31.5 0.0 collective-permute-start.1
  31.5 1.7 %collective-permute-done.1.got_ref = f32[4,4,2,16,128]{4,3,2,1,0:T(8,128)S(1)} collective-permute-done((f32[4,4,2,16,128]{4,3,2,1,0:T(8,128)}, f32[4,4,2,16,128]{4,3,2,1,0:T(8,128)S(1)}, u32[]{:S(2)}, u32[]{:S(2)}) %collective-permute-start.1) | collective-permute-done | bytes 262176 | tf_op jit(solution)/shard_map/ppermute | solution.py:460
  33.3 0.7 %copy-done.5 = f32[4,4,2,16,128]{4,3,2,1,0:T(8,128)} copy-done((f32[4,4,2,16,128]{4,3,2,1,0:T(8,128)}, f32[4,4,2,16,128]{4,3,2,1,0:T(8,128)S(1)}, u32[]{:S(2)}) %copy-start.5) | copy-done | bytes 262168
  34.0 1.7 %fold.1 = (f32[4,2,16,128]{3,2,1,0:T(8,128)}, f32[4,2,16,128]{3,2,1,0:T(8,128)}, f32[4,2,16,128]{3,2,1,0:T(8,128)}, f32[4,2,16,128]{3,2,1,0:T(8,128)}) custom-call(f32[4,4,2,16,128]{4,3,2,1,0:T(8,128)} %get-tuple-element.15.keep_ref, f32[4,4,2,16,128]{4,3,2,1,0:T(8,128)} %copy-done.5), custom_call_target="tpu_custom_call" | custom-call | flops 1000000 | bytes 1000000 | tf_op jit(solution)/shard_map/fold/pallas_call | solution.py:326
  35.7 0.0 collective-permute-start.2
  35.7 1.2 %collective-permute-start.3 = (f32[4,2,16,128]{3,2,1,0:T(8,128)}, f32[4,2,16,128]{3,2,1,0:T(8,128)S(1)}, u32[]{:S(2)}, u32[]{:S(2)}) collective-permute-start(f32[4,2,16,128]{3,2,1,0:T(8,128)} %get-tuple-element.19), channel_id=1, source_target_pairs={{0,4},{1,5},{2,6},{3,7},{4,0},{5,1},{6,2},{7,3},{8,12},{9,13},{10,... | collective-permute-start | bytes 196616 | tf_op jit(solution)/shard_map/ppermute | solution.py:465
  36.9 2.3 %collective-permute-start.4 = (f32[4,2,16,128]{3,2,1,0:T(8,128)}, f32[4,2,16,128]{3,2,1,0:T(8,128)S(1)}, u32[]{:S(2)}, u32[]{:S(2)}) collective-permute-start(f32[4,2,16,128]{3,2,1,0:T(8,128)} %get-tuple-element.20), channel_id=1, source_target_pairs={{0,6},{1,7},{2,4},{3,5},{4,2},{5,3},{6,0},{7,1},{8,14},{9,15},{10,... | collective-permute-start | bytes 196616 | tf_op jit(solution)/shard_map/ppermute | solution.py:465
  39.2 1.3 %collective-permute-done.2.refs_1_ = f32[4,2,16,128]{3,2,1,0:T(8,128)S(1)} collective-permute-done((f32[4,2,16,128]{3,2,1,0:T(8,128)}, f32[4,2,16,128]{3,2,1,0:T(8,128)S(1)}, u32[]{:S(2)}, u32[]{:S(2)}) %collective-permute-start.2) | collective-permute-done | bytes 65568 | tf_op jit(solution)/shard_map/ppermute | solution.py:465
  40.5 0.0 collective-permute-done.3.refs_2_
  40.5 1.8 %collective-permute-done.4.refs_3_ = f32[4,2,16,128]{3,2,1,0:T(8,128)S(1)} collective-permute-done((f32[4,2,16,128]{3,2,1,0:T(8,128)}, f32[4,2,16,128]{3,2,1,0:T(8,128)S(1)}, u32[]{:S(2)}, u32[]{:S(2)}) %collective-permute-start.4) | collective-permute-done | bytes 65568 | tf_op jit(solution)/shard_map/ppermute | solution.py:465
  42.3 0.0 copy-done.7
  42.3 0.6 %copy-done.8 = f32[4,2,16,128]{3,2,1,0:T(8,128)} copy-done((f32[4,2,16,128]{3,2,1,0:T(8,128)}, f32[4,2,16,128]{3,2,1,0:T(8,128)S(1)}, u32[]{:S(2)}) %copy-start.8) | copy-done | bytes 65560
  43.0 1.6 %total.1.refs_0_ = bf16[4,2,16,128]{3,2,1,0:T(8,128)(2,1)} custom-call(f32[4,2,16,128]{3,2,1,0:T(8,128)} %get-tuple-element.17.refs_0_, f32[4,2,16,128]{3,2,1,0:T(8,128)} %copy-done.6, f32[4,2,16,128]{3,2,1,0:T(8,128)} %copy-done.7, f32[4,2,16,128]{3,2,1,0:T(8,128)} %copy-done.8), custom_call_target="tpu_custom_call" | custom-call | flops 1000000 | bytes 1000000 | tf_op jit(solution)/shard_map/total/pallas_call | solution.py:344
  44.5 3.6 %collective-permute-start.7 = (bf16[4,2,16,128]{3,2,1,0:T(8,128)(2,1)}, bf16[4,2,16,128]{3,2,1,0:T(8,128)(2,1)S(1)}, u32[]{:S(2)}, u32[]{:S(2)}) collective-permute-start(bf16[4,2,16,128]{3,2,1,0:T(8,128)(2,1)} %total.1.refs_0_), channel_id=1, source_target_pairs={{0,24},{8,16},{16,8},{24,0},{1,25},{9,17},{17,9},{25,1},{2,26},{10... | collective-permute-start | bytes 98312 | tf_op jit(solution)/shard_map/ppermute | solution.py:470
  48.1 0.0 collective-permute-start.6
  48.1 0.8 %collective-permute-start.5 = (bf16[4,2,16,128]{3,2,1,0:T(8,128)(2,1)}, bf16[4,2,16,128]{3,2,1,0:T(8,128)(2,1)S(1)}, u32[]{:S(2)}, u32[]{:S(2)}) collective-permute-start(bf16[4,2,16,128]{3,2,1,0:T(8,128)(2,1)} %total.1.refs_0_), channel_id=1, source_target_pairs={{0,8},{8,0},{16,24},{24,16},{1,9},{9,1},{17,25},{25,17},{2,10},{10... | collective-permute-start | bytes 98312 | tf_op jit(solution)/shard_map/ppermute | solution.py:470
  48.9 2.6 %table.1.table_ref = s32[73]{0:T(128)} custom-call(s32[96]{0:T(128)} %bitcast.17, s32[96]{0:T(128)} %elem_ref.1, s32[96]{0:T(128)} %source_ref.1, s32[96]{0:T(128)} %spin_ref.1), custom_call_target="tpu_custom_call" | custom-call | flops 100000 | bytes 10000 | tf_op jit(solution)/shard_map/table/pallas_call | solution.py:377
  51.5 0.0 collective-permute-done.7.refs_3_
  51.5 0.0 copy-start.9
  51.5 1.6 %collective-permute-done.6.refs_2_ = bf16[4,2,16,128]{3,2,1,0:T(8,128)(2,1)S(1)} collective-permute-done((bf16[4,2,16,128]{3,2,1,0:T(8,128)(2,1)}, bf16[4,2,16,128]{3,2,1,0:T(8,128)(2,1)S(1)}, u32[]{:S(2)}, u32[]{:S(2)}) %collective-permute-start.6) | collective-permute-done | bytes 32800 | tf_op jit(solution)/shard_map/ppermute | solution.py:470
  53.1 0.0 collective-permute-done.5.refs_1_
  53.1 0.6 %copy-done.10 = bf16[4,2,16,128]{3,2,1,0:T(8,128)(2,1)} copy-done((bf16[4,2,16,128]{3,2,1,0:T(8,128)(2,1)}, bf16[4,2,16,128]{3,2,1,0:T(8,128)(2,1)S(1)}, u32[]{:S(2)}) %copy-start.10) | copy-done | bytes 32792
  53.8 2.5 %dress.1 = bf16[4,18,2,16,128]{4,3,2,1,0:T(8,128)(2,1)} custom-call(s32[73]{0:T(128)} %table.1.table_ref, bf16[8,2,128,128]{3,2,1,0:T(8,128)(2,1)} %bitcast.18, bf16[4,2,16,128]{3,2,1,0:T(8,128)(2,1)} %total.1.refs_0_, bf16[4,2,16,128]{3,2,1,0:T(8,128)(2,1)} %copy-done.11, bf16[4,2,16,128]{3,2,1,0:T(8,128)(2,1)} %copy-done.10, bf16[4,2,16,128]{3,2,1,0:T(8,128)(2,1)} %copy-done.9), custom_call_target="tpu_custom_call" | custom-call | flops 1000000000 | bytes 2000000 | tf_op jit(solution)/shard_map/dress/pallas_call | solution.py:416
  (15 shorter events, 0.0 us)
Async XLA Ops:
  0.0 9.8 %copy-start.2 = (f32[64]{0:T(128)S(1)}, f32[64]{0:T(128)}, u32[]{:S(2)}) copy-start(f32[64]{0:T(128)} %constant.2.clone.phase_ref) | copy-start | bytes 772
  0.0 9.8 %copy-start = (bf16[1,128,2,3,4,512]{5,4,3,2,1,0:T(4,128)(2,1)S(1)}, bf16[1,128,2,3,4,512]{5,4,3,2,1,0:T(4,128)(2,1)}, u32[]{:S(2)}) copy-start(bf16[1,128,2,3,4,512]{5,4,3,2,1,0:T(4,128)(2,1)} %param.8) | copy-start | bytes 9437188
  6.5 21.5 %collective-permute-start = (bf16[24,128,128]{2,1,0:T(8,128)(2,1)}, bf16[24,128,128]{2,1,0:T(8,128)(2,1)}, u32[]{:S(2)}, u32[]{:S(2)}) collective-permute-start(bf16[24,128,128]{2,1,0:T(8,128)(2,1)} %rim.1), channel_id=1, source_target_pairs={{0,7},{1,0},{2,1},{3,2},{4,3},{5,4},{6,5},{7,6},{8,15},{9,8},{10,9... | collective-permute-start | bytes 2359304 | tf_op jit(solution)/shard_map/ppermute | solution.py:453
  9.8 1.0 %copy-start.1 = (f32[1,3,2,3,3,4,512]{6,5,4,3,2,1,0:T(4,128)S(1)}, f32[1,3,2,3,3,4,512]{6,5,4,3,2,1,0:T(4,128)}, u32[]{:S(2)}) copy-start(f32[1,3,2,3,3,4,512]{6,5,4,3,2,1,0:T(4,128)} %param.9) | copy-start | bytes 1327108
  26.3 0.9 %copy-start.3 = (bf16[2,256,768]{2,1,0:T(8,128)(2,1)}, bf16[2,256,768]{2,1,0:T(8,128)(2,1)S(1)}, u32[]{:S(2)}) copy-start(bf16[2,256,768]{2,1,0:T(8,128)(2,1)S(1)} %get-tuple-element.13.lhs_ref) | copy-start | bytes 2359300
  27.2 0.8 %copy-start.4 = (f32[4,2,128,128]{3,2,1,0:T(8,128)}, f32[4,2,128,128]{3,2,1,0:T(8,128)S(1)}, u32[]{:S(2)}) copy-start(f32[4,2,128,128]{3,2,1,0:T(8,128)S(1)} %get-tuple-element.14.sums_ref) | copy-start | bytes 1572868
  31.5 1.7 %collective-permute-start.1 = (f32[4,4,2,16,128]{4,3,2,1,0:T(8,128)}, f32[4,4,2,16,128]{4,3,2,1,0:T(8,128)S(1)}, u32[]{:S(2)}, u32[]{:S(2)}) collective-permute-start(f32[4,4,2,16,128]{4,3,2,1,0:T(8,128)} %get-tuple-element.16), channel_id=1, source_target_pairs={{0,1},{1,0},{2,3},{3,2},{4,5},{5,4},{6,7},{7,6},{8,9},{9,8},{10,11... | collective-permute-start | bytes 786440 | tf_op jit(solution)/shard_map/ppermute | solution.py:460
  33.3 0.7 %copy-start.5 = (f32[4,4,2,16,128]{4,3,2,1,0:T(8,128)}, f32[4,4,2,16,128]{4,3,2,1,0:T(8,128)S(1)}, u32[]{:S(2)}) copy-start(f32[4,4,2,16,128]{4,3,2,1,0:T(8,128)S(1)} %collective-permute-done.1.got_ref) | copy-start | bytes 786436
  35.7 4.8 %collective-permute-start.2 = (f32[4,2,16,128]{3,2,1,0:T(8,128)}, f32[4,2,16,128]{3,2,1,0:T(8,128)S(1)}, u32[]{:S(2)}, u32[]{:S(2)}) collective-permute-start(f32[4,2,16,128]{3,2,1,0:T(8,128)} %get-tuple-element.18), channel_id=1, source_target_pairs={{0,2},{1,3},{2,0},{3,1},{4,6},{5,7},{6,4},{7,5},{8,10},{9,11},{10,... | collective-permute-start | bytes 196616 | tf_op jit(solution)/shard_map/ppermute | solution.py:465
  35.7 4.8 %collective-permute-start.3 = (f32[4,2,16,128]{3,2,1,0:T(8,128)}, f32[4,2,16,128]{3,2,1,0:T(8,128)S(1)}, u32[]{:S(2)}, u32[]{:S(2)}) collective-permute-start(f32[4,2,16,128]{3,2,1,0:T(8,128)} %get-tuple-element.19), channel_id=1, source_target_pairs={{0,4},{1,5},{2,6},{3,7},{4,0},{5,1},{6,2},{7,3},{8,12},{9,13},{10,... | collective-permute-start | bytes 196616 | tf_op jit(solution)/shard_map/ppermute | solution.py:465
  36.9 5.4 %collective-permute-start.4 = (f32[4,2,16,128]{3,2,1,0:T(8,128)}, f32[4,2,16,128]{3,2,1,0:T(8,128)S(1)}, u32[]{:S(2)}, u32[]{:S(2)}) collective-permute-start(f32[4,2,16,128]{3,2,1,0:T(8,128)} %get-tuple-element.20), channel_id=1, source_target_pairs={{0,6},{1,7},{2,4},{3,5},{4,2},{5,3},{6,0},{7,1},{8,14},{9,15},{10,... | collective-permute-start | bytes 196616 | tf_op jit(solution)/shard_map/ppermute | solution.py:465
  40.5 1.8 %copy-start.6 = (f32[4,2,16,128]{3,2,1,0:T(8,128)}, f32[4,2,16,128]{3,2,1,0:T(8,128)S(1)}, u32[]{:S(2)}) copy-start(f32[4,2,16,128]{3,2,1,0:T(8,128)S(1)} %collective-permute-done.2.refs_1_) | copy-start | bytes 196612
  40.5 1.8 %copy-start.7 = (f32[4,2,16,128]{3,2,1,0:T(8,128)}, f32[4,2,16,128]{3,2,1,0:T(8,128)S(1)}, u32[]{:S(2)}) copy-start(f32[4,2,16,128]{3,2,1,0:T(8,128)S(1)} %collective-permute-done.3.refs_2_) | copy-start | bytes 196612
  42.3 0.6 %copy-start.8 = (f32[4,2,16,128]{3,2,1,0:T(8,128)}, f32[4,2,16,128]{3,2,1,0:T(8,128)S(1)}, u32[]{:S(2)}) copy-start(f32[4,2,16,128]{3,2,1,0:T(8,128)S(1)} %collective-permute-done.4.refs_3_) | copy-start | bytes 196612
  44.5 7.0 %collective-permute-start.7 = (bf16[4,2,16,128]{3,2,1,0:T(8,128)(2,1)}, bf16[4,2,16,128]{3,2,1,0:T(8,128)(2,1)S(1)}, u32[]{:S(2)}, u32[]{:S(2)}) collective-permute-start(bf16[4,2,16,128]{3,2,1,0:T(8,128)(2,1)} %total.1.refs_0_), channel_id=1, source_target_pairs={{0,24},{8,16},{16,8},{24,0},{1,25},{9,17},{17,9},{25,1},{2,26},{10... | collective-permute-start | bytes 98312 | tf_op jit(solution)/shard_map/ppermute | solution.py:470
  48.1 5.0 %collective-permute-start.6 = (bf16[4,2,16,128]{3,2,1,0:T(8,128)(2,1)}, bf16[4,2,16,128]{3,2,1,0:T(8,128)(2,1)S(1)}, u32[]{:S(2)}, u32[]{:S(2)}) collective-permute-start(bf16[4,2,16,128]{3,2,1,0:T(8,128)(2,1)} %total.1.refs_0_), channel_id=1, source_target_pairs={{0,16},{8,24},{16,0},{24,8},{1,17},{9,25},{17,1},{25,9},{2,18},{10... | collective-permute-start | bytes 98312 | tf_op jit(solution)/shard_map/ppermute | solution.py:470
  48.1 5.0 %collective-permute-start.5 = (bf16[4,2,16,128]{3,2,1,0:T(8,128)(2,1)}, bf16[4,2,16,128]{3,2,1,0:T(8,128)(2,1)S(1)}, u32[]{:S(2)}, u32[]{:S(2)}) collective-permute-start(bf16[4,2,16,128]{3,2,1,0:T(8,128)(2,1)} %total.1.refs_0_), channel_id=1, source_target_pairs={{0,8},{8,0},{16,24},{24,16},{1,9},{9,1},{17,25},{25,17},{2,10},{10... | collective-permute-start | bytes 98312 | tf_op jit(solution)/shard_map/ppermute | solution.py:470
  51.5 1.6 %copy-start.9 = (bf16[4,2,16,128]{3,2,1,0:T(8,128)(2,1)}, bf16[4,2,16,128]{3,2,1,0:T(8,128)(2,1)S(1)}, u32[]{:S(2)}) copy-start(bf16[4,2,16,128]{3,2,1,0:T(8,128)(2,1)S(1)} %collective-permute-done.7.refs_3_) | copy-start | bytes 98308
  53.1 0.6 %copy-start.10 = (bf16[4,2,16,128]{3,2,1,0:T(8,128)(2,1)}, bf16[4,2,16,128]{3,2,1,0:T(8,128)(2,1)S(1)}, u32[]{:S(2)}) copy-start(bf16[4,2,16,128]{3,2,1,0:T(8,128)(2,1)S(1)} %collective-permute-done.6.refs_2_) | copy-start | bytes 98308
  53.1 0.6 %copy-start.11 = (bf16[4,2,16,128]{3,2,1,0:T(8,128)(2,1)}, bf16[4,2,16,128]{3,2,1,0:T(8,128)(2,1)S(1)}, u32[]{:S(2)}) copy-start(bf16[4,2,16,128]{3,2,1,0:T(8,128)(2,1)S(1)} %collective-permute-done.5.refs_1_) | copy-start | bytes 98308
where the time goes:
time: 56.6 us; the launch traced here: 56.2 us
  Pallas kernels  33.8 us (60%)
  starting transfers between devices  11.2 us (20%)
  waiting for transfers between devices  6.47 us (11%)
  local copies, waits for them, and re-layouts  4.67 us (8%)
    pallas_call x1, Pallas kernels, gram(): pl.pallas_call(partial(gram_kernel, count, tiles, planes, lx), in_specs=[...  15.4 us
    pallas_call x1, Pallas kernels, rim_plane(): pl.pallas_call(partial(rim_kernel, tiles, planes), grid=(count // GROUP,)...  6.46 us
    unnamed x24, local copies, waits for them, and re-layouts  4.67 us
    ppermute x3, starting transfers between devices, fast_shards(): lax.ppermute(own, 'tm', [(i, i ^ step) for i in range(groups)])  4.39 us
    pallas_call x1, Pallas kernels, edge(): pl.pallas_call(partial(edge_kernel, count, tiles, planes, rows, cores), i...  3.52 us
    ppermute x3, starting transfers between devices, fast_shards(): lax.ppermute(parts[step], 'space', [(i, i ^ step * cores) for i in range(...  3.49 us
    ppermute x1, starting transfers between devices, fast_shards(): lax.ppermute(rim, 'space', [(i, (i - 1) % space_size) for i in range(spac...  3.37 us
    ppermute x3, waiting for transfers between devices, fast_shards(): lax.ppermute(parts[step], 'space', [(i, i ^ step * cores) for i in range(...  3.11 us
  transfers between devices with their start and end apart: 8, of which 4 were waited for; matrix products, arithmetic and copies ran while one was open for 0% of the time, Pallas kernels for 32%

commit v1 on v0

--- a/solution.py
+++ b/solution.py
@@ -34,6 +34,10 @@
     return pl.CostEstimate(flops=flops, bytes_accessed=moved, transcendentals=0)
 
 
+def limit(mebibytes):
+    return pltpu.CompilerParams(vmem_limit_bytes=mebibytes * 2**20)
+
+
 def pick_matrix(rows, cols, source_of):
     row = lax.broadcasted_iota(jnp.int32, (rows, cols), 0)
     col = lax.broadcasted_iota(jnp.int32, (rows, cols), 1)
@@ -44,48 +48,71 @@
     return lax.dot_general(left, right, (((1,), (1,)), ((), ())), preferred_element_type=F32)
 
 
-def rim_kernel(tiles, planes, x_ref, out_ref):
+def rim_kernel(tiles, planes, x_hbm, u_hbm, out_ref, x_ref, u_ref, pick_ref, sems):
     spots = tiles * planes
+    chunk = GROUP * 6 * spots
+    chunks = x_hbm.shape[0] // chunk
+    copies = []
+    for g in range(chunks):
+        rows = pl.ds(g * chunk, chunk)
+        copies.append(pltpu.make_async_copy(x_hbm.at[rows], x_ref.at[rows], sems.at[g]))
+    copies.append(pltpu.make_async_copy(u_hbm, u_ref, sems.at[chunks]))
+    for copy in copies:
+        copy.start()
 
     def source(row):
-        return (row % GROUP) * spots + (row // GROUP) * planes
-
-    chosen = pick_matrix(tiles * GROUP, GROUP * spots, source)
-    block = x_ref[...].reshape(GROUP, 6, spots, LANES)
-    for part in range(6):
-        rows = block[:, part].reshape(GROUP * spots, LANES)
-        taken = jnp.dot(chosen, rows, preferred_element_type=F32).astype(BF16)
-        for tile in range(tiles):
-            out_ref[part * tiles + tile] = taken[tile * GROUP : (tile + 1) * GROUP]
-
-
-def rim_plane(x, count, tiles, planes):
+        return (row & (GROUP - 1)) * spots + (row // GROUP) * planes
+
+    pick_ref[...] = pick_matrix(tiles * GROUP, GROUP * spots, source)
+    chosen = pick_ref[...]
+    for g in range(chunks):
+        copies[g].wait()
+        block = x_ref[g * chunk : (g + 1) * chunk, :].reshape(GROUP, 6, spots, LANES)
+        for part in range(0, 6, 2):
+            rows = jnp.concatenate(
+                [block[:, part + k].reshape(GROUP * spots, LANES) for k in range(2)], axis=1
+            )
+            taken = jnp.dot(chosen, rows, preferred_element_type=F32).astype(BF16)
+            for k in range(2):
+                for tile in range(tiles):
+                    out_ref[(part + k) * tiles + tile, g * GROUP : (g + 1) * GROUP] = taken[
+                        tile * GROUP : (tile + 1) * GROUP, k * LANES : (k + 1) * LANES
+                    ]
+    copies[chunks].wait()
+
+
+def rim_plane(x, u, count, tiles, planes):
     spots = tiles * planes
     return pl.pallas_call(
         partial(rim_kernel, tiles, planes),
-        grid=(count // GROUP,),
-        in_specs=[pl.BlockSpec((GROUP * 6 * spots, LANES), lambda g: (g, 0))],
-        out_specs=pl.BlockSpec((6 * tiles, GROUP, LANES), lambda g: (0, g, 0)),
-        out_shape=jax.ShapeDtypeStruct((6 * tiles, count, LANES), BF16),
+        in_specs=[pl.BlockSpec(memory_space=pltpu.HBM)] * 2,
+        out_specs=[vspec()] * 3,
+        out_shape=[
+            jax.ShapeDtypeStruct((6 * tiles, count, LANES), BF16),
+            jax.ShapeDtypeStruct(x.shape, BF16),
+            jax.ShapeDtypeStruct(u.shape, F32),
+        ],
+        scratch_shapes=[
+            VMEM((tiles * GROUP, GROUP * spots), BF16),
+            pltpu.SemaphoreType.DMA((count // GROUP + 1,)),
+        ],
+        compiler_params=limit(8),
         cost_estimate=cost(10**8, 4 * 10**6),
         name="rim",
-    )(x)
-
-
-def link_product(links, vec):
+    )(x, u)
+
+
+def link_product(links, vec_re, vec_im):
+    plus = [vec_re[c] + vec_im[c] for c in range(3)]
+    minus = [vec_im[c] - vec_re[c] for c in range(3)]
     outs_re, outs_im = [], []
     for row in range(3):
-        total_re = None
-        for col in range(3):
-            link_re, link_im = links[0][row][col], links[1][row][col]
-            part_re = link_re * vec[0][col] - link_im * vec[1][col]
-            part_im = link_re * vec[1][col] + link_im * vec[0][col]
-            if total_re is None:
-                total_re, total_im = part_re, part_im
-            else:
-                total_re, total_im = total_re + part_re, total_im + part_im
-        outs_re.append(total_re)
-        outs_im.append(total_im)
+        link_re, link_im, link_sum = links[0][row], links[1][row], links[2][row]
+        one = link_sum[0] * vec_re[0] + link_sum[1] * vec_re[1] + link_sum[2] * vec_re[2]
+        two = link_re[0] * minus[0] + link_re[1] * minus[1] + link_re[2] * minus[2]
+        three = link_im[0] * plus[0] + link_im[1] * plus[1] + link_im[2] * plus[2]
+        outs_re.append(one - three)
+        outs_im.append(one + two)
     return outs_re, outs_im
 
 
@@ -94,117 +121,141 @@
         at = (((direction * 2 + part) * 3 + row) * 3 + col) * spots + spot
         return jnp.broadcast_to(u_ref[pl.ds(at, 1), :], (8, LANES))
 
-    return [[[one(part, row, col) for col in range(3)] for row in range(3)] for part in range(2)]
+    grid = [[[one(part, row, col) for col in range(3)] for row in range(3)] for part in range(2)]
+    total = [[grid[0][row][col] + grid[1][row][col] for col in range(3)] for row in range(3)]
+    return grid + [total]
 
 
 def paired(grid, count):
     real = grid[:count, :count] + grid[count:, count:]
-    imag = grid[:count, count:] - grid[count:, :count]
+    imag = grid[count:, :count] - grid[:count, count:]
     return real, imag
 
 
 def anti(real, imag):
-    return 0.5 * (real - real.T), 0.5 * (imag + imag.T)
+    return 0.5 * (real.T - real), 0.5 * (imag.T + imag)
 
 
 def gram_kernel(
-    count, tiles, planes, lx, x_ref, u_ref, phase_ref, sums_ref, rim_lhs_ref, v_ref, lhs_ref, op_ref, acc_ref, g_ref
+    count, tiles, planes, lx, groups, slots, empty,
+    x_ref, u_ref, phase_ref, owner_ref, elem_ref, source_ref, spin_ref,
+    sums_ref, rim_lhs_ref, table_ref,
+    v_ref, lhs_ref, op_ref, acc_ref, g_ref, pick_ref,
 ):
     spots = tiles * planes
-    groups = count // GROUP
-    blocks = count // 8
     pair = 2
-    steps = planes * (tiles // pair)
+    halves = tiles // pair
+    steps = planes * halves
+    total_jobs = owner_ref.shape[0]
+    jobs = total_jobs // groups
+    me = lax.axis_index("tm")
 
     def source(row):
         spot = row // GROUP
-        return (row % GROUP) * spots + (spot % tiles) * planes + spot // tiles
-
-    chosen = pick_matrix(GROUP * spots, GROUP * spots, source)
-
-    def regroup(group, carry):
-        start = pl.multiple_of(group * GROUP * 6 * spots, GROUP * 6 * spots)
-        block = x_ref[pl.ds(start, GROUP * 6 * spots), :].reshape(GROUP, 6, spots, LANES)
-        at = pl.multiple_of(group * GROUP, GROUP)
-        for part in range(6):
-            rows = block[:, part].reshape(GROUP * spots, LANES)
-            taken = jnp.dot(chosen, rows, preferred_element_type=F32)
-            half, colour = part // 3, part % 3
-            for spot in range(spots):
-                piece = taken[spot * GROUP : (spot + 1) * GROUP]
-                v_ref[spot * 6 + part, pl.ds(at, GROUP), :] = piece
-                plane, tile = spot // tiles, spot % tiles
-                lhs_ref[
-                    plane * (tiles // pair) + tile // pair,
-                    pl.ds(half * count + at, GROUP),
-                    ((tile % pair) * 3 + colour) * LANES : ((tile % pair) * 3 + colour + 1) * LANES,
-                ] = piece.astype(BF16)
-        return carry
-
-    lax.fori_loop(0, groups, regroup, 0)
-    for k in range(tiles * 6):
-        v_ref[spots * 6 + k] = jnp.zeros((count, LANES), F32)
+        return (row & (GROUP - 1)) * spots + (spot % tiles) * planes + spot // tiles
+
+    pick_ref[...] = pick_matrix(GROUP * spots, GROUP * spots, source)
     acc_ref[...] = jnp.zeros_like(acc_ref)
     g_ref[...] = jnp.zeros_like(g_ref)
+    for at in range(groups * slots):
+        table_ref[at] = empty
+
+    chosen = pick_ref[...]
+    for at in range(0, count, GROUP):
+        block = x_ref[at * 6 * spots : (at + GROUP) * 6 * spots, :].reshape(GROUP, 6, spots, LANES)
+        for first in range(0, 6, 2):
+            rows = jnp.concatenate(
+                [block[:, first + k].reshape(GROUP * spots, LANES) for k in range(2)], axis=1
+            )
+            taken = jnp.dot(chosen, rows, preferred_element_type=F32)
+            for k in range(2):
+                part = first + k
+                half, colour = part // 3, part % 3
+                for spot in range(spots):
+                    piece = taken[spot * GROUP : (spot + 1) * GROUP, k * LANES : (k + 1) * LANES]
+                    v_ref[spot * 6 + part, at : at + GROUP, :] = piece
+                    plane, tile = spot // tiles, spot % tiles
+                    lhs_ref[
+                        plane * halves + tile // pair,
+                        half * count + at : half * count + at + GROUP,
+                        ((tile % pair) * 3 + colour) * LANES : ((tile % pair) * 3 + colour + 1) * LANES,
+                    ] = piece.astype(BF16)
 
     lane = lax.broadcasted_iota(jnp.int32, (8, LANES), 1)
-    wraps = (lane % LZ) == LZ - 1
+    wraps = (lane & (LZ - 1)) == LZ - 1
     spills = lane < LZ
 
-    def elementwise(step, slot):
-        plane = step // (tiles // pair)
-        half_tile = step % (tiles // pair)
+    def elementwise(step, slot, directions):
+        plane = step // halves
+        half_tile = step % halves
         for sub in range(pair):
             tile = half_tile * pair + sub
             spot = plane * tiles + tile
-            next_tile = plane * tiles + lax.rem(tile + 1, tiles)
-            for direction in range(3):
+            next_tile = plane * tiles + (tile + 1) % tiles
+            for direction in directions:
                 links = load_links(u_ref, direction, tile * planes + plane, spots)
-                for block in range(blocks):
-                    at = block * 8
+                for at in range(0, count, 8):
+
+                    def part(where, k):
+                        return v_ref[where * 6 + k, at : at + 8, :]
+
                     if direction == 0:
-                        base = (spot + tiles) * 6
-                        parts = [v_ref[base + k, at : at + 8, :] for k in range(6)]
+                        vec = [part(spot + tiles, k) for k in range(6)]
                     elif direction == 1:
-                        parts = []
-                        for k in range(6):
-                            here = v_ref[spot * 6 + k, at : at + 8, :]
-                            there = v_ref[next_tile * 6 + k, at : at + 8, :]
-                            parts.append(pltpu.roll(jnp.where(spills, there, here), LANES - LZ, 1))
+                        vec = [
+                            pltpu.roll(jnp.where(spills, part(next_tile, k), part(spot, k)), LANES - LZ, 1)
+                            for k in range(6)
+                        ]
                     else:
-                        parts = []
-                        for k in range(6):
-                            here = v_ref[spot * 6 + k, at : at + 8, :]
-                            parts.append(
-                                jnp.where(wraps, pltpu.roll(here, LZ - 1, 1), pltpu.roll(here, LANES - 1, 1))
+                        vec = [
+                            jnp.where(
+                                wraps,
+                                pltpu.roll(part(spot, k), LZ - 1, 1),
+                                pltpu.roll(part(spot, k), LANES - 1, 1),
                             )
-                    outs = link_product(links, (parts[:3], parts[3:]))
+                            for k in range(6)
+                        ]
+                    outs = link_product(links, vec[:3], vec[3:])
                     for half in range(2):
+                        row = (direction * 2 + half) * count + at
                         for colour in range(3):
-                            op_ref[
-                                slot,
-                                direction,
-                                half * count + at : half * count + at + 8,
-                                (sub * 3 + colour) * LANES : (sub * 3 + colour + 1) * LANES,
-                            ] = outs[half][colour].astype(BF16)
-
-    def multiply(step, slot):
-        left = lhs_ref[step]
-        plane = step // (tiles // pair)
-        g_ref[plane] += nt_dot(left, left)
-        for direction in range(3):
-            acc_ref[direction] += nt_dot(left, op_ref[slot, direction])
-
-    elementwise(0, 0)
+                            column = (sub * 3 + colour) * LANES
+                            op_ref[slot, row : row + 8, column : column + LANES] = outs[half][colour].astype(
+                                BF16
+                            )
+
+    def multiply(step, slot, directions):
+        fixed = lhs_ref[step]
+        g_ref[step // halves] += nt_dot(fixed, fixed)
+        low = min(directions) * 2 * count
+        high = (max(directions) + 1) * 2 * count
+        acc_ref[low:high, :] += nt_dot(op_ref[slot, low:high, :], fixed)
+
+    def place(group):
+        used = jnp.int32(0)
+        for at in range(group * jobs, (group + 1) * jobs):
+            mine = owner_ref[at] == me
+            product = source_ref[at] * (SPIN * groups * OPS) + spin_ref[at] * (groups * OPS) + elem_ref[at]
+            table_ref[jnp.where(mine, group * slots + used, groups * slots)] = product + group * OPS
+            used = used + jnp.where(mine, 1, 0)
+
+    every, side = (0, 1, 2), (1, 2)
+    inner = steps - halves
+    elementwise(0, 0, every)
 
     def body(step, carry):
-        slot = lax.rem(step, 2)
-        multiply(step - 1, 1 - slot)
-        elementwise(step, slot)
+        slot = step & 1
+        multiply(step - 1, 1 - slot, every)
+        elementwise(step, slot, every)
         return carry
 
-    lax.fori_loop(1, steps, body, 0)
-    multiply(steps - 1, (steps - 1) % 2)
+    lax.fori_loop(1, inner, body, 0)
+    multiply(inner - 1, (inner - 1) & 1, every)
+    for step in range(inner, steps):
+        elementwise(step, step & 1, side)
+        multiply(step, step & 1, side)
+    for group in range(groups):
+        place(group)
 
     first = lax.axis_index("space") * planes
     total_re = jnp.zeros((count, count), F32)
@@ -213,77 +264,80 @@
         real, imag = paired(g_ref[plane], count)
         cosine = phase_ref[first + plane]
         sine = phase_ref[lx + first + plane]
-        total_re += cosine * real + sine * imag
-        total_im += cosine * imag - sine * real
+        total_re += cosine * real - sine * imag
+        total_im += cosine * imag + sine * real
     sums_ref[0, 0] = total_re
-    sums_ref[0, 1] = total_im
+    sums_ref[0, 1] = -total_im
     for direction in range(3):
-        real, imag = anti(*paired(acc_ref[direction], count))
+        grid = acc_ref[direction * 2 * count : (direction + 1) * 2 * count, :]
+        real, imag = anti(*paired(grid, count))
         sums_ref[direction + 1, 0] = real
         sums_ref[direction + 1, 1] = imag
-    for half in range(tiles // pair):
-        rim_lhs_ref[half] = lhs_ref[(planes - 1) * (tiles // pair) + half]
-
-
-def gram(x, u, phases, count, tiles, planes, lx):
+    for half in range(halves):
+        rim_lhs_ref[half] = lhs_ref[(planes - 1) * halves + half]
+
+
+def gram(x, u, phases, tables, count, tiles, planes, lx, groups, slots, empty):
     spots = tiles * planes
     pair = 2
     steps = planes * (tiles // pair)
+    wide = pair * 3 * LANES
     return pl.pallas_call(
-        partial(gram_kernel, count, tiles, planes, lx),
-        in_specs=[vspec(), vspec(), sspec()],
-        out_specs=[vspec(), vspec()],
+        partial(gram_kernel, count, tiles, planes, lx, groups, slots, empty),
+        in_specs=[vspec(), vspec()] + [sspec()] * 5,
+        out_specs=[vspec(), vspec(), sspec()],
         out_shape=[
             jax.ShapeDtypeStruct((OPS, 2, count, count), F32),
-            jax.ShapeDtypeStruct((tiles // pair, 2 * count, pair * 3 * LANES), BF16),
+            jax.ShapeDtypeStruct((tiles // pair, 2 * count, wide), BF16),
+            jax.ShapeDtypeStruct((groups * slots + 1,), jnp.int32),
         ],
         scratch_shapes=[
-            VMEM(((spots + tiles) * 6, count, LANES), F32),
-            VMEM((steps, 2 * count, pair * 3 * LANES), BF16),
-            VMEM((2, 3, 2 * count, pair * 3 * LANES), BF16),
-            VMEM((3, 2 * count, 2 * count), F32),
+            VMEM((spots * 6, count, LANES), F32),
+            VMEM((steps, 2 * count, wide), BF16),
+            VMEM((2, 6 * count, wide), BF16),
+            VMEM((6 * count, 2 * count), F32),
             VMEM((planes, 2 * count, 2 * count), F32),
+            VMEM((GROUP * spots, GROUP * spots), BF16),
         ],
-        compiler_params=pltpu.CompilerParams(vmem_limit_bytes=40 * 2**20),
+        compiler_params=limit(26),
         cost_estimate=cost(8 * 10**9, 5 * 10**6),
         name="gram",
-    )(x, u, phases)
+    )(x, u, phases, *tables)
 
 
 def edge_kernel(
     count, tiles, planes, rows, cores, halo_ref, lhs_ref, u_ref, sums_ref, keep_ref, send_ref, op_ref, tot_ref
 ):
     spots = tiles * planes
-    blocks = count // GROUP
     pair = 2
     total = None
     for half_tile in range(tiles // pair):
         for sub in range(pair):
             tile = half_tile * pair + sub
             links = load_links(u_ref, 0, tile * planes + planes - 1, spots)
-
-            for block in range(blocks):
-                at = block * GROUP
-                parts = [
-                    halo_ref[k * tiles + tile, at : at + GROUP, :].astype(F32) for k in range(6)
+            for at in range(0, count, GROUP):
+                parts = [halo_ref[k * tiles + tile, at : at + GROUP, :].astype(F32) for k in range(6)]
+                outs = [
+                    link_product(
+                        links,
+                        [part[eight : eight + 8] for part in parts[:3]],
+                        [part[eight : eight + 8] for part in parts[3:]],
+                    )
+                    for eight in (0, 8)
                 ]
-                for eight in range(2):
-                    vecs = [piece[eight * 8 : eight * 8 + 8] for piece in parts]
-                    outs = link_product(links, (vecs[:3], vecs[3:]))
-                    for half in range(2):
-                        for colour in range(3):
-                            start = half * count + at + eight * 8
-                            op_ref[
-                                half_tile,
-                                start : start + 8,
-                                (sub * 3 + colour) * LANES : (sub * 3 + colour + 1) * LANES,
-                            ] = outs[half][colour].astype(BF16)
-        got = nt_dot(lhs_ref[half_tile], op_ref[half_tile])
+                for half in range(2):
+                    for colour in range(3):
+                        column = (sub * 3 + colour) * LANES
+                        both = jnp.concatenate([outs[0][half][colour], outs[1][half][colour]], axis=0)
+                        op_ref[
+                            half_tile, half * count + at : half * count + at + GROUP, column : column + LANES
+                        ] = both.astype(BF16)
+        got = nt_dot(op_ref[half_tile], lhs_ref[half_tile])
         total = got if total is None else total + got
     real, imag = anti(*paired(total, count))
     tot_ref[0] = real
     tot_ref[1] = imag
-    mine = lax.rem(lax.axis_index("space"), cores)
+    mine = lax.axis_index("space") & (cores - 1)
     for chip in range(count // (rows * cores)):
         for which, ref in ((mine, keep_ref), (1 - mine, send_ref)):
             at = pl.multiple_of((chip * cores + which) * rows, rows)
@@ -307,6 +361,7 @@
             VMEM((tiles // pair, 2 * count, pair * 3 * LANES), BF16),
             VMEM((2, count, count), F32),
         ],
+        compiler_params=limit(8),
         cost_estimate=cost(10**9, 3 * 10**6),
         name="edge",
     )(halo, rim_lhs, u, sums)
@@ -328,6 +383,7 @@
         in_specs=[vspec()] * 2,
         out_specs=[vspec()] * chips,
         out_shape=[shape] * chips,
+        compiler_params=limit(4),
         cost_estimate=cost(10**6, 10**6),
         name="fold",
     )(keep, got)
@@ -346,42 +402,10 @@
         in_specs=[vspec()] * len(parts),
         out_specs=vspec(),
         out_shape=jax.ShapeDtypeStruct(parts[0].shape, BF16),
+        compiler_params=limit(4),
         cost_estimate=cost(10**6, 10**6),
         name="total",
     )(*parts)
-
-
-def table_kernel(groups, jobs, slots, empty, owner_ref, elem_ref, source_ref, spin_ref, out_ref):
-    me = lax.axis_index("tm")
-
-    def clear(at, carry):
-        out_ref[at] = empty
-        return carry
-
-    lax.fori_loop(0, groups * slots + 1, clear, 0)
-    for group in range(groups):
-
-        def place(job, used):
-            at = group * jobs + job
-            mine = owner_ref[at] == me
-            product = (source_ref[at] * SPIN + spin_ref[at]) * (groups * OPS) + group * OPS + elem_ref[at]
-            spot = jnp.where(mine, group * slots + used, groups * slots)
-            out_ref[spot] = product
-            return used + mine.astype(jnp.int32)
-
-        lax.fori_loop(0, jobs, place, jnp.int32(0))
-
-
-def job_table(owner, elem, source, spin, groups, slots, empty):
-    jobs = owner.shape[0] // groups
-    return pl.pallas_call(
-        partial(table_kernel, groups, jobs, slots, empty),
-        in_specs=[sspec()] * 4,
-        out_specs=sspec(),
-        out_shape=jax.ShapeDtypeStruct((groups * slots + 1,), jnp.int32),
-        cost_estimate=cost(10**5, 10**4),
-        name="table",
-    )(owner, elem, source, spin)
 
 
 def dress_kernel(groups, slots, taus, rows, count, table_ref, per_ref, *refs):
@@ -422,6 +446,7 @@
             VMEM((groups * OPS * rows, 2 * count), BF16),
             VMEM((taus * groups * OPS + 1, rows, 2 * count), BF16),
         ],
+        compiler_params=limit(8),
         cost_estimate=cost(10**9, 2 * 10**6),
         name="dress",
     )(table, per, *slabs)
@@ -449,12 +474,13 @@
     angle = 2.0 * math.pi / lx * np.arange(lx)
     phases = jnp.asarray(np.concatenate([np.cos(angle), np.sin(angle)]).astype(np.float32))
 
-    rim = rim_plane(x, count, tiles, planes)
+    per = perambulator.reshape(-1, 2, count, count)
+    empty = per.shape[0] * groups * OPS
+    rim, x, u = rim_plane(x, u, count, tiles, planes)
     halo = lax.ppermute(rim, "space", [(i, (i - 1) % space_size) for i in range(space_size)])
-    sums, rim_lhs = gram(x, u, phases, count, tiles, planes, lx)
-    per = perambulator.reshape(-1, 2, count, count)
-    table = job_table(
-        job_owner.reshape(-1), job_elemental, job_source, job_spin, groups, slots, per.shape[0] * groups * OPS
+    tables = (job_owner.reshape(-1), job_elemental, job_source, job_spin)
+    sums, rim_lhs, table = gram(
+        x, u, phases, tables, count, tiles, planes, lx, groups, slots, empty
     )
     keep, send = edge(halo, rim_lhs, u, sums, count, tiles, planes, rows, cores)
     got = lax.ppermute(send, "space", [(i, i ^ 1) for i in range(space_size)])

time: 56.6 us -> 41.2 us (0.73)
  Pallas kernels: 33.8 us -> 17.9 us
  waiting for transfers between devices: 6.47 us -> 8.51 us
  local copies, waits for them, and re-layouts: 4.67 us -> 2.98 us
    pallas_call x3 -> x2, Pallas kernels: 24.5 us -> 15.1 us  [the longest x1 11.6 us: gram(): pl.pallas_call(partial(gram_kernel, count, tiles, planes, lx, groups, slo...]
    pallas_call x1, Pallas kernels: 3.52 us -> 0.94 us  [edge(): pl.pallas_call(partial(edge_kernel, count, tiles, planes, rows, cores), i...]
    ppermute x3, waiting for transfers between devices: 1.62 us -> 4.03 us  [fast_shards(): lax.ppermute(own, 'tm', [(i, i ^ step) for i in range(groups)])]
    pallas_call x1, Pallas kernels: 1.75 us -> 0.03 us  [fold(): pl.pallas_call(partial(fold_kernel, chips), in_specs=[vspec()] * 2, out_s...]
    unnamed x24 -> x16, local copies, waits for them, and re-layouts: 4.67 us -> 2.98 us
    pallas_call x1, Pallas kernels: 1.56 us -> 0.02 us  [total_rows(): pl.pallas_call(total_kernel, in_specs=[vspec()] * len(parts), out_specs=v...]
  transfers between devices with their start and end apart: 8 -> 8, of which waited for: 4 -> 5; matrix products, arithmetic and copies ran while one was open for 0% -> 0% of each run, Pallas kernels for 32% -> 28%
where the time goes in v1:
time: 41.2 us; the launch traced here: 41 us
  Pallas kernels  17.9 us (43%)
  starting transfers between devices  11.5 us (28%)
  waiting for transfers between devices  8.51 us (21%)
  local copies, waits for them, and re-layouts  2.98 us (7%)
    pallas_call x1, Pallas kernels, gram(): pl.pallas_call(partial(gram_kernel, count, tiles, planes, lx, groups, slo...  11.6 us
    ppermute x3, starting transfers between devices, fast_shards(): lax.ppermute(own, 'tm', [(i, i ^ step) for i in range(groups)])  4.45 us
    ppermute x3, waiting for transfers between devices, fast_shards(): lax.ppermute(own, 'tm', [(i, i ^ step) for i in range(groups)])  4.03 us
    ppermute x3, starting transfers between devices, fast_shards(): lax.ppermute(parts[step], 'space', [(i, i ^ step * cores) for i in range(...  3.55 us
    pallas_call x1, Pallas kernels, rim_plane(): pl.pallas_call(partial(rim_kernel, tiles, planes), in_specs=[pl.BlockSpec...  3.5 us
    ppermute x1, starting transfers between devices, fast_shards(): lax.ppermute(rim, 'space', [(i, (i - 1) % space_size) for i in range(spac...  3.41 us
    unnamed x16, local copies, waits for them, and re-layouts  2.98 us
    ppermute x3, waiting for transfers between devices, fast_shards(): lax.ppermute(parts[step], 'space', [(i, i ^ step * cores) for i in range(...  2.96 us
  transfers between devices with their start and end apart: 8, of which 5 were waited for; matrix products, arithmetic and copies ran while one was open for 0% of the time, Pallas kernels for 28%

profile of v1, /device:TPU:0, one launch (start us, length us, event | category | flops | bytes accessed | tf_op | source)
XLA Modules:
  0.0 41.0 jit_solution(11156446740442550441)
XLA Ops:
  0.0 0.0 copy-start.7
  0.0 0.0 copy-start.6
  0.0 0.0 copy-start
  0.0 1.9 %copy-done = bf16[1,128,2,3,4,512]{5,4,3,2,1,0:T(4,128)(2,1)S(1)} copy-done((bf16[1,128,2,3,4,512]{5,4,3,2,1,0:T(4,128)(2,1)S(1)}, bf16[1,128,2,3,4,512]{5,4,3,2,1,0:T(4,128)(2,1)}, u32[]{:S(2)}) %copy-start) | copy-done | bytes 3145752
  2.0 1.0 %copy-done.1 = f32[1,3,2,3,3,4,512]{6,5,4,3,2,1,0:T(4,128)S(1)} copy-done((f32[1,3,2,3,3,4,512]{6,5,4,3,2,1,0:T(4,128)S(1)}, f32[1,3,2,3,3,4,512]{6,5,4,3,2,1,0:T(4,128)}, u32[]{:S(2)}) %copy-start.1) | copy-done | bytes 442392
  3.0 3.5 %rim.1 = (bf16[24,128,128]{2,1,0:T(8,128)(2,1)S(1)}, bf16[12288,128]{1,0:T(8,128)(2,1)S(1)}, f32[864,128]{1,0:T(8,128)S(1)}) custom-call(bf16[12288,128]{1,0:T(8,128)(2,1)S(1)} %bitcast.13, f32[864,128]{1,0:T(8,128)S(1)} %bitcast.14), custom_call_target="tpu_custom_call" | custom-call | flops 100000000 | bytes 4000000 | tf_op jit(solution)/shard_map/rim/pallas_call | solution.py:86
  6.5 3.4 %collective-permute-start = (bf16[24,128,128]{2,1,0:T(8,128)(2,1)S(1)}, bf16[24,128,128]{2,1,0:T(8,128)(2,1)S(1)}, u32[]{:S(2)}, u32[]{:S(2)}) collective-permute-start(bf16[24,128,128]{2,1,0:T(8,128)(2,1)S(1)} %get-tuple-element.20), channel_id=1, source_target_pairs={{0,7},{1,0},{2,1},{3,2},{4,3},{5,4},{6,5},{7,6},{8,15},{9,8},{10,9... | collective-permute-start | bytes 2359304 | tf_op jit(solution)/shard_map/ppermute | solution.py:480
  9.9 0.0 copy-done.7
  9.9 0.0 copy-done.6
  9.9 0.0 copy-done.5
  9.9 0.0 copy-done.4
  9.9 0.0 copy-done.3
  9.9 11.6 %gram.1 = (f32[4,2,128,128]{3,2,1,0:T(8,128)S(1)}, bf16[2,256,768]{2,1,0:T(8,128)(2,1)S(1)}, s32[73]{0:T(128)S(1)}) custom-call(bf16[12288,128]{1,0:T(8,128)(2,1)S(1)} %get-tuple-element.17.x_ref, f32[864,128]{1,0:T(8,128)S(1)} %get-tuple-element.18.u_ref, f32[64]{0:T(128)S(1)} %copy-done.7, s32[96]{0:T(128)S(1)} %bitcast.16, s32[96]{0:T(128)S(1)} %copy-done.4, ...), custom_call_target="tpu_custom_call" | custom-call | flops 8000000000 | bytes 5000000 | tf_op jit(solution)/shard_map/gram/pallas_call | solution.py:285
  21.5 0.0 copy-start.2
  21.5 0.0 collective-permute-done.halo_ref
  21.5 0.9 %edge.1 = (f32[4,4,2,16,128]{4,3,2,1,0:T(8,128)S(1)}, f32[4,4,2,16,128]{4,3,2,1,0:T(8,128)S(1)}) custom-call(bf16[24,128,128]{2,1,0:T(8,128)(2,1)S(1)} %collective-permute-done.halo_ref, bf16[2,256,768]{2,1,0:T(8,128)(2,1)S(1)} %get-tuple-element.21.lhs_ref, f32[864,128]{1,0:T(8,128)S(1)} %get-tuple-element.18.u_ref, ...), custom_call_target="tpu_custom_call" | custom-call | flops 1000000000 | bytes 3000000 | tf_op jit(solution)/shard_map/edge/pallas_call | solution.py:355
  22.5 0.1 collective-permute-start.1
  22.5 1.5 %collective-permute-done.1.got_ref = f32[4,4,2,16,128]{4,3,2,1,0:T(8,128)S(1)} collective-permute-done((f32[4,4,2,16,128]{4,3,2,1,0:T(8,128)S(1)}, f32[4,4,2,16,128]{4,3,2,1,0:T(8,128)S(1)}, u32[]{:S(2)}, u32[]{:S(2)}) %collective-permute-start.1) | collective-permute-done | bytes 262176 | tf_op jit(solution)/shard_map/ppermute | solution.py:486
  24.1 0.1 collective-permute-start.2
  24.2 1.3 %collective-permute-start.3 = (f32[4,2,16,128]{3,2,1,0:T(8,128)S(1)}, f32[4,2,16,128]{3,2,1,0:T(8,128)S(1)}, u32[]{:S(2)}, u32[]{:S(2)}) collective-permute-start(f32[4,2,16,128]{3,2,1,0:T(8,128)S(1)} %get-tuple-element.27), channel_id=1, source_target_pairs={{0,4},{1,5},{2,6},{3,7},{4,0},{5,1},{6,2},{7,3},{8,12},{9,13},{10,... | collective-permute-start | bytes 196616 | tf_op jit(solution)/shard_map/ppermute | solution.py:491
  25.4 2.2 %collective-permute-start.4 = (f32[4,2,16,128]{3,2,1,0:T(8,128)S(1)}, f32[4,2,16,128]{3,2,1,0:T(8,128)S(1)}, u32[]{:S(2)}, u32[]{:S(2)}) collective-permute-start(f32[4,2,16,128]{3,2,1,0:T(8,128)S(1)} %get-tuple-element.28), channel_id=1, source_target_pairs={{0,6},{1,7},{2,4},{3,5},{4,2},{5,3},{6,0},{7,1},{8,14},{9,15},{10,... | collective-permute-start | bytes 196616 | tf_op jit(solution)/shard_map/ppermute | solution.py:491
  27.7 1.0 %collective-permute-done.2.refs_1_ = f32[4,2,16,128]{3,2,1,0:T(8,128)S(1)} collective-permute-done((f32[4,2,16,128]{3,2,1,0:T(8,128)S(1)}, f32[4,2,16,128]{3,2,1,0:T(8,128)S(1)}, u32[]{:S(2)}, u32[]{:S(2)}) %collective-permute-start.2) | collective-permute-done | bytes 65568 | tf_op jit(solution)/shard_map/ppermute | solution.py:491
  28.7 0.0 collective-permute-done.3.refs_2_
  28.7 1.9 %collective-permute-done.4.refs_3_ = f32[4,2,16,128]{3,2,1,0:T(8,128)S(1)} collective-permute-done((f32[4,2,16,128]{3,2,1,0:T(8,128)S(1)}, f32[4,2,16,128]{3,2,1,0:T(8,128)S(1)}, u32[]{:S(2)}, u32[]{:S(2)}) %collective-permute-start.4) | collective-permute-done | bytes 65568 | tf_op jit(solution)/shard_map/ppermute | solution.py:491
  30.6 3.7 %collective-permute-start.7 = (bf16[4,2,16,128]{3,2,1,0:T(8,128)(2,1)S(1)}, bf16[4,2,16,128]{3,2,1,0:T(8,128)(2,1)S(1)}, u32[]{:S(2)}, u32[]{:S(2)}) collective-permute-start(bf16[4,2,16,128]{3,2,1,0:T(8,128)(2,1)S(1)} %total.1.refs_0_), channel_id=1, source_target_pairs={{0,24},{8,16},{16,8},{24,0},{1,25},{9,17},{17,9},{25,1},{2,26},{10... | collective-permute-start | bytes 98312 | tf_op jit(solution)/shard_map/ppermute | solution.py:496
  34.3 0.0 collective-permute-start.6
  34.3 0.8 %collective-permute-start.5 = (bf16[4,2,16,128]{3,2,1,0:T(8,128)(2,1)S(1)}, bf16[4,2,16,128]{3,2,1,0:T(8,128)(2,1)S(1)}, u32[]{:S(2)}, u32[]{:S(2)}) collective-permute-start(bf16[4,2,16,128]{3,2,1,0:T(8,128)(2,1)S(1)} %total.1.refs_0_), channel_id=1, source_target_pairs={{0,8},{8,0},{16,24},{24,16},{1,9},{9,1},{17,25},{25,17},{2,10},{10... | collective-permute-start | bytes 98312 | tf_op jit(solution)/shard_map/ppermute | solution.py:496
  35.1 1.3 %collective-permute-done.7.refs_3_ = bf16[4,2,16,128]{3,2,1,0:T(8,128)(2,1)S(1)} collective-permute-done((bf16[4,2,16,128]{3,2,1,0:T(8,128)(2,1)S(1)}, bf16[4,2,16,128]{3,2,1,0:T(8,128)(2,1)S(1)}, u32[]{:S(2)}, u32[]{:S(2)}) %collective-permute-start.7) | collective-permute-done | bytes 32800 | tf_op jit(solution)/shard_map/ppermute | solution.py:496
  36.4 2.7 %collective-permute-done.6.refs_2_ = bf16[4,2,16,128]{3,2,1,0:T(8,128)(2,1)S(1)} collective-permute-done((bf16[4,2,16,128]{3,2,1,0:T(8,128)(2,1)S(1)}, bf16[4,2,16,128]{3,2,1,0:T(8,128)(2,1)S(1)}, u32[]{:S(2)}, u32[]{:S(2)}) %collective-permute-start.6) | collective-permute-done | bytes 32800 | tf_op jit(solution)/shard_map/ppermute | solution.py:496
  39.1 0.0 collective-permute-done.5.refs_1_
  39.1 0.0 copy-done.2
  39.1 1.9 %dress.1 = bf16[4,18,2,16,128]{4,3,2,1,0:T(8,128)(2,1)} custom-call(s32[73]{0:T(128)S(1)} %get-tuple-element.19.table_ref, bf16[8,2,128,128]{3,2,1,0:T(8,128)(2,1)S(1)} %bitcast.15, bf16[4,2,16,128]{3,2,1,0:T(8,128)(2,1)S(1)} %total.1.refs_0_, bf16[4,2,16,128]{3,2,1,0:T(8,128)(2,1)S(1)} %collective-permute-done.5.refs_1_, ...), custom_call_target="tpu_custom_call" | custom-call | flops 1000000000 | bytes 2000000 | tf_op jit(solution)/shard_map/dress/pallas_call | solution.py:440
  (6 shorter events, 0.1 us)
Async XLA Ops:
  0.0 9.9 %copy-start.7 = (f32[64]{0:T(128)S(1)}, f32[64]{0:T(128)}, u32[]{:S(2)}) copy-start(f32[64]{0:T(128)} %constant.2.clone.phase_ref) | copy-start | bytes 772
  0.0 9.9 %copy-start.6 = (s32[96]{0:T(128)S(1)}, s32[96]{0:T(128)}, u32[]{:S(2)}) copy-start(s32[96]{0:T(128)} %spin_ref.1) | copy-start | bytes 1156
  0.0 9.9 %copy-start.5 = (s32[96]{0:T(128)S(1)}, s32[96]{0:T(128)}, u32[]{:S(2)}) copy-start(s32[96]{0:T(128)} %source_ref.1) | copy-start | bytes 1156
  0.0 9.9 %copy-start.4 = (s32[96]{0:T(128)S(1)}, s32[96]{0:T(128)}, u32[]{:S(2)}) copy-start(s32[96]{0:T(128)} %elem_ref.1) | copy-start | bytes 1156
  0.0 9.9 %copy-start.3 = (s32[96,1]{0,1:T(1,128)S(1)}, s32[96,1]{0,1:T(1,128)}, u32[]{:S(2)}) copy-start(s32[96,1]{0,1:T(1,128)} %param.11) | copy-start | bytes 1156
  0.0 2.0 %copy-start = (bf16[1,128,2,3,4,512]{5,4,3,2,1,0:T(4,128)(2,1)S(1)}, bf16[1,128,2,3,4,512]{5,4,3,2,1,0:T(4,128)(2,1)}, u32[]{:S(2)}) copy-start(bf16[1,128,2,3,4,512]{5,4,3,2,1,0:T(4,128)(2,1)} %param.8) | copy-start | bytes 9437188
  2.0 1.0 %copy-start.1 = (f32[1,3,2,3,3,4,512]{6,5,4,3,2,1,0:T(4,128)S(1)}, f32[1,3,2,3,3,4,512]{6,5,4,3,2,1,0:T(4,128)}, u32[]{:S(2)}) copy-start(f32[1,3,2,3,3,4,512]{6,5,4,3,2,1,0:T(4,128)} %param.9) | copy-start | bytes 1327108
  6.5 15.0 %collective-permute-start = (bf16[24,128,128]{2,1,0:T(8,128)(2,1)S(1)}, bf16[24,128,128]{2,1,0:T(8,128)(2,1)S(1)}, u32[]{:S(2)}, u32[]{:S(2)}) collective-permute-start(bf16[24,128,128]{2,1,0:T(8,128)(2,1)S(1)} %get-tuple-element.20), channel_id=1, source_target_pairs={{0,7},{1,0},{2,1},{3,2},{4,3},{5,4},{6,5},{7,6},{8,15},{9,8},{10,9... | collective-permute-start | bytes 2359304 | tf_op jit(solution)/shard_map/ppermute | solution.py:480
  21.5 17.6 %copy-start.2 = (bf16[2,4,2,128,128]{4,3,2,1,0:T(8,128)(2,1)S(1)}, bf16[2,4,2,128,128]{4,3,2,1,0:T(8,128)(2,1)}, u32[]{:S(2)}) copy-start(bf16[2,4,2,128,128]{4,3,2,1,0:T(8,128)(2,1)} %param.10) | copy-start | bytes 1572868
  22.5 1.6 %collective-permute-start.1 = (f32[4,4,2,16,128]{4,3,2,1,0:T(8,128)S(1)}, f32[4,4,2,16,128]{4,3,2,1,0:T(8,128)S(1)}, u32[]{:S(2)}, u32[]{:S(2)}) collective-permute-start(f32[4,4,2,16,128]{4,3,2,1,0:T(8,128)S(1)} %get-tuple-element.24), channel_id=1, source_target_pairs={{0,1},{1,0},{2,3},{3,2},{4,5},{5,4},{6,7},{7,6},{8,9},{9,8},{10,11... | collective-permute-start | bytes 786440 | tf_op jit(solution)/shard_map/ppermute | solution.py:486
  24.1 4.6 %collective-permute-start.2 = (f32[4,2,16,128]{3,2,1,0:T(8,128)S(1)}, f32[4,2,16,128]{3,2,1,0:T(8,128)S(1)}, u32[]{:S(2)}, u32[]{:S(2)}) collective-permute-start(f32[4,2,16,128]{3,2,1,0:T(8,128)S(1)} %get-tuple-element.26), channel_id=1, source_target_pairs={{0,2},{1,3},{2,0},{3,1},{4,6},{5,7},{6,4},{7,5},{8,10},{9,11},{10,... | collective-permute-start | bytes 196616 | tf_op jit(solution)/shard_map/ppermute | solution.py:491
  24.2 4.5 %collective-permute-start.3 = (f32[4,2,16,128]{3,2,1,0:T(8,128)S(1)}, f32[4,2,16,128]{3,2,1,0:T(8,128)S(1)}, u32[]{:S(2)}, u32[]{:S(2)}) collective-permute-start(f32[4,2,16,128]{3,2,1,0:T(8,128)S(1)} %get-tuple-element.27), channel_id=1, source_target_pairs={{0,4},{1,5},{2,6},{3,7},{4,0},{5,1},{6,2},{7,3},{8,12},{9,13},{10,... | collective-permute-start | bytes 196616 | tf_op jit(solution)/shard_map/ppermute | solution.py:491
  25.4 5.2 %collective-permute-start.4 = (f32[4,2,16,128]{3,2,1,0:T(8,128)S(1)}, f32[4,2,16,128]{3,2,1,0:T(8,128)S(1)}, u32[]{:S(2)}, u32[]{:S(2)}) collective-permute-start(f32[4,2,16,128]{3,2,1,0:T(8,128)S(1)} %get-tuple-element.28), channel_id=1, source_target_pairs={{0,6},{1,7},{2,4},{3,5},{4,2},{5,3},{6,0},{7,1},{8,14},{9,15},{10,... | collective-permute-start | bytes 196616 | tf_op jit(solution)/shard_map/ppermute | solution.py:491
  30.6 5.8 %collective-permute-start.7 = (bf16[4,2,16,128]{3,2,1,0:T(8,128)(2,1)S(1)}, bf16[4,2,16,128]{3,2,1,0:T(8,128)(2,1)S(1)}, u32[]{:S(2)}, u32[]{:S(2)}) collective-permute-start(bf16[4,2,16,128]{3,2,1,0:T(8,128)(2,1)S(1)} %total.1.refs_0_), channel_id=1, source_target_pairs={{0,24},{8,16},{16,8},{24,0},{1,25},{9,17},{17,9},{25,1},{2,26},{10... | collective-permute-start | bytes 98312 | tf_op jit(solution)/shard_map/ppermute | solution.py:496
  34.3 4.8 %collective-permute-start.6 = (bf16[4,2,16,128]{3,2,1,0:T(8,128)(2,1)S(1)}, bf16[4,2,16,128]{3,2,1,0:T(8,128)(2,1)S(1)}, u32[]{:S(2)}, u32[]{:S(2)}) collective-permute-start(bf16[4,2,16,128]{3,2,1,0:T(8,128)(2,1)S(1)} %total.1.refs_0_), channel_id=1, source_target_pairs={{0,16},{8,24},{16,0},{24,8},{1,17},{9,25},{17,1},{25,9},{2,18},{10... | collective-permute-start | bytes 98312 | tf_op jit(solution)/shard_map/ppermute | solution.py:496
  34.3 4.8 %collective-permute-start.5 = (bf16[4,2,16,128]{3,2,1,0:T(8,128)(2,1)S(1)}, bf16[4,2,16,128]{3,2,1,0:T(8,128)(2,1)S(1)}, u32[]{:S(2)}, u32[]{:S(2)}) collective-permute-start(bf16[4,2,16,128]{3,2,1,0:T(8,128)(2,1)S(1)} %total.1.refs_0_), channel_id=1, source_target_pairs={{0,8},{8,0},{16,24},{24,16},{1,9},{9,1},{17,25},{25,17},{2,10},{10... | collective-permute-start | bytes 98312 | tf_op jit(solution)/shard_map/ppermute | solution.py:496

commit v2 on v1

--- a/solution.py
+++ b/solution.py
@@ -104,13 +104,12 @@
 
 def link_product(links, vec_re, vec_im):
     plus = [vec_re[c] + vec_im[c] for c in range(3)]
-    minus = [vec_im[c] - vec_re[c] for c in range(3)]
     outs_re, outs_im = [], []
     for row in range(3):
-        link_re, link_im, link_sum = links[0][row], links[1][row], links[2][row]
-        one = link_sum[0] * vec_re[0] + link_sum[1] * vec_re[1] + link_sum[2] * vec_re[2]
-        two = link_re[0] * minus[0] + link_re[1] * minus[1] + link_re[2] * minus[2]
-        three = link_im[0] * plus[0] + link_im[1] * plus[1] + link_im[2] * plus[2]
+        link_re, link_less, link_more = links[0][row], links[1][row], links[2][row]
+        one = link_re[0] * plus[0] + link_re[1] * plus[1] + link_re[2] * plus[2]
+        two = link_less[0] * vec_re[0] + link_less[1] * vec_re[1] + link_less[2] * vec_re[2]
+        three = link_more[0] * vec_im[0] + link_more[1] * vec_im[1] + link_more[2] * vec_im[2]
         outs_re.append(one - three)
         outs_im.append(one + two)
     return outs_re, outs_im
@@ -122,8 +121,9 @@
         return jnp.broadcast_to(u_ref[pl.ds(at, 1), :], (8, LANES))
 
     grid = [[[one(part, row, col) for col in range(3)] for row in range(3)] for part in range(2)]
-    total = [[grid[0][row][col] + grid[1][row][col] for col in range(3)] for row in range(3)]
-    return grid + [total]
+    less = [[grid[1][row][col] - grid[0][row][col] for col in range(3)] for row in range(3)]
+    more = [[grid[1][row][col] + grid[0][row][col] for col in range(3)] for row in range(3)]
+    return grid[0], less, more
 
 
 def paired(grid, count):
@@ -137,18 +137,14 @@
 
 
 def gram_kernel(
-    count, tiles, planes, lx, groups, slots, empty,
-    x_ref, u_ref, phase_ref, owner_ref, elem_ref, source_ref, spin_ref,
-    sums_ref, rim_lhs_ref, table_ref,
+    count, tiles, planes, lx,
+    x_ref, u_ref, phase_ref, sums_ref, rim_lhs_ref,
     v_ref, lhs_ref, op_ref, acc_ref, g_ref, pick_ref,
 ):
     spots = tiles * planes
     pair = 2
     halves = tiles // pair
     steps = planes * halves
-    total_jobs = owner_ref.shape[0]
-    jobs = total_jobs // groups
-    me = lax.axis_index("tm")
 
     def source(row):
         spot = row // GROUP
@@ -157,8 +153,6 @@
     pick_ref[...] = pick_matrix(GROUP * spots, GROUP * spots, source)
     acc_ref[...] = jnp.zeros_like(acc_ref)
     g_ref[...] = jnp.zeros_like(g_ref)
-    for at in range(groups * slots):
-        table_ref[at] = empty
 
     chosen = pick_ref[...]
     for at in range(0, count, GROUP):
@@ -231,14 +225,6 @@
         high = (max(directions) + 1) * 2 * count
         acc_ref[low:high, :] += nt_dot(op_ref[slot, low:high, :], fixed)
 
-    def place(group):
-        used = jnp.int32(0)
-        for at in range(group * jobs, (group + 1) * jobs):
-            mine = owner_ref[at] == me
-            product = source_ref[at] * (SPIN * groups * OPS) + spin_ref[at] * (groups * OPS) + elem_ref[at]
-            table_ref[jnp.where(mine, group * slots + used, groups * slots)] = product + group * OPS
-            used = used + jnp.where(mine, 1, 0)
-
     every, side = (0, 1, 2), (1, 2)
     inner = steps - halves
     elementwise(0, 0, every)
@@ -254,8 +240,6 @@
     for step in range(inner, steps):
         elementwise(step, step & 1, side)
         multiply(step, step & 1, side)
-    for group in range(groups):
-        place(group)
 
     first = lax.axis_index("space") * planes
     total_re = jnp.zeros((count, count), F32)
@@ -277,19 +261,18 @@
         rim_lhs_ref[half] = lhs_ref[(planes - 1) * halves + half]
 
 
-def gram(x, u, phases, tables, count, tiles, planes, lx, groups, slots, empty):
+def gram(x, u, phases, count, tiles, planes, lx):
     spots = tiles * planes
     pair = 2
     steps = planes * (tiles // pair)
     wide = pair * 3 * LANES
     return pl.pallas_call(
-        partial(gram_kernel, count, tiles, planes, lx, groups, slots, empty),
-        in_specs=[vspec(), vspec()] + [sspec()] * 5,
-        out_specs=[vspec(), vspec(), sspec()],
+        partial(gram_kernel, count, tiles, planes, lx),
+        in_specs=[vspec(), vspec(), sspec()],
+        out_specs=[vspec(), vspec()],
         out_shape=[
             jax.ShapeDtypeStruct((OPS, 2, count, count), F32),
             jax.ShapeDtypeStruct((tiles // pair, 2 * count, wide), BF16),
-            jax.ShapeDtypeStruct((groups * slots + 1,), jnp.int32),
         ],
         scratch_shapes=[
             VMEM((spots * 6, count, LANES), F32),
@@ -302,7 +285,7 @@
         compiler_params=limit(26),
         cost_estimate=cost(8 * 10**9, 5 * 10**6),
         name="gram",
-    )(x, u, phases, *tables)
+    )(x, u, phases)
 
 
 def edge_kernel(
@@ -408,6 +391,32 @@
     )(*parts)
 
 
+def table_kernel(groups, slots, empty, owner_ref, elem_ref, source_ref, spin_ref, table_ref):
+    me = lax.axis_index("tm")
+    jobs = owner_ref.shape[0] // groups
+    for at in range(groups * slots):
+        table_ref[at] = empty
+    for group in range(groups):
+        used = jnp.int32(0)
+        for at in range(group * jobs, (group + 1) * jobs):
+            mine = owner_ref[at] == me
+            product = source_ref[at] * (SPIN * groups * OPS) + spin_ref[at] * (groups * OPS) + elem_ref[at]
+            table_ref[jnp.where(mine, group * slots + used, groups * slots)] = product + group * OPS
+            used = used + jnp.where(mine, 1, 0)
+
+
+def job_table(tables, groups, slots, empty):
+    return pl.pallas_call(
+        partial(table_kernel, groups, slots, empty),
+        in_specs=[sspec()] * 4,
+        out_specs=sspec(),
+        out_shape=jax.ShapeDtypeStruct((groups * slots + 1,), jnp.int32),
+        compiler_params=limit(1),
+        cost_estimate=cost(10**5, 10**4),
+        name="table",
+    )(*tables)
+
+
 def dress_kernel(groups, slots, taus, rows, count, table_ref, per_ref, *refs):
     slab_refs = refs[:groups]
     out_ref, lhs_ref, prod_ref = refs[groups:]
@@ -476,12 +485,13 @@
 
     per = perambulator.reshape(-1, 2, count, count)
     empty = per.shape[0] * groups * OPS
+    x = pltpu.with_memory_space_constraint(x, pltpu.HBM)
+    u = pltpu.with_memory_space_constraint(u, pltpu.HBM)
     rim, x, u = rim_plane(x, u, count, tiles, planes)
     halo = lax.ppermute(rim, "space", [(i, (i - 1) % space_size) for i in range(space_size)])
     tables = (job_owner.reshape(-1), job_elemental, job_source, job_spin)
-    sums, rim_lhs, table = gram(
-        x, u, phases, tables, count, tiles, planes, lx, groups, slots, empty
-    )
+    table = job_table(tables, groups, slots, empty)
+    sums, rim_lhs = gram(x, u, phases, count, tiles, planes, lx)
     keep, send = edge(halo, rim_lhs, u, sums, count, tiles, planes, rows, cores)
     got = lax.ppermute(send, "space", [(i, i ^ 1) for i in range(space_size)])
     parts = fold(keep, got)

time: 41.2 us -> 38.9 us (0.944)
  local copies, waits for them, and re-layouts: 2.98 us -> 0.04 us
  waiting for transfers between devices: 8.51 us -> 9.43 us
    unnamed x16 -> x12, local copies, waits for them, and re-layouts: 2.98 us -> 0.04 us
    ppermute x3, waiting for transfers between devices: 2.96 us -> 4.05 us  [fast_shards(): lax.ppermute(parts[step], 'space', [(i, i ^ step * cores) for i in range(...]
    pallas_call x1, Pallas kernels: 3.5 us -> 2.76 us  [rim_plane(): pl.pallas_call(partial(rim_kernel, tiles, planes), in_specs=[pl.BlockSpec...]
    pallas_call x1 -> x2, Pallas kernels: 11.6 us -> 12 us  [the longest x1 10.4 us: gram(): pl.pallas_call(partial(gram_kernel, count, tiles, planes, lx), in_specs=[...]
  transfers between devices with their start and end apart: 8 -> 8, of which waited for: 5 -> 6; matrix products, arithmetic and copies ran while one was open for 0% -> 0% of each run, Pallas kernels for 28% -> 31%
where the time goes in v2:
time: 38.9 us; the launch traced here: 38.7 us
  Pallas kernels  17.6 us (45%)
  starting transfers between devices  11.5 us (30%)
  waiting for transfers between devices  9.43 us (24%)
    pallas_call x1, Pallas kernels, gram(): pl.pallas_call(partial(gram_kernel, count, tiles, planes, lx), in_specs=[...  10.4 us
    ppermute x3, starting transfers between devices, fast_shards(): lax.ppermute(own, 'tm', [(i, i ^ step) for i in range(groups)])  4.45 us
    ppermute x3, waiting for transfers between devices, fast_shards(): lax.ppermute(parts[step], 'space', [(i, i ^ step * cores) for i in range(...  4.05 us
    ppermute x3, waiting for transfers between devices, fast_shards(): lax.ppermute(own, 'tm', [(i, i ^ step) for i in range(groups)])  3.86 us
    ppermute x3, starting transfers between devices, fast_shards(): lax.ppermute(parts[step], 'space', [(i, i ^ step * cores) for i in range(...  3.55 us
    ppermute x1, starting transfers between devices, fast_shards(): lax.ppermute(rim, 'space', [(i, (i - 1) % space_size) for i in range(spac...  3.41 us
    pallas_call x1, Pallas kernels, rim_plane(): pl.pallas_call(partial(rim_kernel, tiles, planes), in_specs=[pl.BlockSpec...  2.76 us
    pallas_call x1, Pallas kernels, dress(): pl.pallas_call(partial(dress_kernel, groups, slots, taus, rows, count), i...  1.9 us
  transfers between devices with their start and end apart: 8, of which 6 were waited for; matrix products, arithmetic and copies ran while one was open for 0% of the time, Pallas kernels for 31%

profile of v2, /device:TPU:0, one launch (start us, length us, event | category | flops | bytes accessed | tf_op | source)
XLA Modules:
  0.0 38.7 jit_solution(10876254282670149726)
XLA Ops:
  0.0 2.8 %rim.1 = (bf16[24,128,128]{2,1,0:T(8,128)(2,1)S(1)}, bf16[12288,128]{1,0:T(8,128)(2,1)S(1)}, f32[864,128]{1,0:T(8,128)S(1)}) custom-call(bf16[12288,128]{1,0:T(8,128)(2,1)} %bitcast.15, f32[864,128]{1,0:T(8,128)} %bitcast.16), custom_call_target="tpu_custom_call" | custom-call | flops 100000000 | bytes 4000000 | tf_op jit(solution)/shard_map/rim/pallas_call | solution.py:86
  2.8 3.4 %collective-permute-start = (bf16[24,128,128]{2,1,0:T(8,128)(2,1)S(1)}, bf16[24,128,128]{2,1,0:T(8,128)(2,1)S(1)}, u32[]{:S(2)}, u32[]{:S(2)}) collective-permute-start(bf16[24,128,128]{2,1,0:T(8,128)(2,1)S(1)} %get-tuple-element.16), channel_id=1, source_target_pairs={{0,7},{1,0},{2,1},{3,2},{4,3},{5,4},{6,5},{7,6},{8,15},{9,8},{10,9... | collective-permute-start | bytes 2359304 | tf_op jit(solution)/shard_map/ppermute | solution.py:491
  6.2 0.0 copy-done.5
  6.2 10.4 %gram.1 = (f32[4,2,128,128]{3,2,1,0:T(8,128)S(1)}, bf16[2,256,768]{2,1,0:T(8,128)(2,1)S(1)}) custom-call(bf16[12288,128]{1,0:T(8,128)(2,1)S(1)} %get-tuple-element.17.x_ref, f32[864,128]{1,0:T(8,128)S(1)} %get-tuple-element.18.u_ref, f32[64]{0:T(128)S(1)} %copy-done.5), custom_call_target="tpu_custom_call" | custom-call | flops 8000000000 | bytes 5000000 | tf_op jit(solution)/shard_map/gram/pallas_call | solution.py:269
  16.6 0.0 copy-start
  16.7 0.0 copy-start.1
  16.7 0.0 copy-start.2
  16.7 0.0 copy-start.3
  16.7 0.0 copy-start.4
  16.7 0.0 collective-permute-done.halo_ref
  16.7 0.9 %edge.1 = (f32[4,4,2,16,128]{4,3,2,1,0:T(8,128)S(1)}, f32[4,4,2,16,128]{4,3,2,1,0:T(8,128)S(1)}) custom-call(bf16[24,128,128]{2,1,0:T(8,128)(2,1)S(1)} %collective-permute-done.halo_ref, bf16[2,256,768]{2,1,0:T(8,128)(2,1)S(1)} %get-tuple-element.19.lhs_ref, f32[864,128]{1,0:T(8,128)S(1)} %get-tuple-element.18.u_ref, ...), custom_call_target="tpu_custom_call" | custom-call | flops 1000000000 | bytes 3000000 | tf_op jit(solution)/shard_map/edge/pallas_call | solution.py:338
  17.6 0.1 collective-permute-start.1
  17.7 1.5 %collective-permute-done.1.got_ref = f32[4,4,2,16,128]{4,3,2,1,0:T(8,128)S(1)} collective-permute-done((f32[4,4,2,16,128]{4,3,2,1,0:T(8,128)S(1)}, f32[4,4,2,16,128]{4,3,2,1,0:T(8,128)S(1)}, u32[]{:S(2)}, u32[]{:S(2)}) %collective-permute-start.1) | collective-permute-done | bytes 262176 | tf_op jit(solution)/shard_map/ppermute | solution.py:496
  19.2 0.9 %collective-permute-start.2 = (f32[4,2,16,128]{3,2,1,0:T(8,128)S(1)}, f32[4,2,16,128]{3,2,1,0:T(8,128)S(1)}, u32[]{:S(2)}, u32[]{:S(2)}) collective-permute-start(f32[4,2,16,128]{3,2,1,0:T(8,128)S(1)} %get-tuple-element.24), channel_id=1, source_target_pairs={{0,2},{1,3},{2,0},{3,1},{4,6},{5,7},{6,4},{7,5},{8,10},{9,11},{10,... | collective-permute-start | bytes 196616 | tf_op jit(solution)/shard_map/ppermute | solution.py:501
  20.2 1.5 %collective-permute-start.3 = (f32[4,2,16,128]{3,2,1,0:T(8,128)S(1)}, f32[4,2,16,128]{3,2,1,0:T(8,128)S(1)}, u32[]{:S(2)}, u32[]{:S(2)}) collective-permute-start(f32[4,2,16,128]{3,2,1,0:T(8,128)S(1)} %get-tuple-element.25), channel_id=1, source_target_pairs={{0,4},{1,5},{2,6},{3,7},{4,0},{5,1},{6,2},{7,3},{8,12},{9,13},{10,... | collective-permute-start | bytes 196616 | tf_op jit(solution)/shard_map/ppermute | solution.py:501
  21.7 1.1 %collective-permute-start.4 = (f32[4,2,16,128]{3,2,1,0:T(8,128)S(1)}, f32[4,2,16,128]{3,2,1,0:T(8,128)S(1)}, u32[]{:S(2)}, u32[]{:S(2)}) collective-permute-start(f32[4,2,16,128]{3,2,1,0:T(8,128)S(1)} %get-tuple-element.26), channel_id=1, source_target_pairs={{0,6},{1,7},{2,4},{3,5},{4,2},{5,3},{6,0},{7,1},{8,14},{9,15},{10,... | collective-permute-start | bytes 196616 | tf_op jit(solution)/shard_map/ppermute | solution.py:501
  22.8 0.8 %collective-permute-done.2.refs_1_ = f32[4,2,16,128]{3,2,1,0:T(8,128)S(1)} collective-permute-done((f32[4,2,16,128]{3,2,1,0:T(8,128)S(1)}, f32[4,2,16,128]{3,2,1,0:T(8,128)S(1)}, u32[]{:S(2)}, u32[]{:S(2)}) %collective-permute-start.2) | collective-permute-done | bytes 65568 | tf_op jit(solution)/shard_map/ppermute | solution.py:501
  23.6 0.9 %collective-permute-done.3.refs_2_ = f32[4,2,16,128]{3,2,1,0:T(8,128)S(1)} collective-permute-done((f32[4,2,16,128]{3,2,1,0:T(8,128)S(1)}, f32[4,2,16,128]{3,2,1,0:T(8,128)S(1)}, u32[]{:S(2)}, u32[]{:S(2)}) %collective-permute-start.3) | collective-permute-done | bytes 65568 | tf_op jit(solution)/shard_map/ppermute | solution.py:501
  24.4 2.4 %collective-permute-done.4.refs_3_ = f32[4,2,16,128]{3,2,1,0:T(8,128)S(1)} collective-permute-done((f32[4,2,16,128]{3,2,1,0:T(8,128)S(1)}, f32[4,2,16,128]{3,2,1,0:T(8,128)S(1)}, u32[]{:S(2)}, u32[]{:S(2)}) %collective-permute-start.4) | collective-permute-done | bytes 65568 | tf_op jit(solution)/shard_map/ppermute | solution.py:501
  26.9 1.6 %collective-permute-start.5 = (bf16[4,2,16,128]{3,2,1,0:T(8,128)(2,1)S(1)}, bf16[4,2,16,128]{3,2,1,0:T(8,128)(2,1)S(1)}, u32[]{:S(2)}, u32[]{:S(2)}) collective-permute-start(bf16[4,2,16,128]{3,2,1,0:T(8,128)(2,1)S(1)} %total.1.refs_0_), channel_id=1, source_target_pairs={{0,8},{8,0},{16,24},{24,16},{1,9},{9,1},{17,25},{25,17},{2,10},{10... | collective-permute-start | bytes 98312 | tf_op jit(solution)/shard_map/ppermute | solution.py:506
  28.5 2.6 %collective-permute-start.6 = (bf16[4,2,16,128]{3,2,1,0:T(8,128)(2,1)S(1)}, bf16[4,2,16,128]{3,2,1,0:T(8,128)(2,1)S(1)}, u32[]{:S(2)}, u32[]{:S(2)}) collective-permute-start(bf16[4,2,16,128]{3,2,1,0:T(8,128)(2,1)S(1)} %total.1.refs_0_), channel_id=1, source_target_pairs={{0,16},{8,24},{16,0},{24,8},{1,17},{9,25},{17,1},{25,9},{2,18},{10... | collective-permute-start | bytes 98312 | tf_op jit(solution)/shard_map/ppermute | solution.py:506
  31.1 0.2 collective-permute-start.7
  31.3 0.0 copy-done
  31.3 0.0 copy-done.1
  31.3 0.0 copy-done.2
  31.3 0.0 copy-done.3
  31.3 1.6 %table.1.table_ref = s32[73]{0:T(128)S(1)} custom-call(s32[96]{0:T(128)S(1)} %bitcast.13, s32[96]{0:T(128)S(1)} %copy-done.1, s32[96]{0:T(128)S(1)} %copy-done.2, s32[96]{0:T(128)S(1)} %copy-done.3), custom_call_target="tpu_custom_call" | custom-call | flops 100000 | bytes 10000 | tf_op jit(solution)/shard_map/table/pallas_call | solution.py:409
  32.9 0.0 collective-permute-done.5.refs_1_
  33.0 0.6 %collective-permute-done.6.refs_2_ = bf16[4,2,16,128]{3,2,1,0:T(8,128)(2,1)S(1)} collective-permute-done((bf16[4,2,16,128]{3,2,1,0:T(8,128)(2,1)S(1)}, bf16[4,2,16,128]{3,2,1,0:T(8,128)(2,1)S(1)}, u32[]{:S(2)}, u32[]{:S(2)}) %collective-permute-start.6) | collective-permute-done | bytes 32800 | tf_op jit(solution)/shard_map/ppermute | solution.py:506
  33.6 3.2 %collective-permute-done.7.refs_3_ = bf16[4,2,16,128]{3,2,1,0:T(8,128)(2,1)S(1)} collective-permute-done((bf16[4,2,16,128]{3,2,1,0:T(8,128)(2,1)S(1)}, bf16[4,2,16,128]{3,2,1,0:T(8,128)(2,1)S(1)}, u32[]{:S(2)}, u32[]{:S(2)}) %collective-permute-start.7) | collective-permute-done | bytes 32800 | tf_op jit(solution)/shard_map/ppermute | solution.py:506
  36.8 0.0 copy-done.4
  36.8 1.9 %dress.1 = bf16[4,18,2,16,128]{4,3,2,1,0:T(8,128)(2,1)} custom-call(s32[73]{0:T(128)S(1)} %table.1.table_ref, bf16[8,2,128,128]{3,2,1,0:T(8,128)(2,1)S(1)} %bitcast.14, bf16[4,2,16,128]{3,2,1,0:T(8,128)(2,1)S(1)} %total.1.refs_0_, bf16[4,2,16,128]{3,2,1,0:T(8,128)(2,1)S(1)} %collective-permute-done.5.refs_1_, ...), custom_call_target="tpu_custom_call" | custom-call | flops 1000000000 | bytes 2000000 | tf_op jit(solution)/shard_map/dress/pallas_call | solution.py:449
  (3 shorter events, 0.0 us)
Async XLA Ops:
  0.0 6.2 %copy-start.5 = (f32[64]{0:T(128)S(1)}, f32[64]{0:T(128)}, u32[]{:S(2)}) copy-start(f32[64]{0:T(128)} %constant.2.clone.phase_ref) | copy-start | bytes 772
  2.8 13.9 %collective-permute-start = (bf16[24,128,128]{2,1,0:T(8,128)(2,1)S(1)}, bf16[24,128,128]{2,1,0:T(8,128)(2,1)S(1)}, u32[]{:S(2)}, u32[]{:S(2)}) collective-permute-start(bf16[24,128,128]{2,1,0:T(8,128)(2,1)S(1)} %get-tuple-element.16), channel_id=1, source_target_pairs={{0,7},{1,0},{2,1},{3,2},{4,3},{5,4},{6,5},{7,6},{8,15},{9,8},{10,9... | collective-permute-start | bytes 2359304 | tf_op jit(solution)/shard_map/ppermute | solution.py:491
  16.6 14.7 %copy-start = (s32[96,1]{0,1:T(1,128)S(1)}, s32[96,1]{0,1:T(1,128)}, u32[]{:S(2)}) copy-start(s32[96,1]{0,1:T(1,128)} %param.11) | copy-start | bytes 1156
  16.7 14.7 %copy-start.1 = (s32[96]{0:T(128)S(1)}, s32[96]{0:T(128)}, u32[]{:S(2)}) copy-start(s32[96]{0:T(128)} %elem_ref.1) | copy-start | bytes 1156
  16.7 14.7 %copy-start.2 = (s32[96]{0:T(128)S(1)}, s32[96]{0:T(128)}, u32[]{:S(2)}) copy-start(s32[96]{0:T(128)} %source_ref.1) | copy-start | bytes 1156
  16.7 14.7 %copy-start.3 = (s32[96]{0:T(128)S(1)}, s32[96]{0:T(128)}, u32[]{:S(2)}) copy-start(s32[96]{0:T(128)} %spin_ref.1) | copy-start | bytes 1156
  16.7 20.1 %copy-start.4 = (bf16[2,4,2,128,128]{4,3,2,1,0:T(8,128)(2,1)S(1)}, bf16[2,4,2,128,128]{4,3,2,1,0:T(8,128)(2,1)}, u32[]{:S(2)}) copy-start(bf16[2,4,2,128,128]{4,3,2,1,0:T(8,128)(2,1)} %param.10) | copy-start | bytes 1572868
  17.6 1.6 %collective-permute-start.1 = (f32[4,4,2,16,128]{4,3,2,1,0:T(8,128)S(1)}, f32[4,4,2,16,128]{4,3,2,1,0:T(8,128)S(1)}, u32[]{:S(2)}, u32[]{:S(2)}) collective-permute-start(f32[4,4,2,16,128]{4,3,2,1,0:T(8,128)S(1)} %get-tuple-element.22), channel_id=1, source_target_pairs={{0,1},{1,0},{2,3},{3,2},{4,5},{5,4},{6,7},{7,6},{8,9},{9,8},{10,11... | collective-permute-start | bytes 786440 | tf_op jit(solution)/shard_map/ppermute | solution.py:496
  19.2 4.3 %collective-permute-start.2 = (f32[4,2,16,128]{3,2,1,0:T(8,128)S(1)}, f32[4,2,16,128]{3,2,1,0:T(8,128)S(1)}, u32[]{:S(2)}, u32[]{:S(2)}) collective-permute-start(f32[4,2,16,128]{3,2,1,0:T(8,128)S(1)} %get-tuple-element.24), channel_id=1, source_target_pairs={{0,2},{1,3},{2,0},{3,1},{4,6},{5,7},{6,4},{7,5},{8,10},{9,11},{10,... | collective-permute-start | bytes 196616 | tf_op jit(solution)/shard_map/ppermute | solution.py:501
  20.2 4.3 %collective-permute-start.3 = (f32[4,2,16,128]{3,2,1,0:T(8,128)S(1)}, f32[4,2,16,128]{3,2,1,0:T(8,128)S(1)}, u32[]{:S(2)}, u32[]{:S(2)}) collective-permute-start(f32[4,2,16,128]{3,2,1,0:T(8,128)S(1)} %get-tuple-element.25), channel_id=1, source_target_pairs={{0,4},{1,5},{2,6},{3,7},{4,0},{5,1},{6,2},{7,3},{8,12},{9,13},{10,... | collective-permute-start | bytes 196616 | tf_op jit(solution)/shard_map/ppermute | solution.py:501
  21.7 5.2 %collective-permute-start.4 = (f32[4,2,16,128]{3,2,1,0:T(8,128)S(1)}, f32[4,2,16,128]{3,2,1,0:T(8,128)S(1)}, u32[]{:S(2)}, u32[]{:S(2)}) collective-permute-start(f32[4,2,16,128]{3,2,1,0:T(8,128)S(1)} %get-tuple-element.26), channel_id=1, source_target_pairs={{0,6},{1,7},{2,4},{3,5},{4,2},{5,3},{6,0},{7,1},{8,14},{9,15},{10,... | collective-permute-start | bytes 196616 | tf_op jit(solution)/shard_map/ppermute | solution.py:501
  26.9 6.1 %collective-permute-start.5 = (bf16[4,2,16,128]{3,2,1,0:T(8,128)(2,1)S(1)}, bf16[4,2,16,128]{3,2,1,0:T(8,128)(2,1)S(1)}, u32[]{:S(2)}, u32[]{:S(2)}) collective-permute-start(bf16[4,2,16,128]{3,2,1,0:T(8,128)(2,1)S(1)} %total.1.refs_0_), channel_id=1, source_target_pairs={{0,8},{8,0},{16,24},{24,16},{1,9},{9,1},{17,25},{25,17},{2,10},{10... | collective-permute-start | bytes 98312 | tf_op jit(solution)/shard_map/ppermute | solution.py:506
  28.5 5.1 %collective-permute-start.6 = (bf16[4,2,16,128]{3,2,1,0:T(8,128)(2,1)S(1)}, bf16[4,2,16,128]{3,2,1,0:T(8,128)(2,1)S(1)}, u32[]{:S(2)}, u32[]{:S(2)}) collective-permute-start(bf16[4,2,16,128]{3,2,1,0:T(8,128)(2,1)S(1)} %total.1.refs_0_), channel_id=1, source_target_pairs={{0,16},{8,24},{16,0},{24,8},{1,17},{9,25},{17,1},{25,9},{2,18},{10... | collective-permute-start | bytes 98312 | tf_op jit(solution)/shard_map/ppermute | solution.py:506
  31.1 5.7 %collective-permute-start.7 = (bf16[4,2,16,128]{3,2,1,0:T(8,128)(2,1)S(1)}, bf16[4,2,16,128]{3,2,1,0:T(8,128)(2,1)S(1)}, u32[]{:S(2)}, u32[]{:S(2)}) collective-permute-start(bf16[4,2,16,128]{3,2,1,0:T(8,128)(2,1)S(1)} %total.1.refs_0_), channel_id=1, source_target_pairs={{0,24},{8,16},{16,8},{24,0},{1,25},{9,17},{17,9},{25,1},{2,26},{10... | collective-permute-start | bytes 98312 | tf_op jit(solution)/shard_map/ppermute | solution.py:506

commit v3 on v1

--- a/solution.py
+++ b/solution.py
@@ -104,13 +104,12 @@
 
 def link_product(links, vec_re, vec_im):
     plus = [vec_re[c] + vec_im[c] for c in range(3)]
-    minus = [vec_im[c] - vec_re[c] for c in range(3)]
     outs_re, outs_im = [], []
     for row in range(3):
-        link_re, link_im, link_sum = links[0][row], links[1][row], links[2][row]
-        one = link_sum[0] * vec_re[0] + link_sum[1] * vec_re[1] + link_sum[2] * vec_re[2]
-        two = link_re[0] * minus[0] + link_re[1] * minus[1] + link_re[2] * minus[2]
-        three = link_im[0] * plus[0] + link_im[1] * plus[1] + link_im[2] * plus[2]
+        link_re, link_less, link_more = links[0][row], links[1][row], links[2][row]
+        one = link_re[0] * plus[0] + link_re[1] * plus[1] + link_re[2] * plus[2]
+        two = link_less[0] * vec_re[0] + link_less[1] * vec_re[1] + link_less[2] * vec_re[2]
+        three = link_more[0] * vec_im[0] + link_more[1] * vec_im[1] + link_more[2] * vec_im[2]
         outs_re.append(one - three)
         outs_im.append(one + two)
     return outs_re, outs_im
@@ -122,8 +121,37 @@
         return jnp.broadcast_to(u_ref[pl.ds(at, 1), :], (8, LANES))
 
     grid = [[[one(part, row, col) for col in range(3)] for row in range(3)] for part in range(2)]
-    total = [[grid[0][row][col] + grid[1][row][col] for col in range(3)] for row in range(3)]
-    return grid + [total]
+    less = [[grid[1][row][col] - grid[0][row][col] for col in range(3)] for row in range(3)]
+    more = [[grid[1][row][col] + grid[0][row][col] for col in range(3)] for row in range(3)]
+    return grid[0], less, more
+
+
+def fill_table(groups, slots, empty, owner_ref, elem_ref, source_ref, spin_ref, table_ref):
+    total = owner_ref.shape[1]
+    jobs = total // groups
+    row = lax.broadcasted_iota(jnp.int32, (total, total), 0)
+    col = lax.broadcasted_iota(jnp.int32, (total, total), 1)
+
+    def group_of(index):
+        return sum((index >= group * jobs).astype(jnp.int32) for group in range(1, groups))
+
+    live = jnp.where(owner_ref[...] == lax.axis_index("tm"), 1.0, 0.0)
+    product = source_ref[...] * (SPIN * groups * OPS) + spin_ref[...] * (groups * OPS) + elem_ref[...]
+
+    def column(mask, values):
+        wide = jnp.broadcast_to(values.astype(F32), (total, total))
+        return jnp.sum(jnp.where(mask, wide, 0.0), axis=1, keepdims=True)
+
+    rank = column((col < row) & (group_of(col) == group_of(row)), live)
+    alive = column(col == row, live)
+    value = column(col == row, product)
+    at_row = lax.broadcasted_iota(jnp.int32, (total, LANES), 0)
+    at_col = lax.broadcasted_iota(jnp.int32, (total, LANES), 1)
+    group = group_of(at_row).astype(F32)
+    place = jnp.where(alive > 0.5, group * slots + rank, -1.0)
+    found = at_col.astype(F32) == place
+    picked = jnp.sum(jnp.where(found, value + group * OPS - empty, 0.0), axis=0, keepdims=True)
+    table_ref[...] = (picked + empty).astype(jnp.int32)
 
 
 def paired(grid, count):
@@ -146,9 +174,6 @@
     pair = 2
     halves = tiles // pair
     steps = planes * halves
-    total_jobs = owner_ref.shape[0]
-    jobs = total_jobs // groups
-    me = lax.axis_index("tm")
 
     def source(row):
         spot = row // GROUP
@@ -157,8 +182,6 @@
     pick_ref[...] = pick_matrix(GROUP * spots, GROUP * spots, source)
     acc_ref[...] = jnp.zeros_like(acc_ref)
     g_ref[...] = jnp.zeros_like(g_ref)
-    for at in range(groups * slots):
-        table_ref[at] = empty
 
     chosen = pick_ref[...]
     for at in range(0, count, GROUP):
@@ -226,18 +249,11 @@
 
     def multiply(step, slot, directions):
         fixed = lhs_ref[step]
-        g_ref[step // halves] += nt_dot(fixed, fixed)
         low = min(directions) * 2 * count
         high = (max(directions) + 1) * 2 * count
-        acc_ref[low:high, :] += nt_dot(op_ref[slot, low:high, :], fixed)
-
-    def place(group):
-        used = jnp.int32(0)
-        for at in range(group * jobs, (group + 1) * jobs):
-            mine = owner_ref[at] == me
-            product = source_ref[at] * (SPIN * groups * OPS) + spin_ref[at] * (groups * OPS) + elem_ref[at]
-            table_ref[jnp.where(mine, group * slots + used, groups * slots)] = product + group * OPS
-            used = used + jnp.where(mine, 1, 0)
+        got = nt_dot(jnp.concatenate([fixed, op_ref[slot, low:high, :]], axis=0), fixed)
+        g_ref[step // halves] += got[: 2 * count]
+        acc_ref[low:high, :] += got[2 * count :]
 
     every, side = (0, 1, 2), (1, 2)
     inner = steps - halves
@@ -254,8 +270,7 @@
     for step in range(inner, steps):
         elementwise(step, step & 1, side)
         multiply(step, step & 1, side)
-    for group in range(groups):
-        place(group)
+    fill_table(groups, slots, empty, owner_ref, elem_ref, source_ref, spin_ref, table_ref)
 
     first = lax.axis_index("space") * planes
     total_re = jnp.zeros((count, count), F32)
@@ -284,12 +299,12 @@
     wide = pair * 3 * LANES
     return pl.pallas_call(
         partial(gram_kernel, count, tiles, planes, lx, groups, slots, empty),
-        in_specs=[vspec(), vspec()] + [sspec()] * 5,
-        out_specs=[vspec(), vspec(), sspec()],
+        in_specs=[vspec()] * 2 + [sspec()] + [vspec()] * 4,
+        out_specs=[vspec()] * 3,
         out_shape=[
             jax.ShapeDtypeStruct((OPS, 2, count, count), F32),
             jax.ShapeDtypeStruct((tiles // pair, 2 * count, wide), BF16),
-            jax.ShapeDtypeStruct((groups * slots + 1,), jnp.int32),
+            jax.ShapeDtypeStruct((1, LANES), jnp.int32),
         ],
         scratch_shapes=[
             VMEM((spots * 6, count, LANES), F32),
@@ -367,33 +382,44 @@
     )(halo, rim_lhs, u, sums)
 
 
-def fold_kernel(chips, keep_ref, got_ref, own_ref, *out_refs):
-    me = lax.axis_index("space") // 2
+def split_sum(block):
+    high = block[0:1].astype(BF16)
+    low = (block[0:1] - high.astype(F32)).astype(BF16)
+    return jnp.concatenate([high, low, block[1:].astype(BF16)], axis=0)
+
+
+def fold_kernel(chips, cores, keep_ref, got_ref, own_ref, *out_refs):
+    me = lax.axis_index("space") // cores
     own_ref[...] = keep_ref[me] + got_ref[me]
     for step in range(1, chips):
         to = me ^ step
-        out_refs[step - 1][...] = keep_ref[to] + got_ref[to]
-
-
-def fold(keep, got):
+        out_refs[step - 1][...] = split_sum(keep_ref[to] + got_ref[to])
+
+
+def fold(keep, got, cores):
     chips = keep.shape[0]
-    shape = jax.ShapeDtypeStruct(keep.shape[1:], F32)
+    shape = keep.shape[1:]
+    sent = jax.ShapeDtypeStruct((shape[0] + 1,) + shape[1:], BF16)
     return pl.pallas_call(
-        partial(fold_kernel, chips),
+        partial(fold_kernel, chips, cores),
         in_specs=[vspec()] * 2,
         out_specs=[vspec()] * chips,
-        out_shape=[shape] * chips,
+        out_shape=[jax.ShapeDtypeStruct(shape, F32)] + [sent] * (chips - 1),
         compiler_params=limit(4),
         cost_estimate=cost(10**6, 10**6),
         name="fold",
     )(keep, got)
 
 
-def total_kernel(*refs):
-    total = refs[0][...]
-    for ref in refs[1:-1]:
-        total = total + ref[...]
-    refs[-1][...] = total.astype(BF16)
+def total_kernel(own_ref, *refs):
+    total_ref = refs[-1]
+    first = own_ref[0:1]
+    rest = own_ref[1:]
+    for ref in refs[:-1]:
+        first = first + (ref[0:1].astype(F32) + ref[1:2].astype(F32))
+        rest = rest + ref[2:].astype(F32)
+    total_ref[0:1] = first.astype(BF16)
+    total_ref[1:] = rest.astype(BF16)
 
 
 def total_rows(parts):
@@ -430,7 +456,7 @@
     prod_ref[taus * groups * OPS] = jnp.zeros((rows, 2 * count), BF16)
     for group in range(groups):
         for slot in range(slots):
-            piece = prod_ref[table_ref[group * slots + slot]]
+            piece = prod_ref[table_ref[0, group * slots + slot]]
             out_ref[group, slot, 0] = piece[:, :count]
             out_ref[group, slot, 1] = piece[:, count:]
 
@@ -476,15 +502,17 @@
 
     per = perambulator.reshape(-1, 2, count, count)
     empty = per.shape[0] * groups * OPS
+    x = pltpu.with_memory_space_constraint(x, pltpu.HBM)
+    u = pltpu.with_memory_space_constraint(u, pltpu.HBM)
     rim, x, u = rim_plane(x, u, count, tiles, planes)
     halo = lax.ppermute(rim, "space", [(i, (i - 1) % space_size) for i in range(space_size)])
-    tables = (job_owner.reshape(-1), job_elemental, job_source, job_spin)
+    tables = [job.reshape(1, -1) for job in (job_owner, job_elemental, job_source, job_spin)]
     sums, rim_lhs, table = gram(
         x, u, phases, tables, count, tiles, planes, lx, groups, slots, empty
     )
     keep, send = edge(halo, rim_lhs, u, sums, count, tiles, planes, rows, cores)
     got = lax.ppermute(send, "space", [(i, i ^ 1) for i in range(space_size)])
-    parts = fold(keep, got)
+    parts = fold(keep, got, cores)
     summed = [parts[0]]
     for step in range(1, space_size // cores):
         summed.append(
@@ -637,9 +665,10 @@
     count, planes, sites = eigvecs.shape[1], eigvecs.shape[4], eigvecs.shape[5]
     space_size, groups = lax.axis_size("space"), lax.axis_size("tm")
     whole_tiles = sites % (2 * LANES) == 0 and count == LANES and planes * (sites // LANES) == GROUP
+    fits = groups * 3 * ((JOB_DEV + groups - 1) // groups) < LANES
     powers = space_size & (space_size - 1) == 0 and groups & (groups - 1) == 0
-    small = space_size * GROUP == count and groups <= 8
-    if whole_tiles and powers and small and eigvecs.shape[0] == 1:
+    small = space_size * GROUP == count and groups <= 8 and args[3].shape[0] <= LANES
+    if whole_tiles and fits and powers and small and eigvecs.shape[0] == 1:
         return fast_shards(*args)
     return plain_shards(*args)
 

time: 41.2 us -> 37.2 us (0.903)
  local copies, waits for them, and re-layouts: 2.98 us -> 0.02 us
  Pallas kernels: 17.9 us -> 16.4 us
  waiting for transfers between devices: 8.51 us -> 9.04 us
    unnamed x16 -> x12, local copies, waits for them, and re-layouts: 2.98 us -> 0.02 us
    pallas_call x1, Pallas kernels: 11.6 us -> 10.8 us  [gram(): pl.pallas_call(partial(gram_kernel, count, tiles, planes, lx, groups, slo...]
    pallas_call x1, Pallas kernels: 3.5 us -> 2.81 us  [rim_plane(): pl.pallas_call(partial(rim_kernel, tiles, planes), in_specs=[pl.BlockSpec...]
    ppermute x3, waiting for transfers between devices: 2.96 us -> 3.49 us  [fast_shards(): lax.ppermute(parts[step], 'space', [(i, i ^ step * cores) for i in range(...]
  transfers between devices with their start and end apart: 8 -> 8, of which waited for: 5 -> 6; matrix products, arithmetic and copies ran while one was open for 0% -> 0% of each run, Pallas kernels for 28% -> 29%
where the time goes in v3:
time: 37.2 us; the launch traced here: 37.1 us
  Pallas kernels  16.4 us (44%)
  starting transfers between devices  11.5 us (31%)
  waiting for transfers between devices  9.04 us (24%)
    pallas_call x1, Pallas kernels, gram(): pl.pallas_call(partial(gram_kernel, count, tiles, planes, lx, groups, slo...  10.8 us
    ppermute x3, starting transfers between devices, fast_shards(): lax.ppermute(own, 'tm', [(i, i ^ step) for i in range(groups)])  4.45 us
    ppermute x3, waiting for transfers between devices, fast_shards(): lax.ppermute(own, 'tm', [(i, i ^ step) for i in range(groups)])  4.03 us
    ppermute x3, starting transfers between devices, fast_shards(): lax.ppermute(parts[step], 'space', [(i, i ^ step * cores) for i in range(...  3.55 us
    ppermute x3, waiting for transfers between devices, fast_shards(): lax.ppermute(parts[step], 'space', [(i, i ^ step * cores) for i in range(...  3.49 us
    ppermute x1, starting transfers between devices, fast_shards(): lax.ppermute(rim, 'space', [(i, (i - 1) % space_size) for i in range(spac...  3.41 us
    pallas_call x1, Pallas kernels, rim_plane(): pl.pallas_call(partial(rim_kernel, tiles, planes), in_specs=[pl.BlockSpec...  2.81 us
    pallas_call x1, Pallas kernels, dress(): pl.pallas_call(partial(dress_kernel, groups, slots, taus, rows, count), i...  1.9 us
  transfers between devices with their start and end apart: 8, of which 6 were waited for; matrix products, arithmetic and copies ran while one was open for 0% of the time, Pallas kernels for 29%

profile of v3, /device:TPU:0, one launch (start us, length us, event | category | flops | bytes accessed | tf_op | source)
XLA Modules:
  0.0 37.1 jit_solution(14399598232916352602)
XLA Ops:
  0.0 0.0 copy-start.5
  0.0 0.0 copy-start.4
  0.0 0.0 copy-start.3
  0.0 0.0 copy-start.2
  0.0 0.0 copy-start.1
  0.0 2.8 %rim.1 = (bf16[24,128,128]{2,1,0:T(8,128)(2,1)S(1)}, bf16[12288,128]{1,0:T(8,128)(2,1)S(1)}, f32[864,128]{1,0:T(8,128)S(1)}) custom-call(bf16[12288,128]{1,0:T(8,128)(2,1)} %bitcast.21, f32[864,128]{1,0:T(8,128)} %bitcast.22), custom_call_target="tpu_custom_call" | custom-call | flops 100000000 | bytes 4000000 | tf_op jit(solution)/shard_map/rim/pallas_call | solution.py:86
  2.8 3.4 %collective-permute-start = (bf16[24,128,128]{2,1,0:T(8,128)(2,1)S(1)}, bf16[24,128,128]{2,1,0:T(8,128)(2,1)S(1)}, u32[]{:S(2)}, u32[]{:S(2)}) collective-permute-start(bf16[24,128,128]{2,1,0:T(8,128)(2,1)S(1)} %get-tuple-element.20), channel_id=1, source_target_pairs={{0,7},{1,0},{2,1},{3,2},{4,3},{5,4},{6,5},{7,6},{8,15},{9,8},{10,9... | collective-permute-start | bytes 2359304 | tf_op jit(solution)/shard_map/ppermute | solution.py:508
  6.2 0.0 copy-done.5
  6.2 0.0 copy-done.4
  6.3 0.0 copy-done.3
  6.3 0.0 copy-done.2
  6.3 0.0 copy-done.1
  6.3 10.8 %gram.1 = (f32[4,2,128,128]{3,2,1,0:T(8,128)S(1)}, bf16[2,256,768]{2,1,0:T(8,128)(2,1)S(1)}, s32[1,128]{1,0:T(1,128)S(1)}) custom-call(bf16[12288,128]{1,0:T(8,128)(2,1)S(1)} %get-tuple-element.17.x_ref, f32[864,128]{1,0:T(8,128)S(1)} %get-tuple-element.18.u_ref, f32[64]{0:T(128)S(1)} %copy-done.5, s32[1,96]{1,0:T(1,128)S(1)} %bitcast.17, ...), custom_call_target="tpu_custom_call" | custom-call | flops 8000000000 | bytes 5000000 | tf_op jit(solution)/shard_map/gram/pallas_call | solution.py:300
  17.0 0.0 copy-start
  17.1 0.0 collective-permute-done.halo_ref
  17.1 0.9 %edge.1 = (f32[4,4,2,16,128]{4,3,2,1,0:T(8,128)S(1)}, f32[4,4,2,16,128]{4,3,2,1,0:T(8,128)S(1)}) custom-call(bf16[24,128,128]{2,1,0:T(8,128)(2,1)S(1)} %collective-permute-done.halo_ref, bf16[2,256,768]{2,1,0:T(8,128)(2,1)S(1)} %get-tuple-element.21.lhs_ref, f32[864,128]{1,0:T(8,128)S(1)} %get-tuple-element.18.u_ref, ...), custom_call_target="tpu_custom_call" | custom-call | flops 1000000000 | bytes 3000000 | tf_op jit(solution)/shard_map/edge/pallas_call | solution.py:370
  18.0 0.1 collective-permute-start.1
  18.1 1.5 %collective-permute-done.1.got_ref = f32[4,4,2,16,128]{4,3,2,1,0:T(8,128)S(1)} collective-permute-done((f32[4,4,2,16,128]{4,3,2,1,0:T(8,128)S(1)}, f32[4,4,2,16,128]{4,3,2,1,0:T(8,128)S(1)}, u32[]{:S(2)}, u32[]{:S(2)}) %collective-permute-start.1) | collective-permute-done | bytes 262176 | tf_op jit(solution)/shard_map/ppermute | solution.py:514
  19.6 0.6 %collective-permute-start.2 = (bf16[5,2,16,128]{3,2,1,0:T(8,128)(2,1)S(1)}, bf16[5,2,16,128]{3,2,1,0:T(8,128)(2,1)S(1)}, u32[]{:S(2)}, u32[]{:S(2)}) collective-permute-start(bf16[5,2,16,128]{3,2,1,0:T(8,128)(2,1)S(1)} %get-tuple-element.26), channel_id=1, source_target_pairs={{0,2},{1,3},{2,0},{3,1},{4,6},{5,7},{6,4},{7,5},{8,10},{9,11},{10,... | collective-permute-start | bytes 122888 | tf_op jit(solution)/shard_map/ppermute | solution.py:519
  20.2 1.5 %collective-permute-start.3 = (bf16[5,2,16,128]{3,2,1,0:T(8,128)(2,1)S(1)}, bf16[5,2,16,128]{3,2,1,0:T(8,128)(2,1)S(1)}, u32[]{:S(2)}, u32[]{:S(2)}) collective-permute-start(bf16[5,2,16,128]{3,2,1,0:T(8,128)(2,1)S(1)} %get-tuple-element.27), channel_id=1, source_target_pairs={{0,4},{1,5},{2,6},{3,7},{4,0},{5,1},{6,2},{7,3},{8,12},{9,13},{10,... | collective-permute-start | bytes 122888 | tf_op jit(solution)/shard_map/ppermute | solution.py:519
  21.8 1.4 %collective-permute-start.4 = (bf16[5,2,16,128]{3,2,1,0:T(8,128)(2,1)S(1)}, bf16[5,2,16,128]{3,2,1,0:T(8,128)(2,1)S(1)}, u32[]{:S(2)}, u32[]{:S(2)}) collective-permute-start(bf16[5,2,16,128]{3,2,1,0:T(8,128)(2,1)S(1)} %get-tuple-element.28), channel_id=1, source_target_pairs={{0,6},{1,7},{2,4},{3,5},{4,2},{5,3},{6,0},{7,1},{8,14},{9,15},{10,... | collective-permute-start | bytes 122888 | tf_op jit(solution)/shard_map/ppermute | solution.py:519
  23.2 0.5 %collective-permute-done.2.refs_0_ = bf16[5,2,16,128]{3,2,1,0:T(8,128)(2,1)S(1)} collective-permute-done((bf16[5,2,16,128]{3,2,1,0:T(8,128)(2,1)S(1)}, bf16[5,2,16,128]{3,2,1,0:T(8,128)(2,1)S(1)}, u32[]{:S(2)}, u32[]{:S(2)}) %collective-permute-start.2) | collective-permute-done | bytes 40992 | tf_op jit(solution)/shard_map/ppermute | solution.py:519
  23.7 0.6 %collective-permute-done.3.refs_1_ = bf16[5,2,16,128]{3,2,1,0:T(8,128)(2,1)S(1)} collective-permute-done((bf16[5,2,16,128]{3,2,1,0:T(8,128)(2,1)S(1)}, bf16[5,2,16,128]{3,2,1,0:T(8,128)(2,1)S(1)}, u32[]{:S(2)}, u32[]{:S(2)}) %collective-permute-start.3) | collective-permute-done | bytes 40992 | tf_op jit(solution)/shard_map/ppermute | solution.py:519
  24.2 2.4 %collective-permute-done.4.refs_2_ = bf16[5,2,16,128]{3,2,1,0:T(8,128)(2,1)S(1)} collective-permute-done((bf16[5,2,16,128]{3,2,1,0:T(8,128)(2,1)S(1)}, bf16[5,2,16,128]{3,2,1,0:T(8,128)(2,1)S(1)}, u32[]{:S(2)}, u32[]{:S(2)}) %collective-permute-start.4) | collective-permute-done | bytes 40992 | tf_op jit(solution)/shard_map/ppermute | solution.py:519
  26.7 3.7 %collective-permute-start.7 = (bf16[4,2,16,128]{3,2,1,0:T(8,128)(2,1)S(1)}, bf16[4,2,16,128]{3,2,1,0:T(8,128)(2,1)S(1)}, u32[]{:S(2)}, u32[]{:S(2)}) collective-permute-start(bf16[4,2,16,128]{3,2,1,0:T(8,128)(2,1)S(1)} %total.1.refs_0_), channel_id=1, source_target_pairs={{0,24},{8,16},{16,8},{24,0},{1,25},{9,17},{17,9},{25,1},{2,26},{10... | collective-permute-start | bytes 98312 | tf_op jit(solution)/shard_map/ppermute | solution.py:524
  30.4 0.0 collective-permute-start.6
  30.4 0.8 %collective-permute-start.5 = (bf16[4,2,16,128]{3,2,1,0:T(8,128)(2,1)S(1)}, bf16[4,2,16,128]{3,2,1,0:T(8,128)(2,1)S(1)}, u32[]{:S(2)}, u32[]{:S(2)}) collective-permute-start(bf16[4,2,16,128]{3,2,1,0:T(8,128)(2,1)S(1)} %total.1.refs_0_), channel_id=1, source_target_pairs={{0,8},{8,0},{16,24},{24,16},{1,9},{9,1},{17,25},{25,17},{2,10},{10... | collective-permute-start | bytes 98312 | tf_op jit(solution)/shard_map/ppermute | solution.py:524
  31.1 1.3 %collective-permute-done.7.refs_3_ = bf16[4,2,16,128]{3,2,1,0:T(8,128)(2,1)S(1)} collective-permute-done((bf16[4,2,16,128]{3,2,1,0:T(8,128)(2,1)S(1)}, bf16[4,2,16,128]{3,2,1,0:T(8,128)(2,1)S(1)}, u32[]{:S(2)}, u32[]{:S(2)}) %collective-permute-start.7) | collective-permute-done | bytes 32800 | tf_op jit(solution)/shard_map/ppermute | solution.py:524
  32.5 2.7 %collective-permute-done.6.refs_2_ = bf16[4,2,16,128]{3,2,1,0:T(8,128)(2,1)S(1)} collective-permute-done((bf16[4,2,16,128]{3,2,1,0:T(8,128)(2,1)S(1)}, bf16[4,2,16,128]{3,2,1,0:T(8,128)(2,1)S(1)}, u32[]{:S(2)}, u32[]{:S(2)}) %collective-permute-start.6) | collective-permute-done | bytes 32800 | tf_op jit(solution)/shard_map/ppermute | solution.py:524
  35.2 0.0 collective-permute-done.5.refs_1_
  35.2 0.0 copy-done
  35.2 1.9 %dress.1 = bf16[4,18,2,16,128]{4,3,2,1,0:T(8,128)(2,1)} custom-call(s32[1,128]{1,0:T(1,128)S(1)} %get-tuple-element.19.table_ref, bf16[8,2,128,128]{3,2,1,0:T(8,128)(2,1)S(1)} %bitcast.16, bf16[4,2,16,128]{3,2,1,0:T(8,128)(2,1)S(1)} %total.1.refs_0_, bf16[4,2,16,128]{3,2,1,0:T(8,128)(2,1)S(1)} %collective-permute-done.5.refs_1_, ...), custom_call_target="tpu_custom_call" | custom-call | flops 1000000000 | bytes 2000000 | tf_op jit(solution)/shard_map/dress/pallas_call | solution.py:466
  (2 shorter events, 0.0 us)
Async XLA Ops:
  0.0 6.2 %copy-start.5 = (f32[64]{0:T(128)S(1)}, f32[64]{0:T(128)}, u32[]{:S(2)}) copy-start(f32[64]{0:T(128)} %constant.2.clone.phase_ref) | copy-start | bytes 772
  0.0 6.2 %copy-start.4 = (s32[96]{0:T(128)S(1)}, s32[96]{0:T(128)}, u32[]{:S(2)}) copy-start(s32[96]{0:T(128)} %param.14) | copy-start | bytes 1156
  0.0 6.2 %copy-start.3 = (s32[96]{0:T(128)S(1)}, s32[96]{0:T(128)}, u32[]{:S(2)}) copy-start(s32[96]{0:T(128)} %param.13) | copy-start | bytes 1156
  0.0 6.2 %copy-start.2 = (s32[96]{0:T(128)S(1)}, s32[96]{0:T(128)}, u32[]{:S(2)}) copy-start(s32[96]{0:T(128)} %param.12) | copy-start | bytes 1156
  0.0 6.3 %copy-start.1 = (s32[96,1]{0,1:T(1,128)S(1)}, s32[96,1]{0,1:T(1,128)}, u32[]{:S(2)}) copy-start(s32[96,1]{0,1:T(1,128)} %param.11) | copy-start | bytes 1156
  2.8 14.2 %collective-permute-start = (bf16[24,128,128]{2,1,0:T(8,128)(2,1)S(1)}, bf16[24,128,128]{2,1,0:T(8,128)(2,1)S(1)}, u32[]{:S(2)}, u32[]{:S(2)}) collective-permute-start(bf16[24,128,128]{2,1,0:T(8,128)(2,1)S(1)} %get-tuple-element.20), channel_id=1, source_target_pairs={{0,7},{1,0},{2,1},{3,2},{4,3},{5,4},{6,5},{7,6},{8,15},{9,8},{10,9... | collective-permute-start | bytes 2359304 | tf_op jit(solution)/shard_map/ppermute | solution.py:508
  17.0 18.1 %copy-start = (bf16[2,4,2,128,128]{4,3,2,1,0:T(8,128)(2,1)S(1)}, bf16[2,4,2,128,128]{4,3,2,1,0:T(8,128)(2,1)}, u32[]{:S(2)}) copy-start(bf16[2,4,2,128,128]{4,3,2,1,0:T(8,128)(2,1)} %param.10) | copy-start | bytes 1572868
  18.0 1.6 %collective-permute-start.1 = (f32[4,4,2,16,128]{4,3,2,1,0:T(8,128)S(1)}, f32[4,4,2,16,128]{4,3,2,1,0:T(8,128)S(1)}, u32[]{:S(2)}, u32[]{:S(2)}) collective-permute-start(f32[4,4,2,16,128]{4,3,2,1,0:T(8,128)S(1)} %get-tuple-element.24), channel_id=1, source_target_pairs={{0,1},{1,0},{2,3},{3,2},{4,5},{5,4},{6,7},{7,6},{8,9},{9,8},{10,11... | collective-permute-start | bytes 786440 | tf_op jit(solution)/shard_map/ppermute | solution.py:514
  19.6 4.1 %collective-permute-start.2 = (bf16[5,2,16,128]{3,2,1,0:T(8,128)(2,1)S(1)}, bf16[5,2,16,128]{3,2,1,0:T(8,128)(2,1)S(1)}, u32[]{:S(2)}, u32[]{:S(2)}) collective-permute-start(bf16[5,2,16,128]{3,2,1,0:T(8,128)(2,1)S(1)} %get-tuple-element.26), channel_id=1, source_target_pairs={{0,2},{1,3},{2,0},{3,1},{4,6},{5,7},{6,4},{7,5},{8,10},{9,11},{10,... | collective-permute-start | bytes 122888 | tf_op jit(solution)/shard_map/ppermute | solution.py:519
  20.2 4.0 %collective-permute-start.3 = (bf16[5,2,16,128]{3,2,1,0:T(8,128)(2,1)S(1)}, bf16[5,2,16,128]{3,2,1,0:T(8,128)(2,1)S(1)}, u32[]{:S(2)}, u32[]{:S(2)}) collective-permute-start(bf16[5,2,16,128]{3,2,1,0:T(8,128)(2,1)S(1)} %get-tuple-element.27), channel_id=1, source_target_pairs={{0,4},{1,5},{2,6},{3,7},{4,0},{5,1},{6,2},{7,3},{8,12},{9,13},{10,... | collective-permute-start | bytes 122888 | tf_op jit(solution)/shard_map/ppermute | solution.py:519
  21.8 4.9 %collective-permute-start.4 = (bf16[5,2,16,128]{3,2,1,0:T(8,128)(2,1)S(1)}, bf16[5,2,16,128]{3,2,1,0:T(8,128)(2,1)S(1)}, u32[]{:S(2)}, u32[]{:S(2)}) collective-permute-start(bf16[5,2,16,128]{3,2,1,0:T(8,128)(2,1)S(1)} %get-tuple-element.28), channel_id=1, source_target_pairs={{0,6},{1,7},{2,4},{3,5},{4,2},{5,3},{6,0},{7,1},{8,14},{9,15},{10,... | collective-permute-start | bytes 122888 | tf_op jit(solution)/shard_map/ppermute | solution.py:519
  26.7 5.8 %collective-permute-start.7 = (bf16[4,2,16,128]{3,2,1,0:T(8,128)(2,1)S(1)}, bf16[4,2,16,128]{3,2,1,0:T(8,128)(2,1)S(1)}, u32[]{:S(2)}, u32[]{:S(2)}) collective-permute-start(bf16[4,2,16,128]{3,2,1,0:T(8,128)(2,1)S(1)} %total.1.refs_0_), channel_id=1, source_target_pairs={{0,24},{8,16},{16,8},{24,0},{1,25},{9,17},{17,9},{25,1},{2,26},{10... | collective-permute-start | bytes 98312 | tf_op jit(solution)/shard_map/ppermute | solution.py:524
  30.4 4.8 %collective-permute-start.6 = (bf16[4,2,16,128]{3,2,1,0:T(8,128)(2,1)S(1)}, bf16[4,2,16,128]{3,2,1,0:T(8,128)(2,1)S(1)}, u32[]{:S(2)}, u32[]{:S(2)}) collective-permute-start(bf16[4,2,16,128]{3,2,1,0:T(8,128)(2,1)S(1)} %total.1.refs_0_), channel_id=1, source_target_pairs={{0,16},{8,24},{16,0},{24,8},{1,17},{9,25},{17,1},{25,9},{2,18},{10... | collective-permute-start | bytes 98312 | tf_op jit(solution)/shard_map/ppermute | solution.py:524
  30.4 4.8 %collective-permute-start.5 = (bf16[4,2,16,128]{3,2,1,0:T(8,128)(2,1)S(1)}, bf16[4,2,16,128]{3,2,1,0:T(8,128)(2,1)S(1)}, u32[]{:S(2)}, u32[]{:S(2)}) collective-permute-start(bf16[4,2,16,128]{3,2,1,0:T(8,128)(2,1)S(1)} %total.1.refs_0_), channel_id=1, source_target_pairs={{0,8},{8,0},{16,24},{24,16},{1,9},{9,1},{17,25},{25,17},{2,10},{10... | collective-permute-start | bytes 98312 | tf_op jit(solution)/shard_map/ppermute | solution.py:524

commit v4 on v3

--- a/solution.py
+++ b/solution.py
@@ -48,58 +48,130 @@
     return lax.dot_general(left, right, (((1,), (1,)), ((), ())), preferred_element_type=F32)
 
 
-def rim_kernel(tiles, planes, x_hbm, u_hbm, out_ref, x_ref, u_ref, pick_ref, sems):
-    spots = tiles * planes
-    chunk = GROUP * 6 * spots
-    chunks = x_hbm.shape[0] // chunk
+def chunk_copies(x_hbm, x_ref, sems, chunks):
+    chunk = x_hbm.shape[0] // chunks
     copies = []
     for g in range(chunks):
         rows = pl.ds(g * chunk, chunk)
         copies.append(pltpu.make_async_copy(x_hbm.at[rows], x_ref.at[rows], sems.at[g]))
-    copies.append(pltpu.make_async_copy(u_hbm, u_ref, sems.at[chunks]))
-    for copy in copies:
-        copy.start()
-
-    def source(row):
-        return (row & (GROUP - 1)) * spots + (row // GROUP) * planes
-
-    pick_ref[...] = pick_matrix(tiles * GROUP, GROUP * spots, source)
-    chosen = pick_ref[...]
-    for g in range(chunks):
-        copies[g].wait()
-        block = x_ref[g * chunk : (g + 1) * chunk, :].reshape(GROUP, 6, spots, LANES)
-        for part in range(0, 6, 2):
-            rows = jnp.concatenate(
-                [block[:, part + k].reshape(GROUP * spots, LANES) for k in range(2)], axis=1
-            )
-            taken = jnp.dot(chosen, rows, preferred_element_type=F32).astype(BF16)
-            for k in range(2):
-                for tile in range(tiles):
-                    out_ref[(part + k) * tiles + tile, g * GROUP : (g + 1) * GROUP] = taken[
-                        tile * GROUP : (tile + 1) * GROUP, k * LANES : (k + 1) * LANES
-                    ]
-    copies[chunks].wait()
-
-
-def rim_plane(x, u, count, tiles, planes):
+    return copies
+
+
+def chunk_rows(x_ref, at, spots, first):
+    block = x_ref[at * 6 * spots : (at + GROUP) * 6 * spots, :].reshape(GROUP, 6, spots, LANES)
+    return jnp.concatenate([block[:, first + k].reshape(GROUP * spots, LANES) for k in range(2)], axis=1)
+
+
+def rim_kernel(tiles, planes, count, cores, x_hbm, out_ref, x_ref, pick_ref, sems):
+    spots = tiles * planes
+    chunks = count // GROUP
+
+    @pl.when((lax.axis_index("space") & (cores - 1)) == 0)
+    def _():
+        copies = chunk_copies(x_hbm, x_ref, sems, chunks)
+        for copy in copies:
+            copy.start()
+
+        def source(row):
+            return (row & (GROUP - 1)) * spots + (row // GROUP) * planes
+
+        pick_ref[...] = pick_matrix(tiles * GROUP, GROUP * spots, source)
+        chosen = pick_ref[...]
+        for g in range(chunks):
+            copies[g].wait()
+            at = g * GROUP
+            for part in range(0, 6, 2):
+                taken = jnp.dot(chosen, chunk_rows(x_ref, at, spots, part), preferred_element_type=F32)
+                taken = taken.astype(BF16)
+                for k in range(2):
+                    for tile in range(tiles):
+                        out_ref[(part + k) * tiles + tile, at : at + GROUP] = taken[
+                            tile * GROUP : (tile + 1) * GROUP, k * LANES : (k + 1) * LANES
+                        ]
+
+
+def rim_plane(x, count, tiles, planes, cores):
     spots = tiles * planes
     return pl.pallas_call(
-        partial(rim_kernel, tiles, planes),
-        in_specs=[pl.BlockSpec(memory_space=pltpu.HBM)] * 2,
-        out_specs=[vspec()] * 3,
-        out_shape=[
-            jax.ShapeDtypeStruct((6 * tiles, count, LANES), BF16),
-            jax.ShapeDtypeStruct(x.shape, BF16),
-            jax.ShapeDtypeStruct(u.shape, F32),
-        ],
+        partial(rim_kernel, tiles, planes, count, cores),
+        in_specs=[pl.BlockSpec(memory_space=pltpu.HBM)],
+        out_specs=vspec(),
+        out_shape=jax.ShapeDtypeStruct((6 * tiles, count, LANES), BF16),
         scratch_shapes=[
+            VMEM(x.shape, BF16),
             VMEM((tiles * GROUP, GROUP * spots), BF16),
-            pltpu.SemaphoreType.DMA((count // GROUP + 1,)),
+            pltpu.SemaphoreType.DMA((count // GROUP,)),
         ],
         compiler_params=limit(8),
         cost_estimate=cost(10**8, 4 * 10**6),
         name="rim",
-    )(x, u)
+    )(x)
+
+
+def spread_kernel(
+    tiles, planes, count, x_hbm, u_hbm, rim_hbm, v_ref, lhs_ref, out_ref, u_ref, x_ref, pick_ref, sems
+):
+    spots = tiles * planes
+    pair = 2
+    halves = tiles // pair
+    chunks = count // GROUP
+    copies = chunk_copies(x_hbm, x_ref, sems, chunks)
+    copies.append(pltpu.make_async_copy(u_hbm, u_ref, sems.at[chunks]))
+    for copy in copies:
+        copy.start()
+
+    def source(row):
+        spot = row // GROUP
+        return (row & (GROUP - 1)) * spots + (spot % tiles) * planes + spot // tiles
+
+    pick_ref[...] = pick_matrix(GROUP * spots, GROUP * spots, source)
+    chosen = pick_ref[...]
+    for g in range(chunks):
+        copies[g].wait()
+        at = g * GROUP
+        for first in range(0, 6, 2):
+            taken = jnp.dot(chosen, chunk_rows(x_ref, at, spots, first), preferred_element_type=F32)
+            for k in range(2):
+                part = first + k
+                half, colour = part // 3, part % 3
+                for spot in range(spots):
+                    piece = taken[spot * GROUP : (spot + 1) * GROUP, k * LANES : (k + 1) * LANES]
+                    plane, tile = spot // tiles, spot % tiles
+                    column = ((tile % pair) * 3 + colour) * LANES
+                    v_ref[spot * 6 + part, at : at + GROUP, :] = piece
+                    rounded = piece.astype(BF16)
+                    lhs_ref[
+                        plane * halves + tile // pair,
+                        half * count + at : half * count + at + GROUP,
+                        column : column + LANES,
+                    ] = rounded
+                    if plane == 0:
+                        out_ref[part * tiles + tile, at : at + GROUP] = rounded
+    copies[chunks].wait()
+
+
+def spread(x, u, rim, count, tiles, planes):
+    spots = tiles * planes
+    pair = 2
+    return pl.pallas_call(
+        partial(spread_kernel, tiles, planes, count),
+        in_specs=[pl.BlockSpec(memory_space=pltpu.HBM)] * 2 + [pl.BlockSpec(memory_space=pl.ANY)],
+        out_specs=[vspec()] * 4,
+        out_shape=[
+            jax.ShapeDtypeStruct((spots * 6, count, LANES), F32),
+            jax.ShapeDtypeStruct((planes * (tiles // pair), 2 * count, pair * 3 * LANES), BF16),
+            jax.ShapeDtypeStruct((6 * tiles, count, LANES), BF16),
+            jax.ShapeDtypeStruct(u.shape, F32),
+        ],
+        scratch_shapes=[
+            VMEM(x.shape, BF16),
+            VMEM((GROUP * spots, GROUP * spots), BF16),
+            pltpu.SemaphoreType.DMA((count // GROUP + 1,)),
+        ],
+        compiler_params=limit(16),
+        cost_estimate=cost(10**9, 14 * 10**6),
+        name="spread",
+    )(x, u, rim)
 
 
 def link_product(links, vec_re, vec_im):
@@ -166,44 +238,16 @@
 
 def gram_kernel(
     count, tiles, planes, lx, groups, slots, empty,
-    x_ref, u_ref, phase_ref, owner_ref, elem_ref, source_ref, spin_ref,
-    sums_ref, rim_lhs_ref, table_ref,
-    v_ref, lhs_ref, op_ref, acc_ref, g_ref, pick_ref,
+    v_ref, lhs_ref, u_ref, phase_ref, owner_ref, elem_ref, source_ref, spin_ref,
+    sums_ref, table_ref,
+    op_ref, acc_ref, g_ref,
 ):
     spots = tiles * planes
     pair = 2
     halves = tiles // pair
     steps = planes * halves
-
-    def source(row):
-        spot = row // GROUP
-        return (row & (GROUP - 1)) * spots + (spot % tiles) * planes + spot // tiles
-
-    pick_ref[...] = pick_matrix(GROUP * spots, GROUP * spots, source)
     acc_ref[...] = jnp.zeros_like(acc_ref)
     g_ref[...] = jnp.zeros_like(g_ref)
-
-    chosen = pick_ref[...]
-    for at in range(0, count, GROUP):
-        block = x_ref[at * 6 * spots : (at + GROUP) * 6 * spots, :].reshape(GROUP, 6, spots, LANES)
-        for first in range(0, 6, 2):
-            rows = jnp.concatenate(
-                [block[:, first + k].reshape(GROUP * spots, LANES) for k in range(2)], axis=1
-            )
-            taken = jnp.dot(chosen, rows, preferred_element_type=F32)
-            for k in range(2):
-                part = first + k
-                half, colour = part // 3, part % 3
-                for spot in range(spots):
-                    piece = taken[spot * GROUP : (spot + 1) * GROUP, k * LANES : (k + 1) * LANES]
-                    v_ref[spot * 6 + part, at : at + GROUP, :] = piece
-                    plane, tile = spot // tiles, spot % tiles
-                    lhs_ref[
-                        plane * halves + tile // pair,
-                        half * count + at : half * count + at + GROUP,
-                        ((tile % pair) * 3 + colour) * LANES : ((tile % pair) * 3 + colour + 1) * LANES,
-                    ] = piece.astype(BF16)
-
     lane = lax.broadcasted_iota(jnp.int32, (8, LANES), 1)
     wraps = (lane & (LZ - 1)) == LZ - 1
     spills = lane < LZ
@@ -257,6 +301,11 @@
 
     every, side = (0, 1, 2), (1, 2)
     inner = steps - halves
+    elementwise(inner, 0, side)
+    for step in range(inner + 1, steps):
+        multiply(step - 1, (step - 1) & 1, side)
+        elementwise(step, step & 1, side)
+    multiply(steps - 1, (steps - 1) & 1, side)
     elementwise(0, 0, every)
 
     def body(step, carry):
@@ -267,9 +316,6 @@
 
     lax.fori_loop(1, inner, body, 0)
     multiply(inner - 1, (inner - 1) & 1, every)
-    for step in range(inner, steps):
-        elementwise(step, step & 1, side)
-        multiply(step, step & 1, side)
     fill_table(groups, slots, empty, owner_ref, elem_ref, source_ref, spin_ref, table_ref)
 
     first = lax.axis_index("space") * planes
@@ -288,40 +334,32 @@
         real, imag = anti(*paired(grid, count))
         sums_ref[direction + 1, 0] = real
         sums_ref[direction + 1, 1] = imag
-    for half in range(halves):
-        rim_lhs_ref[half] = lhs_ref[(planes - 1) * halves + half]
-
-
-def gram(x, u, phases, tables, count, tiles, planes, lx, groups, slots, empty):
-    spots = tiles * planes
+
+
+def gram(v, lhs, u, phases, tables, count, tiles, planes, lx, groups, slots, empty):
     pair = 2
-    steps = planes * (tiles // pair)
     wide = pair * 3 * LANES
     return pl.pallas_call(
         partial(gram_kernel, count, tiles, planes, lx, groups, slots, empty),
-        in_specs=[vspec()] * 2 + [sspec()] + [vspec()] * 4,
-        out_specs=[vspec()] * 3,
+        in_specs=[vspec()] * 3 + [sspec()] + [vspec()] * 4,
+        out_specs=[vspec()] * 2,
         out_shape=[
             jax.ShapeDtypeStruct((OPS, 2, count, count), F32),
-            jax.ShapeDtypeStruct((tiles // pair, 2 * count, wide), BF16),
             jax.ShapeDtypeStruct((1, LANES), jnp.int32),
         ],
         scratch_shapes=[
-            VMEM((spots * 6, count, LANES), F32),
-            VMEM((steps, 2 * count, wide), BF16),
             VMEM((2, 6 * count, wide), BF16),
             VMEM((6 * count, 2 * count), F32),
             VMEM((planes, 2 * count, 2 * count), F32),
-            VMEM((GROUP * spots, GROUP * spots), BF16),
         ],
-        compiler_params=limit(26),
+        compiler_params=limit(16),
         cost_estimate=cost(8 * 10**9, 5 * 10**6),
         name="gram",
-    )(x, u, phases, *tables)
+    )(v, lhs, u, phases, *tables)
 
 
 def edge_kernel(
-    count, tiles, planes, rows, cores, halo_ref, lhs_ref, u_ref, sums_ref, keep_ref, send_ref, op_ref, tot_ref
+    count, tiles, planes, rows, cores, far_ref, near_ref, lhs_ref, u_ref, sums_ref, keep_ref, send_ref, op_ref, tot_ref
 ):
     spots = tiles * planes
     pair = 2
@@ -331,7 +369,11 @@
             tile = half_tile * pair + sub
             links = load_links(u_ref, 0, tile * planes + planes - 1, spots)
             for at in range(0, count, GROUP):
-                parts = [halo_ref[k * tiles + tile, at : at + GROUP, :].astype(F32) for k in range(6)]
+                parts = [
+                    (far_ref[k * tiles + tile, at : at + GROUP] + near_ref[k * tiles + tile, at : at + GROUP])
+                    .astype(F32)
+                    for k in range(6)
+                ]
                 outs = [
                     link_product(
                         links,
@@ -347,7 +389,7 @@
                         op_ref[
                             half_tile, half * count + at : half * count + at + GROUP, column : column + LANES
                         ] = both.astype(BF16)
-        got = nt_dot(op_ref[half_tile], lhs_ref[half_tile])
+        got = nt_dot(op_ref[half_tile], lhs_ref[(planes - 1) * (tiles // pair) + half_tile])
         total = got if total is None else total + got
     real, imag = anti(*paired(total, count))
     tot_ref[0] = real
@@ -364,12 +406,12 @@
                     ref[chip, op, half] = piece
 
 
-def edge(halo, rim_lhs, u, sums, count, tiles, planes, rows, cores):
+def edge(far, near, lhs, u, sums, count, tiles, planes, rows, cores):
     pair = 2
     shape = jax.ShapeDtypeStruct((count // (rows * cores), OPS, 2, rows, count), F32)
     return pl.pallas_call(
         partial(edge_kernel, count, tiles, planes, rows, cores),
-        in_specs=[vspec()] * 4,
+        in_specs=[vspec()] * 5,
         out_specs=[vspec(), vspec()],
         out_shape=[shape, shape],
         scratch_shapes=[
@@ -379,7 +421,7 @@
         compiler_params=limit(8),
         cost_estimate=cost(10**9, 3 * 10**6),
         name="edge",
-    )(halo, rim_lhs, u, sums)
+    )(far, near, lhs, u, sums)
 
 
 def split_sum(block):
@@ -504,13 +546,16 @@
     empty = per.shape[0] * groups * OPS
     x = pltpu.with_memory_space_constraint(x, pltpu.HBM)
     u = pltpu.with_memory_space_constraint(u, pltpu.HBM)
-    rim, x, u = rim_plane(x, u, count, tiles, planes)
-    halo = lax.ppermute(rim, "space", [(i, (i - 1) % space_size) for i in range(space_size)])
+    down = [(i, (i - 1) % space_size) for i in range(space_size)]
+    rim = rim_plane(x, count, tiles, planes, cores)
+    far = lax.ppermute(rim, "space", [move for move in down if move[0] % cores == 0])
+    v, lhs, rim, u = spread(x, u, rim, count, tiles, planes)
+    near = lax.ppermute(rim, "space", [move for move in down if move[0] % cores != 0])
     tables = [job.reshape(1, -1) for job in (job_owner, job_elemental, job_source, job_spin)]
-    sums, rim_lhs, table = gram(
-        x, u, phases, tables, count, tiles, planes, lx, groups, slots, empty
-    )
-    keep, send = edge(halo, rim_lhs, u, sums, count, tiles, planes, rows, cores)
+    sums, table = gram(
+        v, lhs, u, phases, tables, count, tiles, planes, lx, groups, slots, empty
+    )
+    keep, send = edge(far, near, lhs, u, sums, count, tiles, planes, rows, cores)
     got = lax.ppermute(send, "space", [(i, i ^ 1) for i in range(space_size)])
     parts = fold(keep, got, cores)
     summed = [parts[0]]

time: 37.2 us -> 46.6 us (1.25)
  starting transfers between devices: 11.5 us -> 16 us
  Pallas kernels: 16.4 us -> 19 us
  waiting for transfers between devices: 9.04 us -> 11.2 us
    ppermute x1 -> x2, starting transfers between devices: 3.41 us -> 7.94 us  [the longest x1 6.65 us: fast_shards(): lax.ppermute(rim, 'space', [move for move in down if move[0] % cores == 0])]
    pallas_call x1 -> x2, Pallas kernels: 2.81 us -> 6.17 us  [the longest x1 3.43 us: spread(): pl.pallas_call(partial(spread_kernel, tiles, planes, count), in_specs=[pl...]
    ppermute x3, waiting for transfers between devices: 4.03 us -> 5.49 us  [fast_shards(): lax.ppermute(own, 'tm', [(i, i ^ step) for i in range(groups)])]
    pallas_call x1, Pallas kernels: 10.8 us -> 9.96 us  [gram(): pl.pallas_call(partial(gram_kernel, count, tiles, planes, lx, groups, slo...]
    ppermute x3, waiting for transfers between devices: 3.49 us -> 4.19 us  [fast_shards(): lax.ppermute(parts[step], 'space', [(i, i ^ step * cores) for i in range(...]
  transfers between devices with their start and end apart: 8 -> 9, of which waited for: 6 -> 6; matrix products, arithmetic and copies ran while one was open for 0% -> 0% of each run, Pallas kernels for 29% -> 21%
where the time goes in v4:
time: 46.6 us; the launch traced here: 46.5 us
  Pallas kernels  19 us (41%)
  starting transfers between devices  16 us (34%)
  waiting for transfers between devices  11.2 us (24%)
    pallas_call x1, Pallas kernels, gram(): pl.pallas_call(partial(gram_kernel, count, tiles, planes, lx, groups, slo...  9.96 us
    ppermute x1, starting transfers between devices, fast_shards(): lax.ppermute(rim, 'space', [move for move in down if move[0] % cores == 0])  6.65 us
    ppermute x3, waiting for transfers between devices, fast_shards(): lax.ppermute(own, 'tm', [(i, i ^ step) for i in range(groups)])  5.49 us
    ppermute x3, starting transfers between devices, fast_shards(): lax.ppermute(own, 'tm', [(i, i ^ step) for i in range(groups)])  4.45 us
    ppermute x3, waiting for transfers between devices, fast_shards(): lax.ppermute(parts[step], 'space', [(i, i ^ step * cores) for i in range(...  4.19 us
    ppermute x3, starting transfers between devices, fast_shards(): lax.ppermute(parts[step], 'space', [(i, i ^ step * cores) for i in range(...  3.55 us
    pallas_call x1, Pallas kernels, spread(): pl.pallas_call(partial(spread_kernel, tiles, planes, count), in_specs=[pl...  3.43 us
    pallas_call x1, Pallas kernels, rim_plane(): pl.pallas_call(partial(rim_kernel, tiles, planes, count, cores), in_specs...  2.74 us
  transfers between devices with their start and end apart: 9, of which 6 were waited for; matrix products, arithmetic and copies ran while one was open for 0% of the time, Pallas kernels for 21%

profile of v4, /device:TPU:0, one launch (start us, length us, event | category | flops | bytes accessed | tf_op | source)
XLA Modules:
  0.0 46.5 jit_solution(9753575856843287765)
XLA Ops:
  0.0 2.7 %rim.1.rim_hbm = bf16[24,128,128]{2,1,0:T(8,128)(2,1)S(1)} custom-call(bf16[12288,128]{1,0:T(8,128)(2,1)} %bitcast.21), custom_call_target="tpu_custom_call" | custom-call | flops 100000000 | bytes 4000000 | tf_op jit(solution)/shard_map/rim/pallas_call | solution.py:95
  2.7 0.0 copy-start.1
  2.8 0.0 copy-start.2
  2.8 0.0 copy-start.3
  2.8 0.0 copy-start.4
  2.8 0.0 copy-start.5
  2.8 3.4 %spread.1 = (f32[96,128,128]{2,1,0:T(8,128)S(1)}, bf16[8,256,768]{2,1,0:T(8,128)(2,1)S(1)}, bf16[24,128,128]{2,1,0:T(8,128)(2,1)S(1)}, f32[864,128]{1,0:T(8,128)S(1)}) custom-call(bf16[12288,128]{1,0:T(8,128)(2,1)} %bitcast.22, f32[864,128]{1,0:T(8,128)} %bitcast.23, bf16[24,128,128]{2,1,0:T(8,128)(2,1)S(1)} %rim.1.rim_hbm), custom_call_target="tpu_custom_call" | custom-call | flops 1000000000 | bytes 14000000 | tf_op jit(solution)/shard_map/spread/pallas_call | solution.py:156
  6.2 1.3 %collective-permute-start.1 = (bf16[24,128,128]{2,1,0:T(8,128)(2,1)S(1)}, bf16[24,128,128]{2,1,0:T(8,128)(2,1)S(1)}, u32[]{:S(2)}, u32[]{:S(2)}) collective-permute-start(bf16[24,128,128]{2,1,0:T(8,128)(2,1)S(1)} %get-tuple-element.21), channel_id=1, source_target_pairs={{1,0},{3,2},{5,4},{7,6},{9,8},{11,10},{13,12},{15,14},{17,16},{19,... | collective-permute-start | bytes 2359304 | tf_op jit(solution)/shard_map/ppermute | solution.py:553
  7.5 6.7 %collective-permute-start = (bf16[24,128,128]{2,1,0:T(8,128)(2,1)S(1)}, bf16[24,128,128]{2,1,0:T(8,128)(2,1)S(1)}, u32[]{:S(2)}, u32[]{:S(2)}) collective-permute-start(bf16[24,128,128]{2,1,0:T(8,128)(2,1)S(1)} %rim.1.rim_hbm), channel_id=1, source_target_pairs={{0,7},{2,1},{4,3},{6,5},{8,15},{10,9},{12,11},{14,13},{16,23},{18,... | collective-permute-start | bytes 2359304 | tf_op jit(solution)/shard_map/ppermute | solution.py:551
  14.2 0.0 copy-done.1
  14.2 0.0 copy-done.2
  14.2 0.0 copy-done.3
  14.3 10.0 %gram.1 = (f32[4,2,128,128]{3,2,1,0:T(8,128)S(1)}, s32[1,128]{1,0:T(1,128)S(1)}) custom-call(f32[96,128,128]{2,1,0:T(8,128)S(1)} %get-tuple-element.17.v_ref, bf16[8,256,768]{2,1,0:T(8,128)(2,1)S(1)} %get-tuple-element.18.lhs_ref, f32[864,128]{1,0:T(8,128)S(1)} %get-tuple-element.19.u_ref, f32[64]{0:T(128)S(1)} %copy-done.5, s32[1,96]{1,0:T(1,128)S(1)} %bitcast.17, ...), custom_call_target="tpu_custom_call" | custom-call | flops 8000000000 | bytes 5000000 | tf_op jit(solution)/shard_map/gram/pallas_call | solution.py:342
  24.2 0.0 collective-permute-done.1.near_ref
  24.2 0.0 collective-permute-done.far_ref
  24.2 0.0 copy-start
  24.3 1.0 %edge.1 = (f32[4,4,2,16,128]{4,3,2,1,0:T(8,128)S(1)}, f32[4,4,2,16,128]{4,3,2,1,0:T(8,128)S(1)}) custom-call(bf16[24,128,128]{2,1,0:T(8,128)(2,1)S(1)} %collective-permute-done.far_ref, bf16[24,128,128]{2,1,0:T(8,128)(2,1)S(1)} %collective-permute-done.1.near_ref, bf16[8,256,768]{2,1,0:T(8,128)(2,1)S(1)} %get-tuple-element.18.lhs_ref, ...), custom_call_target="tpu_custom_call" | custom-call | flops 1000000000 | bytes 3000000 | tf_op jit(solution)/shard_map/edge/pallas_call | solution.py:412
  25.2 0.1 collective-permute-start.2
  25.3 1.5 %collective-permute-done.2.got_ref = f32[4,4,2,16,128]{4,3,2,1,0:T(8,128)S(1)} collective-permute-done((f32[4,4,2,16,128]{4,3,2,1,0:T(8,128)S(1)}, f32[4,4,2,16,128]{4,3,2,1,0:T(8,128)S(1)}, u32[]{:S(2)}, u32[]{:S(2)}) %collective-permute-start.2) | collective-permute-done | bytes 262176 | tf_op jit(solution)/shard_map/ppermute | solution.py:559
  26.8 1.3 %collective-permute-start.3 = (bf16[5,2,16,128]{3,2,1,0:T(8,128)(2,1)S(1)}, bf16[5,2,16,128]{3,2,1,0:T(8,128)(2,1)S(1)}, u32[]{:S(2)}, u32[]{:S(2)}) collective-permute-start(bf16[5,2,16,128]{3,2,1,0:T(8,128)(2,1)S(1)} %get-tuple-element.26), channel_id=1, source_target_pairs={{0,2},{1,3},{2,0},{3,1},{4,6},{5,7},{6,4},{7,5},{8,10},{9,11},{10,... | collective-permute-start | bytes 122888 | tf_op jit(solution)/shard_map/ppermute | solution.py:564
  28.2 1.5 %collective-permute-start.4 = (bf16[5,2,16,128]{3,2,1,0:T(8,128)(2,1)S(1)}, bf16[5,2,16,128]{3,2,1,0:T(8,128)(2,1)S(1)}, u32[]{:S(2)}, u32[]{:S(2)}) collective-permute-start(bf16[5,2,16,128]{3,2,1,0:T(8,128)(2,1)S(1)} %get-tuple-element.27), channel_id=1, source_target_pairs={{0,4},{1,5},{2,6},{3,7},{4,0},{5,1},{6,2},{7,3},{8,12},{9,13},{10,... | collective-permute-start | bytes 122888 | tf_op jit(solution)/shard_map/ppermute | solution.py:564
  29.7 0.7 %collective-permute-start.5 = (bf16[5,2,16,128]{3,2,1,0:T(8,128)(2,1)S(1)}, bf16[5,2,16,128]{3,2,1,0:T(8,128)(2,1)S(1)}, u32[]{:S(2)}, u32[]{:S(2)}) collective-permute-start(bf16[5,2,16,128]{3,2,1,0:T(8,128)(2,1)S(1)} %get-tuple-element.28), channel_id=1, source_target_pairs={{0,6},{1,7},{2,4},{3,5},{4,2},{5,3},{6,0},{7,1},{8,14},{9,15},{10,... | collective-permute-start | bytes 122888 | tf_op jit(solution)/shard_map/ppermute | solution.py:564
  30.4 0.5 %collective-permute-done.3.refs_0_ = bf16[5,2,16,128]{3,2,1,0:T(8,128)(2,1)S(1)} collective-permute-done((bf16[5,2,16,128]{3,2,1,0:T(8,128)(2,1)S(1)}, bf16[5,2,16,128]{3,2,1,0:T(8,128)(2,1)S(1)}, u32[]{:S(2)}, u32[]{:S(2)}) %collective-permute-start.3) | collective-permute-done | bytes 40992 | tf_op jit(solution)/shard_map/ppermute | solution.py:564
  30.9 1.3 %collective-permute-done.4.refs_1_ = bf16[5,2,16,128]{3,2,1,0:T(8,128)(2,1)S(1)} collective-permute-done((bf16[5,2,16,128]{3,2,1,0:T(8,128)(2,1)S(1)}, bf16[5,2,16,128]{3,2,1,0:T(8,128)(2,1)S(1)}, u32[]{:S(2)}, u32[]{:S(2)}) %collective-permute-start.4) | collective-permute-done | bytes 40992 | tf_op jit(solution)/shard_map/ppermute | solution.py:564
  32.2 2.4 %collective-permute-done.5.refs_2_ = bf16[5,2,16,128]{3,2,1,0:T(8,128)(2,1)S(1)} collective-permute-done((bf16[5,2,16,128]{3,2,1,0:T(8,128)(2,1)S(1)}, bf16[5,2,16,128]{3,2,1,0:T(8,128)(2,1)S(1)}, u32[]{:S(2)}, u32[]{:S(2)}) %collective-permute-start.5) | collective-permute-done | bytes 40992 | tf_op jit(solution)/shard_map/ppermute | solution.py:564
  34.6 1.6 %collective-permute-start.6 = (bf16[4,2,16,128]{3,2,1,0:T(8,128)(2,1)S(1)}, bf16[4,2,16,128]{3,2,1,0:T(8,128)(2,1)S(1)}, u32[]{:S(2)}, u32[]{:S(2)}) collective-permute-start(bf16[4,2,16,128]{3,2,1,0:T(8,128)(2,1)S(1)} %total.1.refs_0_), channel_id=1, source_target_pairs={{0,8},{8,0},{16,24},{24,16},{1,9},{9,1},{17,25},{25,17},{2,10},{10... | collective-permute-start | bytes 98312 | tf_op jit(solution)/shard_map/ppermute | solution.py:569
  36.3 2.6 %collective-permute-start.7 = (bf16[4,2,16,128]{3,2,1,0:T(8,128)(2,1)S(1)}, bf16[4,2,16,128]{3,2,1,0:T(8,128)(2,1)S(1)}, u32[]{:S(2)}, u32[]{:S(2)}) collective-permute-start(bf16[4,2,16,128]{3,2,1,0:T(8,128)(2,1)S(1)} %total.1.refs_0_), channel_id=1, source_target_pairs={{0,16},{8,24},{16,0},{24,8},{1,17},{9,25},{17,1},{25,9},{2,18},{10... | collective-permute-start | bytes 98312 | tf_op jit(solution)/shard_map/ppermute | solution.py:569
  38.9 0.2 collective-permute-start.8
  39.1 0.0 collective-permute-done.6.refs_1_
  39.1 2.2 %collective-permute-done.7.refs_2_ = bf16[4,2,16,128]{3,2,1,0:T(8,128)(2,1)S(1)} collective-permute-done((bf16[4,2,16,128]{3,2,1,0:T(8,128)(2,1)S(1)}, bf16[4,2,16,128]{3,2,1,0:T(8,128)(2,1)S(1)}, u32[]{:S(2)}, u32[]{:S(2)}) %collective-permute-start.7) | collective-permute-done | bytes 32800 | tf_op jit(solution)/shard_map/ppermute | solution.py:569
  41.3 3.2 %collective-permute-done.8.refs_3_ = bf16[4,2,16,128]{3,2,1,0:T(8,128)(2,1)S(1)} collective-permute-done((bf16[4,2,16,128]{3,2,1,0:T(8,128)(2,1)S(1)}, bf16[4,2,16,128]{3,2,1,0:T(8,128)(2,1)S(1)}, u32[]{:S(2)}, u32[]{:S(2)}) %collective-permute-start.8) | collective-permute-done | bytes 32800 | tf_op jit(solution)/shard_map/ppermute | solution.py:569
  44.6 1.9 %dress.1 = bf16[4,18,2,16,128]{4,3,2,1,0:T(8,128)(2,1)} custom-call(s32[1,128]{1,0:T(1,128)S(1)} %get-tuple-element.20.table_ref, bf16[8,2,128,128]{3,2,1,0:T(8,128)(2,1)S(1)} %bitcast.16, bf16[4,2,16,128]{3,2,1,0:T(8,128)(2,1)S(1)} %total.1.refs_0_, bf16[4,2,16,128]{3,2,1,0:T(8,128)(2,1)S(1)} %collective-permute-done.6.refs_1_, ...), custom_call_target="tpu_custom_call" | custom-call | flops 1000000000 | bytes 2000000 | tf_op jit(solution)/shard_map/dress/pallas_call | solution.py:508
  (5 shorter events, 0.1 us)
Async XLA Ops:
  2.7 11.5 %copy-start.1 = (s32[96,1]{0,1:T(1,128)S(1)}, s32[96,1]{0,1:T(1,128)}, u32[]{:S(2)}) copy-start(s32[96,1]{0,1:T(1,128)} %param.11) | copy-start | bytes 1156
  2.8 11.5 %copy-start.2 = (s32[96]{0:T(128)S(1)}, s32[96]{0:T(128)}, u32[]{:S(2)}) copy-start(s32[96]{0:T(128)} %param.12) | copy-start | bytes 1156
  2.8 11.5 %copy-start.3 = (s32[96]{0:T(128)S(1)}, s32[96]{0:T(128)}, u32[]{:S(2)}) copy-start(s32[96]{0:T(128)} %param.13) | copy-start | bytes 1156
  2.8 11.5 %copy-start.4 = (s32[96]{0:T(128)S(1)}, s32[96]{0:T(128)}, u32[]{:S(2)}) copy-start(s32[96]{0:T(128)} %param.14) | copy-start | bytes 1156
  2.8 11.5 %copy-start.5 = (f32[64]{0:T(128)S(1)}, f32[64]{0:T(128)}, u32[]{:S(2)}) copy-start(f32[64]{0:T(128)} %constant.2.clone.phase_ref) | copy-start | bytes 772
  6.2 18.0 %collective-permute-start.1 = (bf16[24,128,128]{2,1,0:T(8,128)(2,1)S(1)}, bf16[24,128,128]{2,1,0:T(8,128)(2,1)S(1)}, u32[]{:S(2)}, u32[]{:S(2)}) collective-permute-start(bf16[24,128,128]{2,1,0:T(8,128)(2,1)S(1)} %get-tuple-element.21), channel_id=1, source_target_pairs={{1,0},{3,2},{5,4},{7,6},{9,8},{11,10},{13,12},{15,14},{17,16},{19,... | collective-permute-start | bytes 2359304 | tf_op jit(solution)/shard_map/ppermute | solution.py:553
  7.5 16.7 %collective-permute-start = (bf16[24,128,128]{2,1,0:T(8,128)(2,1)S(1)}, bf16[24,128,128]{2,1,0:T(8,128)(2,1)S(1)}, u32[]{:S(2)}, u32[]{:S(2)}) collective-permute-start(bf16[24,128,128]{2,1,0:T(8,128)(2,1)S(1)} %rim.1.rim_hbm), channel_id=1, source_target_pairs={{0,7},{2,1},{4,3},{6,5},{8,15},{10,9},{12,11},{14,13},{16,23},{18,... | collective-permute-start | bytes 2359304 | tf_op jit(solution)/shard_map/ppermute | solution.py:551
  24.2 20.3 %copy-start = (bf16[2,4,2,128,128]{4,3,2,1,0:T(8,128)(2,1)S(1)}, bf16[2,4,2,128,128]{4,3,2,1,0:T(8,128)(2,1)}, u32[]{:S(2)}) copy-start(bf16[2,4,2,128,128]{4,3,2,1,0:T(8,128)(2,1)} %param.10) | copy-start | bytes 1572868
  25.2 1.6 %collective-permute-start.2 = (f32[4,4,2,16,128]{4,3,2,1,0:T(8,128)S(1)}, f32[4,4,2,16,128]{4,3,2,1,0:T(8,128)S(1)}, u32[]{:S(2)}, u32[]{:S(2)}) collective-permute-start(f32[4,4,2,16,128]{4,3,2,1,0:T(8,128)S(1)} %get-tuple-element.24), channel_id=1, source_target_pairs={{0,1},{1,0},{2,3},{3,2},{4,5},{5,4},{6,7},{7,6},{8,9},{9,8},{10,11... | collective-permute-start | bytes 786440 | tf_op jit(solution)/shard_map/ppermute | solution.py:559
  26.8 4.1 %collective-permute-start.3 = (bf16[5,2,16,128]{3,2,1,0:T(8,128)(2,1)S(1)}, bf16[5,2,16,128]{3,2,1,0:T(8,128)(2,1)S(1)}, u32[]{:S(2)}, u32[]{:S(2)}) collective-permute-start(bf16[5,2,16,128]{3,2,1,0:T(8,128)(2,1)S(1)} %get-tuple-element.26), channel_id=1, source_target_pairs={{0,2},{1,3},{2,0},{3,1},{4,6},{5,7},{6,4},{7,5},{8,10},{9,11},{10,... | collective-permute-start | bytes 122888 | tf_op jit(solution)/shard_map/ppermute | solution.py:564
  28.2 4.0 %collective-permute-start.4 = (bf16[5,2,16,128]{3,2,1,0:T(8,128)(2,1)S(1)}, bf16[5,2,16,128]{3,2,1,0:T(8,128)(2,1)S(1)}, u32[]{:S(2)}, u32[]{:S(2)}) collective-permute-start(bf16[5,2,16,128]{3,2,1,0:T(8,128)(2,1)S(1)} %get-tuple-element.27), channel_id=1, source_target_pairs={{0,4},{1,5},{2,6},{3,7},{4,0},{5,1},{6,2},{7,3},{8,12},{9,13},{10,... | collective-permute-start | bytes 122888 | tf_op jit(solution)/shard_map/ppermute | solution.py:564
  29.7 4.9 %collective-permute-start.5 = (bf16[5,2,16,128]{3,2,1,0:T(8,128)(2,1)S(1)}, bf16[5,2,16,128]{3,2,1,0:T(8,128)(2,1)S(1)}, u32[]{:S(2)}, u32[]{:S(2)}) collective-permute-start(bf16[5,2,16,128]{3,2,1,0:T(8,128)(2,1)S(1)} %get-tuple-element.28), channel_id=1, source_target_pairs={{0,6},{1,7},{2,4},{3,5},{4,2},{5,3},{6,0},{7,1},{8,14},{9,15},{10,... | collective-permute-start | bytes 122888 | tf_op jit(solution)/shard_map/ppermute | solution.py:564
  34.6 4.5 %collective-permute-start.6 = (bf16[4,2,16,128]{3,2,1,0:T(8,128)(2,1)S(1)}, bf16[4,2,16,128]{3,2,1,0:T(8,128)(2,1)S(1)}, u32[]{:S(2)}, u32[]{:S(2)}) collective-permute-start(bf16[4,2,16,128]{3,2,1,0:T(8,128)(2,1)S(1)} %total.1.refs_0_), channel_id=1, source_target_pairs={{0,8},{8,0},{16,24},{24,16},{1,9},{9,1},{17,25},{25,17},{2,10},{10... | collective-permute-start | bytes 98312 | tf_op jit(solution)/shard_map/ppermute | solution.py:569
  36.3 5.1 %collective-permute-start.7 = (bf16[4,2,16,128]{3,2,1,0:T(8,128)(2,1)S(1)}, bf16[4,2,16,128]{3,2,1,0:T(8,128)(2,1)S(1)}, u32[]{:S(2)}, u32[]{:S(2)}) collective-permute-start(bf16[4,2,16,128]{3,2,1,0:T(8,128)(2,1)S(1)} %total.1.refs_0_), channel_id=1, source_target_pairs={{0,16},{8,24},{16,0},{24,8},{1,17},{9,25},{17,1},{25,9},{2,18},{10... | collective-permute-start | bytes 98312 | tf_op jit(solution)/shard_map/ppermute | solution.py:569
  38.9 5.7 %collective-permute-start.8 = (bf16[4,2,16,128]{3,2,1,0:T(8,128)(2,1)S(1)}, bf16[4,2,16,128]{3,2,1,0:T(8,128)(2,1)S(1)}, u32[]{:S(2)}, u32[]{:S(2)}) collective-permute-start(bf16[4,2,16,128]{3,2,1,0:T(8,128)(2,1)S(1)} %total.1.refs_0_), channel_id=1, source_target_pairs={{0,24},{8,16},{16,8},{24,0},{1,25},{9,17},{17,9},{25,1},{2,26},{10... | collective-permute-start | bytes 98312 | tf_op jit(solution)/shard_map/ppermute | solution.py:569

commit v5 on v3

--- a/solution.py
+++ b/solution.py
@@ -48,53 +48,75 @@
     return lax.dot_general(left, right, (((1,), (1,)), ((), ())), preferred_element_type=F32)
 
 
-def rim_kernel(tiles, planes, x_hbm, u_hbm, out_ref, x_ref, u_ref, pick_ref, sems):
+def rim_kernel(tiles, planes, x_hbm, u_hbm, out_ref, x_ref, u_ref, pick_ref, link_ref, sems):
     spots = tiles * planes
+    pair = 2
+    count = out_ref.shape[1] // 2
     chunk = GROUP * 6 * spots
-    chunks = x_hbm.shape[0] // chunk
+    chunks = count // GROUP
+    first = 18 * spots
+    head, tail = pl.ds(0, first), pl.ds(first, u_hbm.shape[0] - first)
     copies = []
     for g in range(chunks):
         rows = pl.ds(g * chunk, chunk)
         copies.append(pltpu.make_async_copy(x_hbm.at[rows], x_ref.at[rows], sems.at[g]))
-    copies.append(pltpu.make_async_copy(u_hbm, u_ref, sems.at[chunks]))
-    for copy in copies:
+    link_copy = pltpu.make_async_copy(u_hbm.at[head], u_ref.at[head], sems.at[chunks])
+    rest_copy = pltpu.make_async_copy(u_hbm.at[tail], u_ref.at[tail], sems.at[chunks + 1])
+    for copy in [link_copy] + copies + [rest_copy]:
         copy.start()
 
     def source(row):
-        return (row & (GROUP - 1)) * spots + (row // GROUP) * planes
+        return (row & (GROUP - 1)) * spots + (row // GROUP) * planes + planes - 1
 
     pick_ref[...] = pick_matrix(tiles * GROUP, GROUP * spots, source)
+    link_copy.wait()
+    for tile in range(tiles):
+        flat = adjoint(load_rows(u_ref, 0, tile * planes + planes - 1, spots))
+        for k, link in enumerate(flat):
+            link_ref[tile, k] = link
     chosen = pick_ref[...]
     for g in range(chunks):
         copies[g].wait()
         block = x_ref[g * chunk : (g + 1) * chunk, :].reshape(GROUP, 6, spots, LANES)
+        taken = []
         for part in range(0, 6, 2):
             rows = jnp.concatenate(
                 [block[:, part + k].reshape(GROUP * spots, LANES) for k in range(2)], axis=1
             )
-            taken = jnp.dot(chosen, rows, preferred_element_type=F32).astype(BF16)
-            for k in range(2):
-                for tile in range(tiles):
-                    out_ref[(part + k) * tiles + tile, g * GROUP : (g + 1) * GROUP] = taken[
-                        tile * GROUP : (tile + 1) * GROUP, k * LANES : (k + 1) * LANES
-                    ]
-    copies[chunks].wait()
+            got = jnp.dot(chosen, rows, preferred_element_type=F32)
+            taken += [got[:, :LANES], got[:, LANES:]]
+        for tile in range(tiles):
+            links = [[[link_ref[tile, (p * 3 + r) * 3 + c] for c in range(3)] for r in range(3)] for p in range(3)]
+            outs = []
+            for eight in (0, 8):
+                at = tile * GROUP + eight
+                vec = [part[at : at + 8] for part in taken]
+                outs.append(link_product(links, vec[:3], vec[3:]))
+            for half in range(2):
+                row = half * count + g * GROUP
+                for colour in range(3):
+                    column = ((tile % pair) * 3 + colour) * LANES
+                    both = jnp.concatenate([outs[0][half][colour], outs[1][half][colour]], axis=0)
+                    out_ref[tile // pair, row : row + GROUP, column : column + LANES] = both.astype(BF16)
+    rest_copy.wait()
 
 
 def rim_plane(x, u, count, tiles, planes):
     spots = tiles * planes
+    pair = 2
     return pl.pallas_call(
         partial(rim_kernel, tiles, planes),
         in_specs=[pl.BlockSpec(memory_space=pltpu.HBM)] * 2,
         out_specs=[vspec()] * 3,
         out_shape=[
-            jax.ShapeDtypeStruct((6 * tiles, count, LANES), BF16),
+            jax.ShapeDtypeStruct((tiles // pair, 2 * count, pair * 3 * LANES), BF16),
             jax.ShapeDtypeStruct(x.shape, BF16),
             jax.ShapeDtypeStruct(u.shape, F32),
         ],
         scratch_shapes=[
             VMEM((tiles * GROUP, GROUP * spots), BF16),
-            pltpu.SemaphoreType.DMA((count // GROUP + 1,)),
+            VMEM((tiles, 27, 8, LANES), F32),
+            pltpu.SemaphoreType.DMA((count // GROUP + 2,)),
         ],
         compiler_params=limit(8),
         cost_estimate=cost(10**8, 4 * 10**6),
@@ -115,15 +137,29 @@
     return outs_re, outs_im
 
 
-def load_links(u_ref, direction, spot, spots):
+def load_rows(u_ref, direction, spot, spots):
     def one(part, row, col):
         at = (((direction * 2 + part) * 3 + row) * 3 + col) * spots + spot
         return jnp.broadcast_to(u_ref[pl.ds(at, 1), :], (8, LANES))
 
-    grid = [[[one(part, row, col) for col in range(3)] for row in range(3)] for part in range(2)]
-    less = [[grid[1][row][col] - grid[0][row][col] for col in range(3)] for row in range(3)]
-    more = [[grid[1][row][col] + grid[0][row][col] for col in range(3)] for row in range(3)]
-    return grid[0], less, more
+    return [[[one(part, row, col) for col in range(3)] for row in range(3)] for part in range(2)]
+
+
+def load_links(u_ref, direction, spot, spots):
+    real, imag = load_rows(u_ref, direction, spot, spots)
+    less = [[imag[row][col] - real[row][col] for col in range(3)] for row in range(3)]
+    more = [[imag[row][col] + real[row][col] for col in range(3)] for row in range(3)]
+    return real, less, more
+
+
+def adjoint(grid):
+    real, imag = grid
+    order = [(row, col) for row in range(3) for col in range(3)]
+    return (
+        [real[col][row] for row, col in order]
+        + [-imag[col][row] - real[col][row] for row, col in order]
+        + [real[col][row] - imag[col][row] for row, col in order]
+    )
 
 
 def fill_table(groups, slots, empty, owner_ref, elem_ref, source_ref, spin_ref, table_ref):
@@ -257,6 +293,11 @@
 
     every, side = (0, 1, 2), (1, 2)
     inner = steps - halves
+    elementwise(inner, 0, side)
+    for step in range(inner + 1, steps):
+        multiply(step - 1, (step - 1) & 1, side)
+        elementwise(step, step & 1, side)
+    multiply(steps - 1, (steps - 1) & 1, side)
     elementwise(0, 0, every)
 
     def body(step, carry):
@@ -267,9 +308,6 @@
 
     lax.fori_loop(1, inner, body, 0)
     multiply(inner - 1, (inner - 1) & 1, every)
-    for step in range(inner, steps):
-        elementwise(step, step & 1, side)
-        multiply(step, step & 1, side)
     fill_table(groups, slots, empty, owner_ref, elem_ref, source_ref, spin_ref, table_ref)
 
     first = lax.axis_index("space") * planes
@@ -289,7 +327,7 @@
         sums_ref[direction + 1, 0] = real
         sums_ref[direction + 1, 1] = imag
     for half in range(halves):
-        rim_lhs_ref[half] = lhs_ref[(planes - 1) * halves + half]
+        rim_lhs_ref[half] = lhs_ref[half]
 
 
 def gram(x, u, phases, tables, count, tiles, planes, lx, groups, slots, empty):
@@ -320,38 +358,15 @@
     )(x, u, phases, *tables)
 
 
-def edge_kernel(
-    count, tiles, planes, rows, cores, halo_ref, lhs_ref, u_ref, sums_ref, keep_ref, send_ref, op_ref, tot_ref
-):
-    spots = tiles * planes
-    pair = 2
+def edge_kernel(count, rows, cores, halo_ref, lhs_ref, sums_ref, keep_ref, send_ref, tot_ref):
     total = None
-    for half_tile in range(tiles // pair):
-        for sub in range(pair):
-            tile = half_tile * pair + sub
-            links = load_links(u_ref, 0, tile * planes + planes - 1, spots)
-            for at in range(0, count, GROUP):
-                parts = [halo_ref[k * tiles + tile, at : at + GROUP, :].astype(F32) for k in range(6)]
-                outs = [
-                    link_product(
-                        links,
-                        [part[eight : eight + 8] for part in parts[:3]],
-                        [part[eight : eight + 8] for part in parts[3:]],
-                    )
-                    for eight in (0, 8)
-                ]
-                for half in range(2):
-                    for colour in range(3):
-                        column = (sub * 3 + colour) * LANES
-                        both = jnp.concatenate([outs[0][half][colour], outs[1][half][colour]], axis=0)
-                        op_ref[
-                            half_tile, half * count + at : half * count + at + GROUP, column : column + LANES
-                        ] = both.astype(BF16)
-        got = nt_dot(op_ref[half_tile], lhs_ref[half_tile])
+    for half in range(halo_ref.shape[0]):
+        got = nt_dot(halo_ref[half], lhs_ref[half])
         total = got if total is None else total + got
-    real, imag = anti(*paired(total, count))
-    tot_ref[0] = real
-    tot_ref[1] = imag
+    real = total[:count, :count] + total[count:, count:]
+    imag = total[:count, count:] - total[count:, :count]
+    tot_ref[0] = 0.5 * (real - real.T)
+    tot_ref[1] = 0.5 * (imag + imag.T)
     mine = lax.axis_index("space") & (cores - 1)
     for chip in range(count // (rows * cores)):
         for which, ref in ((mine, keep_ref), (1 - mine, send_ref)):
@@ -364,22 +379,18 @@
                     ref[chip, op, half] = piece
 
 
-def edge(halo, rim_lhs, u, sums, count, tiles, planes, rows, cores):
-    pair = 2
+def edge(halo, rim_lhs, sums, count, rows, cores):
     shape = jax.ShapeDtypeStruct((count // (rows * cores), OPS, 2, rows, count), F32)
     return pl.pallas_call(
-        partial(edge_kernel, count, tiles, planes, rows, cores),
-        in_specs=[vspec()] * 4,
+        partial(edge_kernel, count, rows, cores),
+        in_specs=[vspec()] * 3,
         out_specs=[vspec(), vspec()],
         out_shape=[shape, shape],
-        scratch_shapes=[
-            VMEM((tiles // pair, 2 * count, pair * 3 * LANES), BF16),
-            VMEM((2, count, count), F32),
-        ],
+        scratch_shapes=[VMEM((2, count, count), F32)],
         compiler_params=limit(8),
         cost_estimate=cost(10**9, 3 * 10**6),
         name="edge",
-    )(halo, rim_lhs, u, sums)
+    )(halo, rim_lhs, sums)
 
 
 def split_sum(block):
@@ -505,12 +516,12 @@
     x = pltpu.with_memory_space_constraint(x, pltpu.HBM)
     u = pltpu.with_memory_space_constraint(u, pltpu.HBM)
     rim, x, u = rim_plane(x, u, count, tiles, planes)
-    halo = lax.ppermute(rim, "space", [(i, (i - 1) % space_size) for i in range(space_size)])
+    halo = lax.ppermute(rim, "space", [(i, (i + 1) % space_size) for i in range(space_size)])
     tables = [job.reshape(1, -1) for job in (job_owner, job_elemental, job_source, job_spin)]
     sums, rim_lhs, table = gram(
         x, u, phases, tables, count, tiles, planes, lx, groups, slots, empty
     )
-    keep, send = edge(halo, rim_lhs, u, sums, count, tiles, planes, rows, cores)
+    keep, send = edge(halo, rim_lhs, sums, count, rows, cores)
     got = lax.ppermute(send, "space", [(i, i ^ 1) for i in range(space_size)])
     parts = fold(keep, got, cores)
     summed = [parts[0]]

time: 37.2 us -> 36.7 us (0.987)
  starting transfers between devices: 11.5 us -> 9.7 us
  waiting for transfers between devices: 9.04 us -> 10.3 us
    ppermute x1, starting transfers between devices: 3.41 us -> 0.55 us  [fast_shards(): lax.ppermute(rim, 'space', [(i, (i + 1) % space_size) for i in range(spac...]
    ppermute x1, waiting for transfers between devices: 0.01 us -> 1.52 us  [fast_shards(): lax.ppermute(rim, 'space', [(i, (i + 1) % space_size) for i in range(spac...]
    ppermute x1, starting transfers between devices: 0.07 us -> 1.15 us  [fast_shards(): got = lax.ppermute(send, 'space', [(i, i ^ 1) for i in range(space_size)])]
    pallas_call x1, Pallas kernels: 0.91 us -> 0.49 us  [edge(): pl.pallas_call(partial(edge_kernel, count, rows, cores), in_specs=[vspec(...]
  transfers between devices with their start and end apart: 8 -> 8, of which waited for: 6 -> 7; matrix products, arithmetic and copies ran while one was open for 0% -> 0% of each run, Pallas kernels for 29% -> 30%
where the time goes in v5:
time: 36.7 us; the launch traced here: 36.6 us
  Pallas kernels  16.5 us (45%)
  waiting for transfers between devices  10.3 us (28%)
  starting transfers between devices  9.7 us (26%)
    pallas_call x1, Pallas kernels, gram(): pl.pallas_call(partial(gram_kernel, count, tiles, planes, lx, groups, slo...  11 us
    ppermute x3, starting transfers between devices, fast_shards(): lax.ppermute(own, 'tm', [(i, i ^ step) for i in range(groups)])  4.45 us
    ppermute x3, waiting for transfers between devices, fast_shards(): lax.ppermute(own, 'tm', [(i, i ^ step) for i in range(groups)])  4.03 us
    ppermute x3, waiting for transfers between devices, fast_shards(): lax.ppermute(parts[step], 'space', [(i, i ^ step * cores) for i in range(...  3.56 us
    ppermute x3, starting transfers between devices, fast_shards(): lax.ppermute(parts[step], 'space', [(i, i ^ step * cores) for i in range(...  3.55 us
    pallas_call x1, Pallas kernels, rim_plane(): pl.pallas_call(partial(rim_kernel, tiles, planes), in_specs=[pl.BlockSpec...  3.11 us
    pallas_call x1, Pallas kernels, dress(): pl.pallas_call(partial(dress_kernel, groups, slots, taus, rows, count), i...  1.9 us
    ppermute x1, waiting for transfers between devices, fast_shards(): lax.ppermute(rim, 'space', [(i, (i + 1) % space_size) for i in range(spac...  1.52 us
  transfers between devices with their start and end apart: 8, of which 7 were waited for; matrix products, arithmetic and copies ran while one was open for 0% of the time, Pallas kernels for 30%

profile of v5, /device:TPU:0, one launch (start us, length us, event | category | flops | bytes accessed | tf_op | source)
XLA Modules:
  0.0 36.6 jit_solution(18325754862393297709)
XLA Ops:
  0.0 0.0 copy-start.5
  0.0 0.0 copy-start.4
  0.0 0.0 copy-start.3
  0.0 0.0 copy-start.2
  0.0 0.0 copy-start.1
  0.0 3.1 %rim.1 = (bf16[2,256,768]{2,1,0:T(8,128)(2,1)S(1)}, bf16[12288,128]{1,0:T(8,128)(2,1)S(1)}, f32[864,128]{1,0:T(8,128)S(1)}) custom-call(bf16[12288,128]{1,0:T(8,128)(2,1)} %bitcast.21, f32[864,128]{1,0:T(8,128)} %bitcast.22), custom_call_target="tpu_custom_call" | custom-call | flops 100000000 | bytes 4000000 | tf_op jit(solution)/shard_map/rim/pallas_call | solution.py:107
  3.1 0.5 %collective-permute-start = (bf16[2,256,768]{2,1,0:T(8,128)(2,1)S(1)}, bf16[2,256,768]{2,1,0:T(8,128)(2,1)S(1)}, u32[]{:S(2)}, u32[]{:S(2)}) collective-permute-start(bf16[2,256,768]{2,1,0:T(8,128)(2,1)S(1)} %get-tuple-element.20), channel_id=1, source_target_pairs={{0,1},{1,2},{2,3},{3,4},{4,5},{5,6},{6,7},{7,0},{8,9},{9,10},{10,1... | collective-permute-start | bytes 2359304 | tf_op jit(solution)/shard_map/ppermute | solution.py:519
  3.7 0.0 copy-done.5
  3.7 0.0 copy-done.4
  3.7 0.0 copy-done.3
  3.7 0.0 copy-done.2
  3.7 0.0 copy-done.1
  3.7 11.0 %gram.1 = (f32[4,2,128,128]{3,2,1,0:T(8,128)S(1)}, bf16[2,256,768]{2,1,0:T(8,128)(2,1)S(1)}, s32[1,128]{1,0:T(1,128)S(1)}) custom-call(bf16[12288,128]{1,0:T(8,128)(2,1)S(1)} %get-tuple-element.17.x_ref, f32[864,128]{1,0:T(8,128)S(1)} %get-tuple-element.18.u_ref, f32[64]{0:T(128)S(1)} %copy-done.5, s32[1,96]{1,0:T(1,128)S(1)} %bitcast.17, ...), custom_call_target="tpu_custom_call" | custom-call | flops 8000000000 | bytes 5000000 | tf_op jit(solution)/shard_map/gram/pallas_call | solution.py:338
  14.7 0.0 copy-start
  14.7 1.5 %collective-permute-done.halo_ref = bf16[2,256,768]{2,1,0:T(8,128)(2,1)S(1)} collective-permute-done((bf16[2,256,768]{2,1,0:T(8,128)(2,1)S(1)}, bf16[2,256,768]{2,1,0:T(8,128)(2,1)S(1)}, u32[]{:S(2)}, u32[]{:S(2)}) %collective-permute-start) | collective-permute-done | bytes 786464 | tf_op jit(solution)/shard_map/ppermute | solution.py:519
  16.2 0.5 %edge.1 = (f32[4,4,2,16,128]{4,3,2,1,0:T(8,128)S(1)}, f32[4,4,2,16,128]{4,3,2,1,0:T(8,128)S(1)}) custom-call(bf16[2,256,768]{2,1,0:T(8,128)(2,1)S(1)} %collective-permute-done.halo_ref, bf16[2,256,768]{2,1,0:T(8,128)(2,1)S(1)} %get-tuple-element.21.lhs_ref, f32[4,2,128,128]{3,2,1,0:T(8,128)S(1)} %get-tuple-element.22.sums_ref), custom_call_target="tpu_custom_call" | custom-call | flops 1000000000 | bytes 3000000 | tf_op jit(solution)/shard_map/edge/pallas_call | solution.py:384
  16.7 1.2 %collective-permute-start.1 = (f32[4,4,2,16,128]{4,3,2,1,0:T(8,128)S(1)}, f32[4,4,2,16,128]{4,3,2,1,0:T(8,128)S(1)}, u32[]{:S(2)}, u32[]{:S(2)}) collective-permute-start(f32[4,4,2,16,128]{4,3,2,1,0:T(8,128)S(1)} %get-tuple-element.24), channel_id=1, source_target_pairs={{0,1},{1,0},{2,3},{3,2},{4,5},{5,4},{6,7},{7,6},{8,9},{9,8},{10,11... | collective-permute-start | bytes 786440 | tf_op jit(solution)/shard_map/ppermute | solution.py:525
  17.9 1.2 %collective-permute-done.1.got_ref = f32[4,4,2,16,128]{4,3,2,1,0:T(8,128)S(1)} collective-permute-done((f32[4,4,2,16,128]{4,3,2,1,0:T(8,128)S(1)}, f32[4,4,2,16,128]{4,3,2,1,0:T(8,128)S(1)}, u32[]{:S(2)}, u32[]{:S(2)}) %collective-permute-start.1) | collective-permute-done | bytes 262176 | tf_op jit(solution)/shard_map/ppermute | solution.py:525
  19.1 1.6 %collective-permute-start.2 = (bf16[5,2,16,128]{3,2,1,0:T(8,128)(2,1)S(1)}, bf16[5,2,16,128]{3,2,1,0:T(8,128)(2,1)S(1)}, u32[]{:S(2)}, u32[]{:S(2)}) collective-permute-start(bf16[5,2,16,128]{3,2,1,0:T(8,128)(2,1)S(1)} %get-tuple-element.26), channel_id=1, source_target_pairs={{0,2},{1,3},{2,0},{3,1},{4,6},{5,7},{6,4},{7,5},{8,10},{9,11},{10,... | collective-permute-start | bytes 122888 | tf_op jit(solution)/shard_map/ppermute | solution.py:530
  20.6 0.7 %collective-permute-start.3 = (bf16[5,2,16,128]{3,2,1,0:T(8,128)(2,1)S(1)}, bf16[5,2,16,128]{3,2,1,0:T(8,128)(2,1)S(1)}, u32[]{:S(2)}, u32[]{:S(2)}) collective-permute-start(bf16[5,2,16,128]{3,2,1,0:T(8,128)(2,1)S(1)} %get-tuple-element.27), channel_id=1, source_target_pairs={{0,4},{1,5},{2,6},{3,7},{4,0},{5,1},{6,2},{7,3},{8,12},{9,13},{10,... | collective-permute-start | bytes 122888 | tf_op jit(solution)/shard_map/ppermute | solution.py:530
  21.3 1.3 %collective-permute-start.4 = (bf16[5,2,16,128]{3,2,1,0:T(8,128)(2,1)S(1)}, bf16[5,2,16,128]{3,2,1,0:T(8,128)(2,1)S(1)}, u32[]{:S(2)}, u32[]{:S(2)}) collective-permute-start(bf16[5,2,16,128]{3,2,1,0:T(8,128)(2,1)S(1)} %get-tuple-element.28), channel_id=1, source_target_pairs={{0,6},{1,7},{2,4},{3,5},{4,2},{5,3},{6,0},{7,1},{8,14},{9,15},{10,... | collective-permute-start | bytes 122888 | tf_op jit(solution)/shard_map/ppermute | solution.py:530
  22.6 0.5 %collective-permute-done.2.refs_0_ = bf16[5,2,16,128]{3,2,1,0:T(8,128)(2,1)S(1)} collective-permute-done((bf16[5,2,16,128]{3,2,1,0:T(8,128)(2,1)S(1)}, bf16[5,2,16,128]{3,2,1,0:T(8,128)(2,1)S(1)}, u32[]{:S(2)}, u32[]{:S(2)}) %collective-permute-start.2) | collective-permute-done | bytes 40992 | tf_op jit(solution)/shard_map/ppermute | solution.py:530
  23.1 1.9 %collective-permute-done.3.refs_1_ = bf16[5,2,16,128]{3,2,1,0:T(8,128)(2,1)S(1)} collective-permute-done((bf16[5,2,16,128]{3,2,1,0:T(8,128)(2,1)S(1)}, bf16[5,2,16,128]{3,2,1,0:T(8,128)(2,1)S(1)}, u32[]{:S(2)}, u32[]{:S(2)}) %collective-permute-start.3) | collective-permute-done | bytes 40992 | tf_op jit(solution)/shard_map/ppermute | solution.py:530
  25.1 1.1 %collective-permute-done.4.refs_2_ = bf16[5,2,16,128]{3,2,1,0:T(8,128)(2,1)S(1)} collective-permute-done((bf16[5,2,16,128]{3,2,1,0:T(8,128)(2,1)S(1)}, bf16[5,2,16,128]{3,2,1,0:T(8,128)(2,1)S(1)}, u32[]{:S(2)}, u32[]{:S(2)}) %collective-permute-start.4) | collective-permute-done | bytes 40992 | tf_op jit(solution)/shard_map/ppermute | solution.py:530
  26.2 3.7 %collective-permute-start.7 = (bf16[4,2,16,128]{3,2,1,0:T(8,128)(2,1)S(1)}, bf16[4,2,16,128]{3,2,1,0:T(8,128)(2,1)S(1)}, u32[]{:S(2)}, u32[]{:S(2)}) collective-permute-start(bf16[4,2,16,128]{3,2,1,0:T(8,128)(2,1)S(1)} %total.1.refs_0_), channel_id=1, source_target_pairs={{0,24},{8,16},{16,8},{24,0},{1,25},{9,17},{17,9},{25,1},{2,26},{10... | collective-permute-start | bytes 98312 | tf_op jit(solution)/shard_map/ppermute | solution.py:535
  29.9 0.0 collective-permute-start.6
  29.9 0.8 %collective-permute-start.5 = (bf16[4,2,16,128]{3,2,1,0:T(8,128)(2,1)S(1)}, bf16[4,2,16,128]{3,2,1,0:T(8,128)(2,1)S(1)}, u32[]{:S(2)}, u32[]{:S(2)}) collective-permute-start(bf16[4,2,16,128]{3,2,1,0:T(8,128)(2,1)S(1)} %total.1.refs_0_), channel_id=1, source_target_pairs={{0,8},{8,0},{16,24},{24,16},{1,9},{9,1},{17,25},{25,17},{2,10},{10... | collective-permute-start | bytes 98312 | tf_op jit(solution)/shard_map/ppermute | solution.py:535
  30.7 1.4 %collective-permute-done.7.refs_3_ = bf16[4,2,16,128]{3,2,1,0:T(8,128)(2,1)S(1)} collective-permute-done((bf16[4,2,16,128]{3,2,1,0:T(8,128)(2,1)S(1)}, bf16[4,2,16,128]{3,2,1,0:T(8,128)(2,1)S(1)}, u32[]{:S(2)}, u32[]{:S(2)}) %collective-permute-start.7) | collective-permute-done | bytes 32800 | tf_op jit(solution)/shard_map/ppermute | solution.py:535
  32.0 2.7 %collective-permute-done.6.refs_2_ = bf16[4,2,16,128]{3,2,1,0:T(8,128)(2,1)S(1)} collective-permute-done((bf16[4,2,16,128]{3,2,1,0:T(8,128)(2,1)S(1)}, bf16[4,2,16,128]{3,2,1,0:T(8,128)(2,1)S(1)}, u32[]{:S(2)}, u32[]{:S(2)}) %collective-permute-start.6) | collective-permute-done | bytes 32800 | tf_op jit(solution)/shard_map/ppermute | solution.py:535
  34.7 0.0 collective-permute-done.5.refs_1_
  34.7 0.0 copy-done
  34.7 1.9 %dress.1 = bf16[4,18,2,16,128]{4,3,2,1,0:T(8,128)(2,1)} custom-call(s32[1,128]{1,0:T(1,128)S(1)} %get-tuple-element.19.table_ref, bf16[8,2,128,128]{3,2,1,0:T(8,128)(2,1)S(1)} %bitcast.16, bf16[4,2,16,128]{3,2,1,0:T(8,128)(2,1)S(1)} %total.1.refs_0_, bf16[4,2,16,128]{3,2,1,0:T(8,128)(2,1)S(1)} %collective-permute-done.5.refs_1_, ...), custom_call_target="tpu_custom_call" | custom-call | flops 1000000000 | bytes 2000000 | tf_op jit(solution)/shard_map/dress/pallas_call | solution.py:477
  (2 shorter events, 0.0 us)
Async XLA Ops:
  0.0 3.7 %copy-start.5 = (f32[64]{0:T(128)S(1)}, f32[64]{0:T(128)}, u32[]{:S(2)}) copy-start(f32[64]{0:T(128)} %constant.2.clone.phase_ref) | copy-start | bytes 772
  0.0 3.7 %copy-start.4 = (s32[96]{0:T(128)S(1)}, s32[96]{0:T(128)}, u32[]{:S(2)}) copy-start(s32[96]{0:T(128)} %param.14) | copy-start | bytes 1156
  0.0 3.7 %copy-start.3 = (s32[96]{0:T(128)S(1)}, s32[96]{0:T(128)}, u32[]{:S(2)}) copy-start(s32[96]{0:T(128)} %param.13) | copy-start | bytes 1156
  0.0 3.7 %copy-start.2 = (s32[96]{0:T(128)S(1)}, s32[96]{0:T(128)}, u32[]{:S(2)}) copy-start(s32[96]{0:T(128)} %param.12) | copy-start | bytes 1156
  0.0 3.7 %copy-start.1 = (s32[96,1]{0,1:T(1,128)S(1)}, s32[96,1]{0,1:T(1,128)}, u32[]{:S(2)}) copy-start(s32[96,1]{0,1:T(1,128)} %param.11) | copy-start | bytes 1156
  3.1 13.1 %collective-permute-start = (bf16[2,256,768]{2,1,0:T(8,128)(2,1)S(1)}, bf16[2,256,768]{2,1,0:T(8,128)(2,1)S(1)}, u32[]{:S(2)}, u32[]{:S(2)}) collective-permute-start(bf16[2,256,768]{2,1,0:T(8,128)(2,1)S(1)} %get-tuple-element.20), channel_id=1, source_target_pairs={{0,1},{1,2},{2,3},{3,4},{4,5},{5,6},{6,7},{7,0},{8,9},{9,10},{10,1... | collective-permute-start | bytes 2359304 | tf_op jit(solution)/shard_map/ppermute | solution.py:519
  14.7 20.0 %copy-start = (bf16[2,4,2,128,128]{4,3,2,1,0:T(8,128)(2,1)S(1)}, bf16[2,4,2,128,128]{4,3,2,1,0:T(8,128)(2,1)}, u32[]{:S(2)}) copy-start(bf16[2,4,2,128,128]{4,3,2,1,0:T(8,128)(2,1)} %param.10) | copy-start | bytes 1572868
  16.7 2.3 %collective-permute-start.1 = (f32[4,4,2,16,128]{4,3,2,1,0:T(8,128)S(1)}, f32[4,4,2,16,128]{4,3,2,1,0:T(8,128)S(1)}, u32[]{:S(2)}, u32[]{:S(2)}) collective-permute-start(f32[4,4,2,16,128]{4,3,2,1,0:T(8,128)S(1)} %get-tuple-element.24), channel_id=1, source_target_pairs={{0,1},{1,0},{2,3},{3,2},{4,5},{5,4},{6,7},{7,6},{8,9},{9,8},{10,11... | collective-permute-start | bytes 786440 | tf_op jit(solution)/shard_map/ppermute | solution.py:525
  19.1 4.1 %collective-permute-start.2 = (bf16[5,2,16,128]{3,2,1,0:T(8,128)(2,1)S(1)}, bf16[5,2,16,128]{3,2,1,0:T(8,128)(2,1)S(1)}, u32[]{:S(2)}, u32[]{:S(2)}) collective-permute-start(bf16[5,2,16,128]{3,2,1,0:T(8,128)(2,1)S(1)} %get-tuple-element.26), channel_id=1, source_target_pairs={{0,2},{1,3},{2,0},{3,1},{4,6},{5,7},{6,4},{7,5},{8,10},{9,11},{10,... | collective-permute-start | bytes 122888 | tf_op jit(solution)/shard_map/ppermute | solution.py:530
  20.6 4.4 %collective-permute-start.3 = (bf16[5,2,16,128]{3,2,1,0:T(8,128)(2,1)S(1)}, bf16[5,2,16,128]{3,2,1,0:T(8,128)(2,1)S(1)}, u32[]{:S(2)}, u32[]{:S(2)}) collective-permute-start(bf16[5,2,16,128]{3,2,1,0:T(8,128)(2,1)S(1)} %get-tuple-element.27), channel_id=1, source_target_pairs={{0,4},{1,5},{2,6},{3,7},{4,0},{5,1},{6,2},{7,3},{8,12},{9,13},{10,... | collective-permute-start | bytes 122888 | tf_op jit(solution)/shard_map/ppermute | solution.py:530
  21.3 4.9 %collective-permute-start.4 = (bf16[5,2,16,128]{3,2,1,0:T(8,128)(2,1)S(1)}, bf16[5,2,16,128]{3,2,1,0:T(8,128)(2,1)S(1)}, u32[]{:S(2)}, u32[]{:S(2)}) collective-permute-start(bf16[5,2,16,128]{3,2,1,0:T(8,128)(2,1)S(1)} %get-tuple-element.28), channel_id=1, source_target_pairs={{0,6},{1,7},{2,4},{3,5},{4,2},{5,3},{6,0},{7,1},{8,14},{9,15},{10,... | collective-permute-start | bytes 122888 | tf_op jit(solution)/shard_map/ppermute | solution.py:530
  26.2 5.8 %collective-permute-start.7 = (bf16[4,2,16,128]{3,2,1,0:T(8,128)(2,1)S(1)}, bf16[4,2,16,128]{3,2,1,0:T(8,128)(2,1)S(1)}, u32[]{:S(2)}, u32[]{:S(2)}) collective-permute-start(bf16[4,2,16,128]{3,2,1,0:T(8,128)(2,1)S(1)} %total.1.refs_0_), channel_id=1, source_target_pairs={{0,24},{8,16},{16,8},{24,0},{1,25},{9,17},{17,9},{25,1},{2,26},{10... | collective-permute-start | bytes 98312 | tf_op jit(solution)/shard_map/ppermute | solution.py:535
  29.9 4.8 %collective-permute-start.6 = (bf16[4,2,16,128]{3,2,1,0:T(8,128)(2,1)S(1)}, bf16[4,2,16,128]{3,2,1,0:T(8,128)(2,1)S(1)}, u32[]{:S(2)}, u32[]{:S(2)}) collective-permute-start(bf16[4,2,16,128]{3,2,1,0:T(8,128)(2,1)S(1)} %total.1.refs_0_), channel_id=1, source_target_pairs={{0,16},{8,24},{16,0},{24,8},{1,17},{9,25},{17,1},{25,9},{2,18},{10... | collective-permute-start | bytes 98312 | tf_op jit(solution)/shard_map/ppermute | solution.py:535
  29.9 4.8 %collective-permute-start.5 = (bf16[4,2,16,128]{3,2,1,0:T(8,128)(2,1)S(1)}, bf16[4,2,16,128]{3,2,1,0:T(8,128)(2,1)S(1)}, u32[]{:S(2)}, u32[]{:S(2)}) collective-permute-start(bf16[4,2,16,128]{3,2,1,0:T(8,128)(2,1)S(1)} %total.1.refs_0_), channel_id=1, source_target_pairs={{0,8},{8,0},{16,24},{24,16},{1,9},{9,1},{17,25},{25,17},{2,10},{10... | collective-permute-start | bytes 98312 | tf_op jit(solution)/shard_map/ppermute | solution.py:535

commit v6 on v5

--- a/solution.py
+++ b/solution.py
@@ -16,6 +16,7 @@
 JOB_DEV = 24
 LANES = 128
 GROUP = 16
+NARROW = (1, 2)
 F32 = jnp.float32
 BF16 = jnp.bfloat16
 VMEM = pltpu.VMEM
@@ -44,6 +45,10 @@
     return jnp.where(col == source_of(row), 1.0, 0.0).astype(BF16)
 
 
+def joined(pieces):
+    return jnp.concatenate(pieces, axis=1)
+
+
 def nt_dot(left, right):
     return lax.dot_general(left, right, (((1,), (1,)), ((), ())), preferred_element_type=F32)
 
@@ -51,7 +56,7 @@
 def rim_kernel(tiles, planes, x_hbm, u_hbm, out_ref, x_ref, u_ref, pick_ref, link_ref, sems):
     spots = tiles * planes
     pair = 2
-    count = out_ref.shape[1] // 2
+    count = out_ref.shape[2] // 2
     chunk = GROUP * 6 * spots
     chunks = count // GROUP
     first = 18 * spots
@@ -95,9 +100,8 @@
             for half in range(2):
                 row = half * count + g * GROUP
                 for colour in range(3):
-                    column = ((tile % pair) * 3 + colour) * LANES
                     both = jnp.concatenate([outs[0][half][colour], outs[1][half][colour]], axis=0)
-                    out_ref[tile // pair, row : row + GROUP, column : column + LANES] = both.astype(BF16)
+                    out_ref[tile // pair, (tile % pair) * 3 + colour, row : row + GROUP] = both.astype(BF16)
     rest_copy.wait()
 
 
@@ -109,7 +113,7 @@
         in_specs=[pl.BlockSpec(memory_space=pltpu.HBM)] * 2,
         out_specs=[vspec()] * 3,
         out_shape=[
-            jax.ShapeDtypeStruct((tiles // pair, 2 * count, pair * 3 * LANES), BF16),
+            jax.ShapeDtypeStruct((tiles // pair, 3 * pair, 2 * count, LANES), BF16),
             jax.ShapeDtypeStruct(x.shape, BF16),
             jax.ShapeDtypeStruct(u.shape, F32),
         ],
@@ -137,6 +141,25 @@
     return outs_re, outs_im
 
 
+def narrow_product(links, vec_re, vec_im):
+    real, imag = links
+    outs_re, outs_im = [], []
+    for row in range(3):
+        ones = [real[row][c] * vec_re[c] - imag[row][c] * vec_im[c] for c in range(3)]
+        twos = [real[row][c] * vec_im[c] + imag[row][c] * vec_re[c] for c in range(3)]
+        outs_re.append(ones[0] + ones[1] + ones[2])
+        outs_im.append(twos[0] + twos[1] + twos[2])
+    return outs_re, outs_im
+
+
+def narrow_links(u_ref, direction, spot, spots):
+    def one(part, row, col):
+        at = (((direction * 2 + part) * 3 + row) * 3 + col) * spots + spot
+        return jnp.broadcast_to(u_ref[pl.ds(at, 1), :], (GROUP, LANES)).astype(BF16)
+
+    return [[[one(part, row, col) for col in range(3)] for row in range(3)] for part in range(2)]
+
+
 def load_rows(u_ref, direction, spot, spots):
     def one(part, row, col):
         at = (((direction * 2 + part) * 3 + row) * 3 + col) * spots + spot
@@ -204,7 +227,7 @@
     count, tiles, planes, lx, groups, slots, empty,
     x_ref, u_ref, phase_ref, owner_ref, elem_ref, source_ref, spin_ref,
     sums_ref, rim_lhs_ref, table_ref,
-    v_ref, lhs_ref, op_ref, acc_ref, g_ref, pick_ref,
+    lhs_ref, op_ref, acc_ref, g_ref, pick_ref,
 ):
     spots = tiles * planes
     pair = 2
@@ -232,15 +255,14 @@
                 half, colour = part // 3, part % 3
                 for spot in range(spots):
                     piece = taken[spot * GROUP : (spot + 1) * GROUP, k * LANES : (k + 1) * LANES]
-                    v_ref[spot * 6 + part, at : at + GROUP, :] = piece
                     plane, tile = spot // tiles, spot % tiles
                     lhs_ref[
                         plane * halves + tile // pair,
+                        (tile % pair) * 3 + colour,
                         half * count + at : half * count + at + GROUP,
-                        ((tile % pair) * 3 + colour) * LANES : ((tile % pair) * 3 + colour + 1) * LANES,
                     ] = piece.astype(BF16)
 
-    lane = lax.broadcasted_iota(jnp.int32, (8, LANES), 1)
+    lane = lax.broadcasted_iota(jnp.int32, (GROUP, LANES), 1)
     wraps = (lane & (LZ - 1)) == LZ - 1
     spills = lane < LZ
 
@@ -249,45 +271,60 @@
         half_tile = step % halves
         for sub in range(pair):
             tile = half_tile * pair + sub
-            spot = plane * tiles + tile
-            next_tile = plane * tiles + (tile + 1) % tiles
+            ahead = step if sub + 1 < pair else plane * halves + (half_tile + 1) % halves
             for direction in directions:
-                links = load_links(u_ref, direction, tile * planes + plane, spots)
-                for at in range(0, count, 8):
-
-                    def part(where, k):
-                        return v_ref[where * 6 + k, at : at + 8, :]
+                narrow = direction in NARROW
+                links = (narrow_links if narrow else load_links)(
+                    u_ref, direction, tile * planes + plane, spots
+                )
+                for at in range(0, count, GROUP):
+
+                    def part(where, turn, k):
+                        row = k // 3 * count + at
+                        return lhs_ref[where, turn * 3 + k % 3, row : row + GROUP]
 
                     if direction == 0:
-                        vec = [part(spot + tiles, k) for k in range(6)]
+                        vec = [part(step + halves, sub, k) for k in range(6)]
                     elif direction == 1:
                         vec = [
-                            pltpu.roll(jnp.where(spills, part(next_tile, k), part(spot, k)), LANES - LZ, 1)
+                            pltpu.roll(
+                                jnp.where(spills, part(ahead, (sub + 1) % pair, k), part(step, sub, k)), LANES - LZ, 1
+                            )
                             for k in range(6)
                         ]
                     else:
                         vec = [
                             jnp.where(
                                 wraps,
-                                pltpu.roll(part(spot, k), LZ - 1, 1),
-                                pltpu.roll(part(spot, k), LANES - 1, 1),
+                                pltpu.roll(part(step, sub, k), LZ - 1, 1),
+                                pltpu.roll(part(step, sub, k), LANES - 1, 1),
                             )
                             for k in range(6)
                         ]
-                    outs = link_product(links, vec[:3], vec[3:])
+                    if narrow:
+                        outs = narrow_product(links, vec[:3], vec[3:])
+                    else:
+                        wide = [piece.astype(F32) for piece in vec]
+                        pieces = [[piece[eight : eight + 8] for piece in wide] for eight in (0, 8)]
+                        low, high = [link_product(links, piece[:3], piece[3:]) for piece in pieces]
+                        outs = [
+                            [
+                                jnp.concatenate([low[half][colour], high[half][colour]], axis=0).astype(BF16)
+                                for colour in range(3)
+                            ]
+                            for half in range(2)
+                        ]
                     for half in range(2):
                         row = (direction * 2 + half) * count + at
                         for colour in range(3):
-                            column = (sub * 3 + colour) * LANES
-                            op_ref[slot, row : row + 8, column : column + LANES] = outs[half][colour].astype(
-                                BF16
-                            )
+                            op_ref[slot, sub * 3 + colour, row : row + GROUP] = outs[half][colour]
 
     def multiply(step, slot, directions):
-        fixed = lhs_ref[step]
+        fixed = joined([lhs_ref[step, k] for k in range(3 * pair)])
         low = min(directions) * 2 * count
         high = (max(directions) + 1) * 2 * count
-        got = nt_dot(jnp.concatenate([fixed, op_ref[slot, low:high, :]], axis=0), fixed)
+        moving = joined([op_ref[slot, k, low:high] for k in range(3 * pair)])
+        got = nt_dot(jnp.concatenate([fixed, moving], axis=0), fixed)
         g_ref[step // halves] += got[: 2 * count]
         acc_ref[low:high, :] += got[2 * count :]
 
@@ -300,13 +337,9 @@
     multiply(steps - 1, (steps - 1) & 1, side)
     elementwise(0, 0, every)
 
-    def body(step, carry):
-        slot = step & 1
-        multiply(step - 1, 1 - slot, every)
-        elementwise(step, slot, every)
-        return carry
-
-    lax.fori_loop(1, inner, body, 0)
+    for step in range(1, inner):
+        multiply(step - 1, (step - 1) & 1, every)
+        elementwise(step, step & 1, every)
     multiply(inner - 1, (inner - 1) & 1, every)
     fill_table(groups, slots, empty, owner_ref, elem_ref, source_ref, spin_ref, table_ref)
 
@@ -334,20 +367,18 @@
     spots = tiles * planes
     pair = 2
     steps = planes * (tiles // pair)
-    wide = pair * 3 * LANES
     return pl.pallas_call(
         partial(gram_kernel, count, tiles, planes, lx, groups, slots, empty),
         in_specs=[vspec()] * 2 + [sspec()] + [vspec()] * 4,
         out_specs=[vspec()] * 3,
         out_shape=[
             jax.ShapeDtypeStruct((OPS, 2, count, count), F32),
-            jax.ShapeDtypeStruct((tiles // pair, 2 * count, wide), BF16),
+            jax.ShapeDtypeStruct((tiles // pair, 3 * pair, 2 * count, LANES), BF16),
             jax.ShapeDtypeStruct((1, LANES), jnp.int32),
         ],
         scratch_shapes=[
-            VMEM((spots * 6, count, LANES), F32),
-            VMEM((steps, 2 * count, wide), BF16),
-            VMEM((2, 6 * count, wide), BF16),
+            VMEM((steps, 3 * pair, 2 * count, LANES), BF16),
+            VMEM((2, 3 * pair, 6 * count, LANES), BF16),
             VMEM((6 * count, 2 * count), F32),
             VMEM((planes, 2 * count, 2 * count), F32),
             VMEM((GROUP * spots, GROUP * spots), BF16),
@@ -361,7 +392,8 @@
 def edge_kernel(count, rows, cores, halo_ref, lhs_ref, sums_ref, keep_ref, send_ref, tot_ref):
     total = None
     for half in range(halo_ref.shape[0]):
-        got = nt_dot(halo_ref[half], lhs_ref[half])
+        sides = [joined([ref[half, k] for k in range(ref.shape[1])]) for ref in (halo_ref, lhs_ref)]
+        got = nt_dot(*sides)
         total = got if total is None else total + got
     real = total[:count, :count] + total[count:, count:]
     imag = total[:count, count:] - total[count:, :count]

time: 36.7 us -> 36.7 us (level)
  waiting for transfers between devices: 10.3 us -> 13.7 us
  Pallas kernels: 16.5 us -> 13.9 us
  starting transfers between devices: 9.7 us -> 8.88 us
    pallas_call x1, Pallas kernels: 11 us -> 8.41 us  [gram(): pl.pallas_call(partial(gram_kernel, count, tiles, planes, lx, groups, slo...]
    ppermute x1, waiting for transfers between devices: 1.52 us -> 4.09 us  [fast_shards(): lax.ppermute(rim, 'space', [(i, (i + 1) % space_size) for i in range(spac...]
    ppermute x1, starting transfers between devices: 1.15 us -> 0.07 us  [fast_shards(): got = lax.ppermute(send, 'space', [(i, i ^ 1) for i in range(space_size)])]
    ppermute x3, waiting for transfers between devices: 3.56 us -> 4.02 us  [fast_shards(): lax.ppermute(parts[step], 'space', [(i, i ^ step * cores) for i in range(...]
  transfers between devices with their start and end apart: 8 -> 8, of which waited for: 7 -> 7; matrix products, arithmetic and copies ran while one was open for 0% -> 0% of each run, Pallas kernels for 30% -> 23%
where the time goes in v6:
time: 36.7 us; the launch traced here: 36.6 us
  Pallas kernels  13.9 us (38%)
  waiting for transfers between devices  13.7 us (37%)
  starting transfers between devices  8.88 us (24%)
    pallas_call x1, Pallas kernels, gram(): pl.pallas_call(partial(gram_kernel, count, tiles, planes, lx, groups, slo...  8.41 us
    ppermute x3, starting transfers between devices, fast_shards(): lax.ppermute(own, 'tm', [(i, i ^ step) for i in range(groups)])  4.45 us
    ppermute x1, waiting for transfers between devices, fast_shards(): lax.ppermute(rim, 'space', [(i, (i + 1) % space_size) for i in range(spac...  4.09 us
    ppermute x3, waiting for transfers between devices, fast_shards(): lax.ppermute(own, 'tm', [(i, i ^ step) for i in range(groups)])  4.03 us
    ppermute x3, waiting for transfers between devices, fast_shards(): lax.ppermute(parts[step], 'space', [(i, i ^ step * cores) for i in range(...  4.02 us
    ppermute x3, starting transfers between devices, fast_shards(): lax.ppermute(parts[step], 'space', [(i, i ^ step * cores) for i in range(...  3.81 us
    pallas_call x1, Pallas kernels, rim_plane(): pl.pallas_call(partial(rim_kernel, tiles, planes), in_specs=[pl.BlockSpec...  3.1 us
    pallas_call x1, Pallas kernels, dress(): pl.pallas_call(partial(dress_kernel, groups, slots, taus, rows, count), i...  1.9 us
  transfers between devices with their start and end apart: 8, of which 7 were waited for; matrix products, arithmetic and copies ran while one was open for 0% of the time, Pallas kernels for 23%

profile of v6, /device:TPU:0, one launch (start us, length us, event | category | flops | bytes accessed | tf_op | source)
XLA Modules:
  0.0 36.6 jit_solution(11025205361848173283)
XLA Ops:
  0.0 0.0 copy-start.5
  0.0 0.0 copy-start.4
  0.0 0.0 copy-start.3
  0.0 0.0 copy-start.2
  0.0 0.0 copy-start.1
  0.0 3.1 %rim.1 = (bf16[2,6,256,128]{3,2,1,0:T(8,128)(2,1)S(1)}, bf16[12288,128]{1,0:T(8,128)(2,1)S(1)}, f32[864,128]{1,0:T(8,128)S(1)}) custom-call(bf16[12288,128]{1,0:T(8,128)(2,1)} %bitcast.21, f32[864,128]{1,0:T(8,128)} %bitcast.22), custom_call_target="tpu_custom_call" | custom-call | flops 100000000 | bytes 4000000 | tf_op jit(solution)/shard_map/rim/pallas_call | solution.py:111
  3.1 0.5 %collective-permute-start = (bf16[2,6,256,128]{3,2,1,0:T(8,128)(2,1)S(1)}, bf16[2,6,256,128]{3,2,1,0:T(8,128)(2,1)S(1)}, u32[]{:S(2)}, u32[]{:S(2)}) collective-permute-start(bf16[2,6,256,128]{3,2,1,0:T(8,128)(2,1)S(1)} %get-tuple-element.20), channel_id=1, source_target_pairs={{0,1},{1,2},{2,3},{3,4},{4,5},{5,6},{6,7},{7,0},{8,9},{9,10},{10,1... | collective-permute-start | bytes 2359304 | tf_op jit(solution)/shard_map/ppermute | solution.py:551
  3.7 0.0 copy-done.5
  3.7 0.0 copy-done.4
  3.7 0.0 copy-done.3
  3.7 0.0 copy-done.2
  3.7 0.0 copy-done.1
  3.7 8.4 %gram.1 = (f32[4,2,128,128]{3,2,1,0:T(8,128)S(1)}, bf16[2,6,256,128]{3,2,1,0:T(8,128)(2,1)S(1)}, s32[1,128]{1,0:T(1,128)S(1)}) custom-call(bf16[12288,128]{1,0:T(8,128)(2,1)S(1)} %get-tuple-element.17.x_ref, f32[864,128]{1,0:T(8,128)S(1)} %get-tuple-element.18.u_ref, f32[64]{0:T(128)S(1)} %copy-done.5, s32[1,96]{1,0:T(1,128)S(1)} %bitcast.17, ...), custom_call_target="tpu_custom_call" | custom-call | flops 8000000000 | bytes 5000000 | tf_op jit(solution)/shard_map/gram/pallas_call | solution.py:370
  12.1 0.0 copy-start
  12.1 4.1 %collective-permute-done.halo_ref = bf16[2,6,256,128]{3,2,1,0:T(8,128)(2,1)S(1)} collective-permute-done((bf16[2,6,256,128]{3,2,1,0:T(8,128)(2,1)S(1)}, bf16[2,6,256,128]{3,2,1,0:T(8,128)(2,1)S(1)}, u32[]{:S(2)}, u32[]{:S(2)}) %collective-permute-start) | collective-permute-done | bytes 786464 | tf_op jit(solution)/shard_map/ppermute | solution.py:551
  16.2 0.5 %edge.1 = (f32[4,4,2,16,128]{4,3,2,1,0:T(8,128)S(1)}, f32[4,4,2,16,128]{4,3,2,1,0:T(8,128)S(1)}) custom-call(bf16[2,6,256,128]{3,2,1,0:T(8,128)(2,1)S(1)} %collective-permute-done.halo_ref, bf16[2,6,256,128]{3,2,1,0:T(8,128)(2,1)S(1)} %get-tuple-element.21.lhs_ref, f32[4,2,128,128]{3,2,1,0:T(8,128)S(1)} %get-tuple-element.22.sums_ref), custom_call_target="tpu_custom_call" | custom-call | flops 1000000000 | bytes 3000000 | tf_op jit(solution)/shard_map/edge/pallas_call | solution.py:416
  16.7 0.1 collective-permute-start.1
  16.8 1.5 %collective-permute-done.1.got_ref = f32[4,4,2,16,128]{4,3,2,1,0:T(8,128)S(1)} collective-permute-done((f32[4,4,2,16,128]{4,3,2,1,0:T(8,128)S(1)}, f32[4,4,2,16,128]{4,3,2,1,0:T(8,128)S(1)}, u32[]{:S(2)}, u32[]{:S(2)}) %collective-permute-start.1) | collective-permute-done | bytes 262176 | tf_op jit(solution)/shard_map/ppermute | solution.py:557
  18.3 1.4 %collective-permute-start.2 = (bf16[5,2,16,128]{3,2,1,0:T(8,128)(2,1)S(1)}, bf16[5,2,16,128]{3,2,1,0:T(8,128)(2,1)S(1)}, u32[]{:S(2)}, u32[]{:S(2)}) collective-permute-start(bf16[5,2,16,128]{3,2,1,0:T(8,128)(2,1)S(1)} %get-tuple-element.26), channel_id=1, source_target_pairs={{0,2},{1,3},{2,0},{3,1},{4,6},{5,7},{6,4},{7,5},{8,10},{9,11},{10,... | collective-permute-start | bytes 122888 | tf_op jit(solution)/shard_map/ppermute | solution.py:562
  19.7 1.5 %collective-permute-start.3 = (bf16[5,2,16,128]{3,2,1,0:T(8,128)(2,1)S(1)}, bf16[5,2,16,128]{3,2,1,0:T(8,128)(2,1)S(1)}, u32[]{:S(2)}, u32[]{:S(2)}) collective-permute-start(bf16[5,2,16,128]{3,2,1,0:T(8,128)(2,1)S(1)} %get-tuple-element.27), channel_id=1, source_target_pairs={{0,4},{1,5},{2,6},{3,7},{4,0},{5,1},{6,2},{7,3},{8,12},{9,13},{10,... | collective-permute-start | bytes 122888 | tf_op jit(solution)/shard_map/ppermute | solution.py:562
  21.3 0.9 %collective-permute-start.4 = (bf16[5,2,16,128]{3,2,1,0:T(8,128)(2,1)S(1)}, bf16[5,2,16,128]{3,2,1,0:T(8,128)(2,1)S(1)}, u32[]{:S(2)}, u32[]{:S(2)}) collective-permute-start(bf16[5,2,16,128]{3,2,1,0:T(8,128)(2,1)S(1)} %get-tuple-element.28), channel_id=1, source_target_pairs={{0,6},{1,7},{2,4},{3,5},{4,2},{5,3},{6,0},{7,1},{8,14},{9,15},{10,... | collective-permute-start | bytes 122888 | tf_op jit(solution)/shard_map/ppermute | solution.py:562
  22.1 0.3 collective-permute-done.2.refs_0_
  22.4 1.3 %collective-permute-done.3.refs_1_ = bf16[5,2,16,128]{3,2,1,0:T(8,128)(2,1)S(1)} collective-permute-done((bf16[5,2,16,128]{3,2,1,0:T(8,128)(2,1)S(1)}, bf16[5,2,16,128]{3,2,1,0:T(8,128)(2,1)S(1)}, u32[]{:S(2)}, u32[]{:S(2)}) %collective-permute-start.3) | collective-permute-done | bytes 40992 | tf_op jit(solution)/shard_map/ppermute | solution.py:562
  23.7 2.4 %collective-permute-done.4.refs_2_ = bf16[5,2,16,128]{3,2,1,0:T(8,128)(2,1)S(1)} collective-permute-done((bf16[5,2,16,128]{3,2,1,0:T(8,128)(2,1)S(1)}, bf16[5,2,16,128]{3,2,1,0:T(8,128)(2,1)S(1)}, u32[]{:S(2)}, u32[]{:S(2)}) %collective-permute-start.4) | collective-permute-done | bytes 40992 | tf_op jit(solution)/shard_map/ppermute | solution.py:562
  26.2 3.7 %collective-permute-start.7 = (bf16[4,2,16,128]{3,2,1,0:T(8,128)(2,1)S(1)}, bf16[4,2,16,128]{3,2,1,0:T(8,128)(2,1)S(1)}, u32[]{:S(2)}, u32[]{:S(2)}) collective-permute-start(bf16[4,2,16,128]{3,2,1,0:T(8,128)(2,1)S(1)} %total.1.refs_0_), channel_id=1, source_target_pairs={{0,24},{8,16},{16,8},{24,0},{1,25},{9,17},{17,9},{25,1},{2,26},{10... | collective-permute-start | bytes 98312 | tf_op jit(solution)/shard_map/ppermute | solution.py:567
  29.9 0.0 collective-permute-start.6
  29.9 0.8 %collective-permute-start.5 = (bf16[4,2,16,128]{3,2,1,0:T(8,128)(2,1)S(1)}, bf16[4,2,16,128]{3,2,1,0:T(8,128)(2,1)S(1)}, u32[]{:S(2)}, u32[]{:S(2)}) collective-permute-start(bf16[4,2,16,128]{3,2,1,0:T(8,128)(2,1)S(1)} %total.1.refs_0_), channel_id=1, source_target_pairs={{0,8},{8,0},{16,24},{24,16},{1,9},{9,1},{17,25},{25,17},{2,10},{10... | collective-permute-start | bytes 98312 | tf_op jit(solution)/shard_map/ppermute | solution.py:567
  30.6 1.4 %collective-permute-done.7.refs_3_ = bf16[4,2,16,128]{3,2,1,0:T(8,128)(2,1)S(1)} collective-permute-done((bf16[4,2,16,128]{3,2,1,0:T(8,128)(2,1)S(1)}, bf16[4,2,16,128]{3,2,1,0:T(8,128)(2,1)S(1)}, u32[]{:S(2)}, u32[]{:S(2)}) %collective-permute-start.7) | collective-permute-done | bytes 32800 | tf_op jit(solution)/shard_map/ppermute | solution.py:567
  32.1 2.6 %collective-permute-done.6.refs_2_ = bf16[4,2,16,128]{3,2,1,0:T(8,128)(2,1)S(1)} collective-permute-done((bf16[4,2,16,128]{3,2,1,0:T(8,128)(2,1)S(1)}, bf16[4,2,16,128]{3,2,1,0:T(8,128)(2,1)S(1)}, u32[]{:S(2)}, u32[]{:S(2)}) %collective-permute-start.6) | collective-permute-done | bytes 32800 | tf_op jit(solution)/shard_map/ppermute | solution.py:567
  34.7 0.0 collective-permute-done.5.refs_1_
  34.7 0.0 copy-done
  34.7 1.9 %dress.1 = bf16[4,18,2,16,128]{4,3,2,1,0:T(8,128)(2,1)} custom-call(s32[1,128]{1,0:T(1,128)S(1)} %get-tuple-element.19.table_ref, bf16[8,2,128,128]{3,2,1,0:T(8,128)(2,1)S(1)} %bitcast.16, bf16[4,2,16,128]{3,2,1,0:T(8,128)(2,1)S(1)} %total.1.refs_0_, bf16[4,2,16,128]{3,2,1,0:T(8,128)(2,1)S(1)} %collective-permute-done.5.refs_1_, ...), custom_call_target="tpu_custom_call" | custom-call | flops 1000000000 | bytes 2000000 | tf_op jit(solution)/shard_map/dress/pallas_call | solution.py:509
  (2 shorter events, 0.0 us)
Async XLA Ops:
  0.0 3.7 %copy-start.5 = (f32[64]{0:T(128)S(1)}, f32[64]{0:T(128)}, u32[]{:S(2)}) copy-start(f32[64]{0:T(128)} %constant.2.clone.phase_ref) | copy-start | bytes 772
  0.0 3.7 %copy-start.4 = (s32[96]{0:T(128)S(1)}, s32[96]{0:T(128)}, u32[]{:S(2)}) copy-start(s32[96]{0:T(128)} %param.14) | copy-start | bytes 1156
  0.0 3.7 %copy-start.3 = (s32[96]{0:T(128)S(1)}, s32[96]{0:T(128)}, u32[]{:S(2)}) copy-start(s32[96]{0:T(128)} %param.13) | copy-start | bytes 1156
  0.0 3.7 %copy-start.2 = (s32[96]{0:T(128)S(1)}, s32[96]{0:T(128)}, u32[]{:S(2)}) copy-start(s32[96]{0:T(128)} %param.12) | copy-start | bytes 1156
  0.0 3.7 %copy-start.1 = (s32[96,1]{0,1:T(1,128)S(1)}, s32[96,1]{0,1:T(1,128)}, u32[]{:S(2)}) copy-start(s32[96,1]{0,1:T(1,128)} %param.11) | copy-start | bytes 1156
  3.1 13.1 %collective-permute-start = (bf16[2,6,256,128]{3,2,1,0:T(8,128)(2,1)S(1)}, bf16[2,6,256,128]{3,2,1,0:T(8,128)(2,1)S(1)}, u32[]{:S(2)}, u32[]{:S(2)}) collective-permute-start(bf16[2,6,256,128]{3,2,1,0:T(8,128)(2,1)S(1)} %get-tuple-element.20), channel_id=1, source_target_pairs={{0,1},{1,2},{2,3},{3,4},{4,5},{5,6},{6,7},{7,0},{8,9},{9,10},{10,1... | collective-permute-start | bytes 2359304 | tf_op jit(solution)/shard_map/ppermute | solution.py:551
  12.1 22.6 %copy-start = (bf16[2,4,2,128,128]{4,3,2,1,0:T(8,128)(2,1)S(1)}, bf16[2,4,2,128,128]{4,3,2,1,0:T(8,128)(2,1)}, u32[]{:S(2)}) copy-start(bf16[2,4,2,128,128]{4,3,2,1,0:T(8,128)(2,1)} %param.10) | copy-start | bytes 1572868
  16.7 1.6 %collective-permute-start.1 = (f32[4,4,2,16,128]{4,3,2,1,0:T(8,128)S(1)}, f32[4,4,2,16,128]{4,3,2,1,0:T(8,128)S(1)}, u32[]{:S(2)}, u32[]{:S(2)}) collective-permute-start(f32[4,4,2,16,128]{4,3,2,1,0:T(8,128)S(1)} %get-tuple-element.24), channel_id=1, source_target_pairs={{0,1},{1,0},{2,3},{3,2},{4,5},{5,4},{6,7},{7,6},{8,9},{9,8},{10,11... | collective-permute-start | bytes 786440 | tf_op jit(solution)/shard_map/ppermute | solution.py:557
  18.3 4.1 %collective-permute-start.2 = (bf16[5,2,16,128]{3,2,1,0:T(8,128)(2,1)S(1)}, bf16[5,2,16,128]{3,2,1,0:T(8,128)(2,1)S(1)}, u32[]{:S(2)}, u32[]{:S(2)}) collective-permute-start(bf16[5,2,16,128]{3,2,1,0:T(8,128)(2,1)S(1)} %get-tuple-element.26), channel_id=1, source_target_pairs={{0,2},{1,3},{2,0},{3,1},{4,6},{5,7},{6,4},{7,5},{8,10},{9,11},{10,... | collective-permute-start | bytes 122888 | tf_op jit(solution)/shard_map/ppermute | solution.py:562
  19.7 4.0 %collective-permute-start.3 = (bf16[5,2,16,128]{3,2,1,0:T(8,128)(2,1)S(1)}, bf16[5,2,16,128]{3,2,1,0:T(8,128)(2,1)S(1)}, u32[]{:S(2)}, u32[]{:S(2)}) collective-permute-start(bf16[5,2,16,128]{3,2,1,0:T(8,128)(2,1)S(1)} %get-tuple-element.27), channel_id=1, source_target_pairs={{0,4},{1,5},{2,6},{3,7},{4,0},{5,1},{6,2},{7,3},{8,12},{9,13},{10,... | collective-permute-start | bytes 122888 | tf_op jit(solution)/shard_map/ppermute | solution.py:562
  21.3 4.9 %collective-permute-start.4 = (bf16[5,2,16,128]{3,2,1,0:T(8,128)(2,1)S(1)}, bf16[5,2,16,128]{3,2,1,0:T(8,128)(2,1)S(1)}, u32[]{:S(2)}, u32[]{:S(2)}) collective-permute-start(bf16[5,2,16,128]{3,2,1,0:T(8,128)(2,1)S(1)} %get-tuple-element.28), channel_id=1, source_target_pairs={{0,6},{1,7},{2,4},{3,5},{4,2},{5,3},{6,0},{7,1},{8,14},{9,15},{10,... | collective-permute-start | bytes 122888 | tf_op jit(solution)/shard_map/ppermute | solution.py:562
  26.2 5.9 %collective-permute-start.7 = (bf16[4,2,16,128]{3,2,1,0:T(8,128)(2,1)S(1)}, bf16[4,2,16,128]{3,2,1,0:T(8,128)(2,1)S(1)}, u32[]{:S(2)}, u32[]{:S(2)}) collective-permute-start(bf16[4,2,16,128]{3,2,1,0:T(8,128)(2,1)S(1)} %total.1.refs_0_), channel_id=1, source_target_pairs={{0,24},{8,16},{16,8},{24,0},{1,25},{9,17},{17,9},{25,1},{2,26},{10... | collective-permute-start | bytes 98312 | tf_op jit(solution)/shard_map/ppermute | solution.py:567
  29.9 4.8 %collective-permute-start.6 = (bf16[4,2,16,128]{3,2,1,0:T(8,128)(2,1)S(1)}, bf16[4,2,16,128]{3,2,1,0:T(8,128)(2,1)S(1)}, u32[]{:S(2)}, u32[]{:S(2)}) collective-permute-start(bf16[4,2,16,128]{3,2,1,0:T(8,128)(2,1)S(1)} %total.1.refs_0_), channel_id=1, source_target_pairs={{0,16},{8,24},{16,0},{24,8},{1,17},{9,25},{17,1},{25,9},{2,18},{10... | collective-permute-start | bytes 98312 | tf_op jit(solution)/shard_map/ppermute | solution.py:567
  29.9 4.8 %collective-permute-start.5 = (bf16[4,2,16,128]{3,2,1,0:T(8,128)(2,1)S(1)}, bf16[4,2,16,128]{3,2,1,0:T(8,128)(2,1)S(1)}, u32[]{:S(2)}, u32[]{:S(2)}) collective-permute-start(bf16[4,2,16,128]{3,2,1,0:T(8,128)(2,1)S(1)} %total.1.refs_0_), channel_id=1, source_target_pairs={{0,8},{8,0},{16,24},{24,16},{1,9},{9,1},{17,25},{25,17},{2,10},{10... | collective-permute-start | bytes 98312 | tf_op jit(solution)/shard_map/ppermute | solution.py:567

commit v7 on v6

--- a/solution.py
+++ b/solution.py
@@ -53,41 +53,42 @@
     return lax.dot_general(left, right, (((1,), (1,)), ((), ())), preferred_element_type=F32)
 
 
-def rim_kernel(tiles, planes, x_hbm, u_hbm, out_ref, x_ref, u_ref, pick_ref, link_ref, sems):
+def rim_kernel(tiles, planes, start, leads, x_hbm, u_hbm, *refs):
+    if leads:
+        out_ref, x_ref, link_ref, u_ref, pick_ref, sems = refs
+    else:
+        link_ref, out_ref, x_ref, u_ref, pick_ref, sems = refs
     spots = tiles * planes
     pair = 2
-    count = out_ref.shape[2] // 2
+    part_count = out_ref.shape[2] // 2
     chunk = GROUP * 6 * spots
-    chunks = count // GROUP
-    first = 18 * spots
-    head, tail = pl.ds(0, first), pl.ds(first, u_hbm.shape[0] - first)
-    copies = []
-    for g in range(chunks):
-        rows = pl.ds(g * chunk, chunk)
-        copies.append(pltpu.make_async_copy(x_hbm.at[rows], x_ref.at[rows], sems.at[g]))
-    link_copy = pltpu.make_async_copy(u_hbm.at[head], u_ref.at[head], sems.at[chunks])
-    rest_copy = pltpu.make_async_copy(u_hbm.at[tail], u_ref.at[tail], sems.at[chunks + 1])
-    for copy in [link_copy] + copies + [rest_copy]:
+    chunks = part_count // GROUP
+    rows_of = [pl.ds(g * chunk, chunk) for g in range(chunks)]
+    copies = [
+        pltpu.make_async_copy(x_hbm.at[pl.ds((start + g) * chunk, chunk)], x_ref.at[rows], sems.at[g])
+        for g, rows in enumerate(rows_of)
+    ]
+    link_copy = pltpu.make_async_copy(u_hbm.at[pl.ds(0, u_ref.shape[0])], u_ref, sems.at[chunks])
+    for copy in [link_copy] + copies if leads else copies + [link_copy]:
         copy.start()
 
     def source(row):
         return (row & (GROUP - 1)) * spots + (row // GROUP) * planes + planes - 1
 
     pick_ref[...] = pick_matrix(tiles * GROUP, GROUP * spots, source)
-    link_copy.wait()
-    for tile in range(tiles):
-        flat = adjoint(load_rows(u_ref, 0, tile * planes + planes - 1, spots))
-        for k, link in enumerate(flat):
-            link_ref[tile, k] = link
+    if leads:
+        link_copy.wait()
+        for tile in range(tiles):
+            flat = adjoint(load_rows(u_ref, 0, tile * planes + planes - 1, spots))
+            for k, link in enumerate(flat):
+                link_ref[tile, k] = link
     chosen = pick_ref[...]
     for g in range(chunks):
         copies[g].wait()
         block = x_ref[g * chunk : (g + 1) * chunk, :].reshape(GROUP, 6, spots, LANES)
         taken = []
         for part in range(0, 6, 2):
-            rows = jnp.concatenate(
-                [block[:, part + k].reshape(GROUP * spots, LANES) for k in range(2)], axis=1
-            )
+            rows = joined([block[:, part + k].reshape(GROUP * spots, LANES) for k in range(2)])
             got = jnp.dot(chosen, rows, preferred_element_type=F32)
             taken += [got[:, :LANES], got[:, LANES:]]
         for tile in range(tiles):
@@ -98,34 +99,44 @@
                 vec = [part[at : at + 8] for part in taken]
                 outs.append(link_product(links, vec[:3], vec[3:]))
             for half in range(2):
-                row = half * count + g * GROUP
+                row = half * part_count + g * GROUP
                 for colour in range(3):
                     both = jnp.concatenate([outs[0][half][colour], outs[1][half][colour]], axis=0)
                     out_ref[tile // pair, (tile % pair) * 3 + colour, row : row + GROUP] = both.astype(BF16)
-    rest_copy.wait()
-
-
-def rim_plane(x, u, count, tiles, planes):
+    if not leads:
+        link_copy.wait()
+
+
+def rim_plane(x, u, links, count, tiles, planes):
     spots = tiles * planes
     pair = 2
+    leads = links is None
+    part_count = count // 2
+    chunks = part_count // GROUP
+    hbm = pl.BlockSpec(memory_space=pltpu.HBM)
+    out_shape = [
+        jax.ShapeDtypeStruct((tiles // pair, 3 * pair, 2 * part_count, LANES), BF16),
+        jax.ShapeDtypeStruct((x.shape[0] // 2, LANES), BF16),
+    ]
+    scratch = [
+        VMEM((tiles * GROUP, GROUP * spots), BF16),
+        pltpu.SemaphoreType.DMA((chunks + 1,)),
+    ]
+    if leads:
+        out_shape.append(jax.ShapeDtypeStruct((tiles, 27, 8, LANES), F32))
+        scratch = [VMEM((18 * spots, LANES), F32)] + scratch
+    else:
+        out_shape.append(jax.ShapeDtypeStruct(u.shape, F32))
     return pl.pallas_call(
-        partial(rim_kernel, tiles, planes),
-        in_specs=[pl.BlockSpec(memory_space=pltpu.HBM)] * 2,
+        partial(rim_kernel, tiles, planes, 0 if leads else chunks, leads),
+        in_specs=[hbm, hbm] + ([] if leads else [vspec()]),
         out_specs=[vspec()] * 3,
-        out_shape=[
-            jax.ShapeDtypeStruct((tiles // pair, 3 * pair, 2 * count, LANES), BF16),
-            jax.ShapeDtypeStruct(x.shape, BF16),
-            jax.ShapeDtypeStruct(u.shape, F32),
-        ],
-        scratch_shapes=[
-            VMEM((tiles * GROUP, GROUP * spots), BF16),
-            VMEM((tiles, 27, 8, LANES), F32),
-            pltpu.SemaphoreType.DMA((count // GROUP + 2,)),
-        ],
-        compiler_params=limit(8),
-        cost_estimate=cost(10**8, 4 * 10**6),
-        name="rim",
-    )(x, u)
+        out_shape=out_shape,
+        scratch_shapes=scratch,
+        compiler_params=limit(6),
+        cost_estimate=cost(10**8, 2 * 10**6),
+        name="rim" if leads else "rest",
+    )(x, u, *([] if leads else [links]))
 
 
 def link_product(links, vec_re, vec_im):
@@ -225,7 +236,7 @@
 
 def gram_kernel(
     count, tiles, planes, lx, groups, slots, empty,
-    x_ref, u_ref, phase_ref, owner_ref, elem_ref, source_ref, spin_ref,
+    low_ref, high_ref, u_ref, phase_ref, owner_ref, elem_ref, source_ref, spin_ref,
     sums_ref, rim_lhs_ref, table_ref,
     lhs_ref, op_ref, acc_ref, g_ref, pick_ref,
 ):
@@ -244,7 +255,8 @@
 
     chosen = pick_ref[...]
     for at in range(0, count, GROUP):
-        block = x_ref[at * 6 * spots : (at + GROUP) * 6 * spots, :].reshape(GROUP, 6, spots, LANES)
+        x_ref, near = (low_ref, at) if at < count // 2 else (high_ref, at - count // 2)
+        block = x_ref[near * 6 * spots : (near + GROUP) * 6 * spots, :].reshape(GROUP, 6, spots, LANES)
         for first in range(0, 6, 2):
             rows = jnp.concatenate(
                 [block[:, first + k].reshape(GROUP * spots, LANES) for k in range(2)], axis=1
@@ -363,13 +375,13 @@
         rim_lhs_ref[half] = lhs_ref[half]
 
 
-def gram(x, u, phases, tables, count, tiles, planes, lx, groups, slots, empty):
+def gram(low, high, u, phases, tables, count, tiles, planes, lx, groups, slots, empty):
     spots = tiles * planes
     pair = 2
     steps = planes * (tiles // pair)
     return pl.pallas_call(
         partial(gram_kernel, count, tiles, planes, lx, groups, slots, empty),
-        in_specs=[vspec()] * 2 + [sspec()] + [vspec()] * 4,
+        in_specs=[vspec()] * 3 + [sspec()] + [vspec()] * 4,
         out_specs=[vspec()] * 3,
         out_shape=[
             jax.ShapeDtypeStruct((OPS, 2, count, count), F32),
@@ -386,17 +398,21 @@
         compiler_params=limit(26),
         cost_estimate=cost(8 * 10**9, 5 * 10**6),
         name="gram",
-    )(x, u, phases, *tables)
-
-
-def edge_kernel(count, rows, cores, halo_ref, lhs_ref, sums_ref, keep_ref, send_ref, tot_ref):
-    total = None
-    for half in range(halo_ref.shape[0]):
-        sides = [joined([ref[half, k] for k in range(ref.shape[1])]) for ref in (halo_ref, lhs_ref)]
-        got = nt_dot(*sides)
-        total = got if total is None else total + got
-    real = total[:count, :count] + total[count:, count:]
-    imag = total[:count, count:] - total[count:, :count]
+    )(low, high, u, phases, *tables)
+
+
+def edge_kernel(count, rows, cores, low_ref, high_ref, lhs_ref, sums_ref, keep_ref, send_ref, tot_ref):
+    reals, imags = [], []
+    for halo_ref in (low_ref, high_ref):
+        total = None
+        for half in range(halo_ref.shape[0]):
+            sides = [joined([ref[half, k] for k in range(ref.shape[1])]) for ref in (halo_ref, lhs_ref)]
+            got = nt_dot(*sides)
+            total = got if total is None else total + got
+        mid = total.shape[0] // 2
+        reals.append(total[:mid, :count] + total[mid:, count:])
+        imags.append(total[:mid, count:] - total[mid:, :count])
+    real, imag = jnp.concatenate(reals, axis=0), jnp.concatenate(imags, axis=0)
     tot_ref[0] = 0.5 * (real - real.T)
     tot_ref[1] = 0.5 * (imag + imag.T)
     mine = lax.axis_index("space") & (cores - 1)
@@ -411,18 +427,18 @@
                     ref[chip, op, half] = piece
 
 
-def edge(halo, rim_lhs, sums, count, rows, cores):
+def edge(halos, rim_lhs, sums, count, rows, cores):
     shape = jax.ShapeDtypeStruct((count // (rows * cores), OPS, 2, rows, count), F32)
     return pl.pallas_call(
         partial(edge_kernel, count, rows, cores),
-        in_specs=[vspec()] * 3,
+        in_specs=[vspec()] * 4,
         out_specs=[vspec(), vspec()],
         out_shape=[shape, shape],
         scratch_shapes=[VMEM((2, count, count), F32)],
         compiler_params=limit(8),
         cost_estimate=cost(10**9, 3 * 10**6),
         name="edge",
-    )(halo, rim_lhs, sums)
+    )(*halos, rim_lhs, sums)
 
 
 def split_sum(block):
@@ -547,17 +563,21 @@
     empty = per.shape[0] * groups * OPS
     x = pltpu.with_memory_space_constraint(x, pltpu.HBM)
     u = pltpu.with_memory_space_constraint(u, pltpu.HBM)
-    rim, x, u = rim_plane(x, u, count, tiles, planes)
-    halo = lax.ppermute(rim, "space", [(i, (i + 1) % space_size) for i in range(space_size)])
+    up = [(i, (i + 1) % space_size) for i in range(space_size)]
+    rim, low, links = rim_plane(x, u, None, count, tiles, planes)
+    halos = [lax.ppermute(rim, "space", up)]
+    rim, high, u = rim_plane(x, u, links, count, tiles, planes)
+    halos.append(lax.ppermute(rim, "space", up))
     tables = [job.reshape(1, -1) for job in (job_owner, job_elemental, job_source, job_spin)]
     sums, rim_lhs, table = gram(
-        x, u, phases, tables, count, tiles, planes, lx, groups, slots, empty
-    )
-    keep, send = edge(halo, rim_lhs, sums, count, rows, cores)
+        low, high, u, phases, tables, count, tiles, planes, lx, groups, slots, empty
+    )
+    keep, send = edge(halos, rim_lhs, sums, count, rows, cores)
     got = lax.ppermute(send, "space", [(i, i ^ 1) for i in range(space_size)])
     parts = fold(keep, got, cores)
     summed = [parts[0]]
-    for step in range(1, space_size // cores):
+    chips = space_size // cores
+    for step in sorted(range(1, chips), key=lambda step: -bin(step).count("1")):
         summed.append(
             lax.ppermute(parts[step], "space", [(i, i ^ (step * cores)) for i in range(space_size)])
         )

time: 36.7 us -> 35.9 us (0.978)
  waiting for transfers between devices: 13.7 us -> 9.14 us
  starting transfers between devices: 8.88 us -> 11.3 us
  Pallas kernels: 13.9 us -> 15.2 us
    ppermute x1 -> x2, waiting for transfers between devices: 4.09 us -> 0.01 us  [the longest x1 0.01 us: fast_shards(): halos.append(lax.ppermute(rim, 'space', up))]
    ppermute x1 -> x2, starting transfers between devices: 0.54 us -> 3.19 us  [the longest x1 2.64 us: fast_shards(): halos.append(lax.ppermute(rim, 'space', up))]
    pallas_call x1 -> x2, Pallas kernels: 3.1 us -> 4.09 us  [rim_plane(): pl.pallas_call(partial(rim_kernel, tiles, planes, 0 if leads else chunks,...]
    ppermute x3, waiting for transfers between devices: 4.02 us -> 3.62 us  [fast_shards(): lax.ppermute(parts[step], 'space', [(i, i ^ step * cores) for i in range(...]
  transfers between devices with their start and end apart: 8 -> 9, of which waited for: 7 -> 6; matrix products, arithmetic and copies ran while one was open for 0% -> 0% of each run, Pallas kernels for 23% -> 29%
where the time goes in v7:
time: 35.9 us; the launch traced here: 35.8 us
  Pallas kernels  15.2 us (42%)
  starting transfers between devices  11.3 us (31%)
  waiting for transfers between devices  9.14 us (25%)
    pallas_call x1, Pallas kernels, gram(): pl.pallas_call(partial(gram_kernel, count, tiles, planes, lx, groups, slo...  8.41 us
    ppermute x3, starting transfers between devices, fast_shards(): lax.ppermute(own, 'tm', [(i, i ^ step) for i in range(groups)])  4.45 us
    pallas_call x2, Pallas kernels, rim_plane(): pl.pallas_call(partial(rim_kernel, tiles, planes, 0 if leads else chunks,...  4.09 us
    ppermute x3, waiting for transfers between devices, fast_shards(): lax.ppermute(own, 'tm', [(i, i ^ step) for i in range(groups)])  4.03 us
    ppermute x3, waiting for transfers between devices, fast_shards(): lax.ppermute(parts[step], 'space', [(i, i ^ step * cores) for i in range(...  3.62 us
    ppermute x3, starting transfers between devices, fast_shards(): lax.ppermute(parts[step], 'space', [(i, i ^ step * cores) for i in range(...  3.55 us
    ppermute x1, starting transfers between devices, fast_shards(): halos.append(lax.ppermute(rim, 'space', up))  2.64 us
    pallas_call x1, Pallas kernels, dress(): pl.pallas_call(partial(dress_kernel, groups, slots, taus, rows, count), i...  1.9 us
  transfers between devices with their start and end apart: 9, of which 6 were waited for; matrix products, arithmetic and copies ran while one was open for 0% of the time, Pallas kernels for 29%

profile of v7, /device:TPU:0, one launch (start us, length us, event | category | flops | bytes accessed | tf_op | source)
XLA Modules:
  0.0 35.8 jit_solution(3854488148204681742)
XLA Ops:
  0.0 2.1 %rim.1 = (bf16[2,6,128,128]{3,2,1,0:T(8,128)(2,1)S(1)}, bf16[6144,128]{1,0:T(8,128)(2,1)S(1)}, f32[4,27,8,128]{3,2,1,0:T(8,128)S(1)}) custom-call(bf16[12288,128]{1,0:T(8,128)(2,1)} %bitcast.21, f32[864,128]{1,0:T(8,128)} %bitcast.23), custom_call_target="tpu_custom_call" | custom-call | flops 100000000 | bytes 2000000 | tf_op jit(solution)/shard_map/rim/pallas_call | solution.py:130
  2.1 0.5 %collective-permute-start = (bf16[2,6,128,128]{3,2,1,0:T(8,128)(2,1)S(1)}, bf16[2,6,128,128]{3,2,1,0:T(8,128)(2,1)S(1)}, u32[]{:S(2)}, u32[]{:S(2)}) collective-permute-start(bf16[2,6,128,128]{3,2,1,0:T(8,128)(2,1)S(1)} %get-tuple-element.25), channel_id=1, source_target_pairs={{0,1},{1,2},{2,3},{3,4},{4,5},{5,6},{6,7},{7,0},{8,9},{9,10},{10,1... | collective-permute-start | bytes 1179656 | tf_op jit(solution)/shard_map/ppermute | solution.py:568
  2.6 0.0 copy-start.1
  2.6 0.0 copy-start.5
  2.6 2.0 %rest.1 = (bf16[2,6,128,128]{3,2,1,0:T(8,128)(2,1)S(1)}, bf16[6144,128]{1,0:T(8,128)(2,1)S(1)}, f32[864,128]{1,0:T(8,128)S(1)}) custom-call(bf16[12288,128]{1,0:T(8,128)(2,1)} %bitcast.22, f32[864,128]{1,0:T(8,128)} %bitcast.24, f32[4,27,8,128]{3,2,1,0:T(8,128)S(1)} %get-tuple-element.21.refs_0_), custom_call_target="tpu_custom_call" | custom-call | flops 100000000 | bytes 2000000 | tf_op jit(solution)/shard_map/rest/pallas_call | solution.py:130
  4.7 2.6 %collective-permute-start.1 = (bf16[2,6,128,128]{3,2,1,0:T(8,128)(2,1)S(1)}, bf16[2,6,128,128]{3,2,1,0:T(8,128)(2,1)S(1)}, u32[]{:S(2)}, u32[]{:S(2)}) collective-permute-start(bf16[2,6,128,128]{3,2,1,0:T(8,128)(2,1)S(1)} %get-tuple-element.26), channel_id=1, source_target_pairs={{0,1},{1,2},{2,3},{3,4},{4,5},{5,6},{6,7},{7,0},{8,9},{9,10},{10,1... | collective-permute-start | bytes 1179656 | tf_op jit(solution)/shard_map/ppermute | solution.py:570
  7.3 0.0 copy-done.1
  7.3 0.0 copy-done.2
  7.3 0.0 copy-done.3
  7.3 0.0 copy-done.4
  7.3 0.0 copy-done.5
  7.3 8.4 %gram.1 = (f32[4,2,128,128]{3,2,1,0:T(8,128)S(1)}, bf16[2,6,256,128]{3,2,1,0:T(8,128)(2,1)S(1)}, s32[1,128]{1,0:T(1,128)S(1)}) custom-call(bf16[6144,128]{1,0:T(8,128)(2,1)S(1)} %get-tuple-element.20.low_ref, bf16[6144,128]{1,0:T(8,128)(2,1)S(1)} %get-tuple-element.22.high_ref, f32[864,128]{1,0:T(8,128)S(1)} %get-tuple-element.23.u_ref, f32[64]{0:T(128)S(1)} %copy-done.5, ...), custom_call_target="tpu_custom_call" | custom-call | flops 8000000000 | bytes 5000000 | tf_op jit(solution)/shard_map/gram/pallas_call | solution.py:382
  15.8 0.0 collective-permute-done.low_ref
  15.8 0.0 collective-permute-done.1.high_ref
  15.8 0.0 copy-start
  15.8 0.7 %edge.1 = (f32[4,4,2,16,128]{4,3,2,1,0:T(8,128)S(1)}, f32[4,4,2,16,128]{4,3,2,1,0:T(8,128)S(1)}) custom-call(bf16[2,6,128,128]{3,2,1,0:T(8,128)(2,1)S(1)} %collective-permute-done.low_ref, bf16[2,6,128,128]{3,2,1,0:T(8,128)(2,1)S(1)} %collective-permute-done.1.high_ref, bf16[2,6,256,128]{3,2,1,0:T(8,128)(2,1)S(1)} %get-tuple-element.27.lhs_ref, ...), custom_call_target="tpu_custom_call" | custom-call | flops 1000000000 | bytes 3000000 | tf_op jit(solution)/shard_map/edge/pallas_call | solution.py:432
  16.5 0.1 collective-permute-start.2
  16.6 1.5 %collective-permute-done.2.got_ref = f32[4,4,2,16,128]{4,3,2,1,0:T(8,128)S(1)} collective-permute-done((f32[4,4,2,16,128]{4,3,2,1,0:T(8,128)S(1)}, f32[4,4,2,16,128]{4,3,2,1,0:T(8,128)S(1)}, u32[]{:S(2)}, u32[]{:S(2)}) %collective-permute-start.2) | collective-permute-done | bytes 262176 | tf_op jit(solution)/shard_map/ppermute | solution.py:576
  18.2 1.7 %collective-permute-start.3 = (bf16[5,2,16,128]{3,2,1,0:T(8,128)(2,1)S(1)}, bf16[5,2,16,128]{3,2,1,0:T(8,128)(2,1)S(1)}, u32[]{:S(2)}, u32[]{:S(2)}) collective-permute-start(bf16[5,2,16,128]{3,2,1,0:T(8,128)(2,1)S(1)} %get-tuple-element.32), channel_id=1, source_target_pairs={{0,6},{1,7},{2,4},{3,5},{4,2},{5,3},{6,0},{7,1},{8,14},{9,15},{10,... | collective-permute-start | bytes 122888 | tf_op jit(solution)/shard_map/ppermute | solution.py:582
  19.9 1.4 %collective-permute-start.4 = (bf16[5,2,16,128]{3,2,1,0:T(8,128)(2,1)S(1)}, bf16[5,2,16,128]{3,2,1,0:T(8,128)(2,1)S(1)}, u32[]{:S(2)}, u32[]{:S(2)}) collective-permute-start(bf16[5,2,16,128]{3,2,1,0:T(8,128)(2,1)S(1)} %get-tuple-element.33), channel_id=1, source_target_pairs={{0,2},{1,3},{2,0},{3,1},{4,6},{5,7},{6,4},{7,5},{8,10},{9,11},{10,... | collective-permute-start | bytes 122888 | tf_op jit(solution)/shard_map/ppermute | solution.py:582
  21.3 0.4 %collective-permute-start.5 = (bf16[5,2,16,128]{3,2,1,0:T(8,128)(2,1)S(1)}, bf16[5,2,16,128]{3,2,1,0:T(8,128)(2,1)S(1)}, u32[]{:S(2)}, u32[]{:S(2)}) collective-permute-start(bf16[5,2,16,128]{3,2,1,0:T(8,128)(2,1)S(1)} %get-tuple-element.34), channel_id=1, source_target_pairs={{0,4},{1,5},{2,6},{3,7},{4,0},{5,1},{6,2},{7,3},{8,12},{9,13},{10,... | collective-permute-start | bytes 122888 | tf_op jit(solution)/shard_map/ppermute | solution.py:582
  21.7 1.5 %collective-permute-done.3.refs_0_ = bf16[5,2,16,128]{3,2,1,0:T(8,128)(2,1)S(1)} collective-permute-done((bf16[5,2,16,128]{3,2,1,0:T(8,128)(2,1)S(1)}, bf16[5,2,16,128]{3,2,1,0:T(8,128)(2,1)S(1)}, u32[]{:S(2)}, u32[]{:S(2)}) %collective-permute-start.3) | collective-permute-done | bytes 40992 | tf_op jit(solution)/shard_map/ppermute | solution.py:582
  23.2 0.7 %collective-permute-done.4.refs_1_ = bf16[5,2,16,128]{3,2,1,0:T(8,128)(2,1)S(1)} collective-permute-done((bf16[5,2,16,128]{3,2,1,0:T(8,128)(2,1)S(1)}, bf16[5,2,16,128]{3,2,1,0:T(8,128)(2,1)S(1)}, u32[]{:S(2)}, u32[]{:S(2)}) %collective-permute-start.4) | collective-permute-done | bytes 40992 | tf_op jit(solution)/shard_map/ppermute | solution.py:582
  23.9 1.4 %collective-permute-done.5.refs_2_ = bf16[5,2,16,128]{3,2,1,0:T(8,128)(2,1)S(1)} collective-permute-done((bf16[5,2,16,128]{3,2,1,0:T(8,128)(2,1)S(1)}, bf16[5,2,16,128]{3,2,1,0:T(8,128)(2,1)S(1)}, u32[]{:S(2)}, u32[]{:S(2)}) %collective-permute-start.5) | collective-permute-done | bytes 40992 | tf_op jit(solution)/shard_map/ppermute | solution.py:582
  25.4 3.7 %collective-permute-start.8 = (bf16[4,2,16,128]{3,2,1,0:T(8,128)(2,1)S(1)}, bf16[4,2,16,128]{3,2,1,0:T(8,128)(2,1)S(1)}, u32[]{:S(2)}, u32[]{:S(2)}) collective-permute-start(bf16[4,2,16,128]{3,2,1,0:T(8,128)(2,1)S(1)} %total.1.refs_0_), channel_id=1, source_target_pairs={{0,24},{8,16},{16,8},{24,0},{1,25},{9,17},{17,9},{25,1},{2,26},{10... | collective-permute-start | bytes 98312 | tf_op jit(solution)/shard_map/ppermute | solution.py:587
  29.0 0.0 collective-permute-start.7
  29.0 0.8 %collective-permute-start.6 = (bf16[4,2,16,128]{3,2,1,0:T(8,128)(2,1)S(1)}, bf16[4,2,16,128]{3,2,1,0:T(8,128)(2,1)S(1)}, u32[]{:S(2)}, u32[]{:S(2)}) collective-permute-start(bf16[4,2,16,128]{3,2,1,0:T(8,128)(2,1)S(1)} %total.1.refs_0_), channel_id=1, source_target_pairs={{0,8},{8,0},{16,24},{24,16},{1,9},{9,1},{17,25},{25,17},{2,10},{10... | collective-permute-start | bytes 98312 | tf_op jit(solution)/shard_map/ppermute | solution.py:587
  29.8 1.3 %collective-permute-done.8.refs_3_ = bf16[4,2,16,128]{3,2,1,0:T(8,128)(2,1)S(1)} collective-permute-done((bf16[4,2,16,128]{3,2,1,0:T(8,128)(2,1)S(1)}, bf16[4,2,16,128]{3,2,1,0:T(8,128)(2,1)S(1)}, u32[]{:S(2)}, u32[]{:S(2)}) %collective-permute-start.8) | collective-permute-done | bytes 32800 | tf_op jit(solution)/shard_map/ppermute | solution.py:587
  31.2 2.7 %collective-permute-done.7.refs_2_ = bf16[4,2,16,128]{3,2,1,0:T(8,128)(2,1)S(1)} collective-permute-done((bf16[4,2,16,128]{3,2,1,0:T(8,128)(2,1)S(1)}, bf16[4,2,16,128]{3,2,1,0:T(8,128)(2,1)S(1)}, u32[]{:S(2)}, u32[]{:S(2)}) %collective-permute-start.7) | collective-permute-done | bytes 32800 | tf_op jit(solution)/shard_map/ppermute | solution.py:587
  33.8 0.0 collective-permute-done.6.refs_1_
  33.8 0.0 copy-done
  33.9 1.9 %dress.1 = bf16[4,18,2,16,128]{4,3,2,1,0:T(8,128)(2,1)} custom-call(s32[1,128]{1,0:T(1,128)S(1)} %get-tuple-element.24.table_ref, bf16[8,2,128,128]{3,2,1,0:T(8,128)(2,1)S(1)} %bitcast.16, bf16[4,2,16,128]{3,2,1,0:T(8,128)(2,1)S(1)} %total.1.refs_0_, bf16[4,2,16,128]{3,2,1,0:T(8,128)(2,1)S(1)} %collective-permute-done.6.refs_1_, ...), custom_call_target="tpu_custom_call" | custom-call | flops 1000000000 | bytes 2000000 | tf_op jit(solution)/shard_map/dress/pallas_call | solution.py:525
  (5 shorter events, 0.1 us)
Async XLA Ops:
  2.1 13.7 %collective-permute-start = (bf16[2,6,128,128]{3,2,1,0:T(8,128)(2,1)S(1)}, bf16[2,6,128,128]{3,2,1,0:T(8,128)(2,1)S(1)}, u32[]{:S(2)}, u32[]{:S(2)}) collective-permute-start(bf16[2,6,128,128]{3,2,1,0:T(8,128)(2,1)S(1)} %get-tuple-element.25), channel_id=1, source_target_pairs={{0,1},{1,2},{2,3},{3,4},{4,5},{5,6},{6,7},{7,0},{8,9},{9,10},{10,1... | collective-permute-start | bytes 1179656 | tf_op jit(solution)/shard_map/ppermute | solution.py:568
  2.6 4.7 %copy-start.1 = (s32[96,1]{0,1:T(1,128)S(1)}, s32[96,1]{0,1:T(1,128)}, u32[]{:S(2)}) copy-start(s32[96,1]{0,1:T(1,128)} %param.11) | copy-start | bytes 1156
  2.6 4.7 %copy-start.2 = (s32[96]{0:T(128)S(1)}, s32[96]{0:T(128)}, u32[]{:S(2)}) copy-start(s32[96]{0:T(128)} %param.12) | copy-start | bytes 1156
  2.6 4.7 %copy-start.3 = (s32[96]{0:T(128)S(1)}, s32[96]{0:T(128)}, u32[]{:S(2)}) copy-start(s32[96]{0:T(128)} %param.13) | copy-start | bytes 1156
  2.6 4.7 %copy-start.4 = (s32[96]{0:T(128)S(1)}, s32[96]{0:T(128)}, u32[]{:S(2)}) copy-start(s32[96]{0:T(128)} %param.14) | copy-start | bytes 1156
  2.6 4.7 %copy-start.5 = (f32[64]{0:T(128)S(1)}, f32[64]{0:T(128)}, u32[]{:S(2)}) copy-start(f32[64]{0:T(128)} %constant.2.clone.phase_ref) | copy-start | bytes 772
  4.7 11.1 %collective-permute-start.1 = (bf16[2,6,128,128]{3,2,1,0:T(8,128)(2,1)S(1)}, bf16[2,6,128,128]{3,2,1,0:T(8,128)(2,1)S(1)}, u32[]{:S(2)}, u32[]{:S(2)}) collective-permute-start(bf16[2,6,128,128]{3,2,1,0:T(8,128)(2,1)S(1)} %get-tuple-element.26), channel_id=1, source_target_pairs={{0,1},{1,2},{2,3},{3,4},{4,5},{5,6},{6,7},{7,0},{8,9},{9,10},{10,1... | collective-permute-start | bytes 1179656 | tf_op jit(solution)/shard_map/ppermute | solution.py:570
  15.8 18.1 %copy-start = (bf16[2,4,2,128,128]{4,3,2,1,0:T(8,128)(2,1)S(1)}, bf16[2,4,2,128,128]{4,3,2,1,0:T(8,128)(2,1)}, u32[]{:S(2)}) copy-start(bf16[2,4,2,128,128]{4,3,2,1,0:T(8,128)(2,1)} %param.10) | copy-start | bytes 1572868
  16.5 1.6 %collective-permute-start.2 = (f32[4,4,2,16,128]{4,3,2,1,0:T(8,128)S(1)}, f32[4,4,2,16,128]{4,3,2,1,0:T(8,128)S(1)}, u32[]{:S(2)}, u32[]{:S(2)}) collective-permute-start(f32[4,4,2,16,128]{4,3,2,1,0:T(8,128)S(1)} %get-tuple-element.30), channel_id=1, source_target_pairs={{0,1},{1,0},{2,3},{3,2},{4,5},{5,4},{6,7},{7,6},{8,9},{9,8},{10,11... | collective-permute-start | bytes 786440 | tf_op jit(solution)/shard_map/ppermute | solution.py:576
  18.2 5.0 %collective-permute-start.3 = (bf16[5,2,16,128]{3,2,1,0:T(8,128)(2,1)S(1)}, bf16[5,2,16,128]{3,2,1,0:T(8,128)(2,1)S(1)}, u32[]{:S(2)}, u32[]{:S(2)}) collective-permute-start(bf16[5,2,16,128]{3,2,1,0:T(8,128)(2,1)S(1)} %get-tuple-element.32), channel_id=1, source_target_pairs={{0,6},{1,7},{2,4},{3,5},{4,2},{5,3},{6,0},{7,1},{8,14},{9,15},{10,... | collective-permute-start | bytes 122888 | tf_op jit(solution)/shard_map/ppermute | solution.py:582
  19.9 4.0 %collective-permute-start.4 = (bf16[5,2,16,128]{3,2,1,0:T(8,128)(2,1)S(1)}, bf16[5,2,16,128]{3,2,1,0:T(8,128)(2,1)S(1)}, u32[]{:S(2)}, u32[]{:S(2)}) collective-permute-start(bf16[5,2,16,128]{3,2,1,0:T(8,128)(2,1)S(1)} %get-tuple-element.33), channel_id=1, source_target_pairs={{0,2},{1,3},{2,0},{3,1},{4,6},{5,7},{6,4},{7,5},{8,10},{9,11},{10,... | collective-permute-start | bytes 122888 | tf_op jit(solution)/shard_map/ppermute | solution.py:582
  21.3 4.0 %collective-permute-start.5 = (bf16[5,2,16,128]{3,2,1,0:T(8,128)(2,1)S(1)}, bf16[5,2,16,128]{3,2,1,0:T(8,128)(2,1)S(1)}, u32[]{:S(2)}, u32[]{:S(2)}) collective-permute-start(bf16[5,2,16,128]{3,2,1,0:T(8,128)(2,1)S(1)} %get-tuple-element.34), channel_id=1, source_target_pairs={{0,4},{1,5},{2,6},{3,7},{4,0},{5,1},{6,2},{7,3},{8,12},{9,13},{10,... | collective-permute-start | bytes 122888 | tf_op jit(solution)/shard_map/ppermute | solution.py:582
  25.4 5.8 %collective-permute-start.8 = (bf16[4,2,16,128]{3,2,1,0:T(8,128)(2,1)S(1)}, bf16[4,2,16,128]{3,2,1,0:T(8,128)(2,1)S(1)}, u32[]{:S(2)}, u32[]{:S(2)}) collective-permute-start(bf16[4,2,16,128]{3,2,1,0:T(8,128)(2,1)S(1)} %total.1.refs_0_), channel_id=1, source_target_pairs={{0,24},{8,16},{16,8},{24,0},{1,25},{9,17},{17,9},{25,1},{2,26},{10... | collective-permute-start | bytes 98312 | tf_op jit(solution)/shard_map/ppermute | solution.py:587
  29.0 4.8 %collective-permute-start.7 = (bf16[4,2,16,128]{3,2,1,0:T(8,128)(2,1)S(1)}, bf16[4,2,16,128]{3,2,1,0:T(8,128)(2,1)S(1)}, u32[]{:S(2)}, u32[]{:S(2)}) collective-permute-start(bf16[4,2,16,128]{3,2,1,0:T(8,128)(2,1)S(1)} %total.1.refs_0_), channel_id=1, source_target_pairs={{0,16},{8,24},{16,0},{24,8},{1,17},{9,25},{17,1},{25,9},{2,18},{10... | collective-permute-start | bytes 98312 | tf_op jit(solution)/shard_map/ppermute | solution.py:587
  29.0 4.8 %collective-permute-start.6 = (bf16[4,2,16,128]{3,2,1,0:T(8,128)(2,1)S(1)}, bf16[4,2,16,128]{3,2,1,0:T(8,128)(2,1)S(1)}, u32[]{:S(2)}, u32[]{:S(2)}) collective-permute-start(bf16[4,2,16,128]{3,2,1,0:T(8,128)(2,1)S(1)} %total.1.refs_0_), channel_id=1, source_target_pairs={{0,8},{8,0},{16,24},{24,16},{1,9},{9,1},{17,25},{25,17},{2,10},{10... | collective-permute-start | bytes 98312 | tf_op jit(solution)/shard_map/ppermute | solution.py:587

commit v8 on v7

--- a/solution.py
+++ b/solution.py
@@ -402,16 +402,16 @@
 
 
 def edge_kernel(count, rows, cores, low_ref, high_ref, lhs_ref, sums_ref, keep_ref, send_ref, tot_ref):
+    total = None
+    for half in range(low_ref.shape[0]):
+        sides = [joined([ref[half, k] for k in range(ref.shape[1])]) for ref in (low_ref, high_ref, lhs_ref)]
+        got = nt_dot(jnp.concatenate(sides[:2], axis=0), sides[2])
+        total = got if total is None else total + got
     reals, imags = [], []
-    for halo_ref in (low_ref, high_ref):
-        total = None
-        for half in range(halo_ref.shape[0]):
-            sides = [joined([ref[half, k] for k in range(ref.shape[1])]) for ref in (halo_ref, lhs_ref)]
-            got = nt_dot(*sides)
-            total = got if total is None else total + got
-        mid = total.shape[0] // 2
-        reals.append(total[:mid, :count] + total[mid:, count:])
-        imags.append(total[:mid, count:] - total[mid:, :count])
+    mid = count // 2
+    for at in (0, count):
+        reals.append(total[at : at + mid, :count] + total[at + mid : at + count, count:])
+        imags.append(total[at : at + mid, count:] - total[at + mid : at + count, :count])
     real, imag = jnp.concatenate(reals, axis=0), jnp.concatenate(imags, axis=0)
     tot_ref[0] = 0.5 * (real - real.T)
     tot_ref[1] = 0.5 * (imag + imag.T)
@@ -493,9 +493,11 @@
     )(*parts)
 
 
-def dress_kernel(groups, slots, taus, rows, count, table_ref, per_ref, *refs):
+def dress_kernel(groups, slots, taus, rows, count, table_any, per_ref, *refs):
     slab_refs = refs[:groups]
-    out_ref, lhs_ref, prod_ref = refs[groups:]
+    out_hbm, lhs_ref, prod_ref, stage_ref, table_ref, sems = refs[groups:]
+    table_copy = pltpu.make_async_copy(table_any, table_ref, sems.at[groups])
+    table_copy.start()
     me = lax.axis_index("tm")
     for step in range(groups):
         group = me ^ step
@@ -506,30 +508,39 @@
     left = lhs_ref[...]
     for tau in range(taus):
         real, imag = per_ref[tau, 0], per_ref[tau, 1]
-        right = jnp.concatenate(
-            [jnp.concatenate([real, imag], axis=1), jnp.concatenate([-imag, real], axis=1)], axis=0
-        )
+        right = jnp.concatenate([joined([real, imag]), joined([-imag, real])], axis=0)
         got = jnp.dot(left, right, preferred_element_type=F32).astype(BF16)
         for piece in range(groups * OPS):
-            prod_ref[tau * groups * OPS + piece] = got[piece * rows : (piece + 1) * rows]
-    prod_ref[taus * groups * OPS] = jnp.zeros((rows, 2 * count), BF16)
+            for half in range(2):
+                prod_ref[tau * groups * OPS + piece, half] = got[
+                    piece * rows : (piece + 1) * rows, half * count : (half + 1) * count
+                ]
+    prod_ref[taus * groups * OPS] = jnp.zeros((2, rows, count), BF16)
+    table_copy.wait()
+    copies = []
     for group in range(groups):
         for slot in range(slots):
-            piece = prod_ref[table_ref[0, group * slots + slot]]
-            out_ref[group, slot, 0] = piece[:, :count]
-            out_ref[group, slot, 1] = piece[:, count:]
+            stage_ref[group, slot] = prod_ref[table_ref[0, group * slots + slot]]
+        copies.append(pltpu.make_async_copy(stage_ref.at[group], out_hbm.at[group], sems.at[group]))
+        copies[group].start()
+    for copy in copies:
+        copy.wait()
 
 
 def dress(table, per, slabs, groups, slots, rows, count):
     taus = per.shape[0]
+    shape = (groups, slots, 2, rows, count)
     return pl.pallas_call(
         partial(dress_kernel, groups, slots, taus, rows, count),
-        in_specs=[sspec(), vspec()] + [vspec()] * groups,
-        out_specs=vspec(),
-        out_shape=jax.ShapeDtypeStruct((groups, slots, 2, rows, count), BF16),
+        in_specs=[pl.BlockSpec(memory_space=pl.ANY), vspec()] + [vspec()] * groups,
+        out_specs=pl.BlockSpec(memory_space=pltpu.HBM),
+        out_shape=jax.ShapeDtypeStruct(shape, BF16),
         scratch_shapes=[
             VMEM((groups * OPS * rows, 2 * count), BF16),
-            VMEM((taus * groups * OPS + 1, rows, 2 * count), BF16),
+            VMEM((taus * groups * OPS + 1, 2, rows, count), BF16),
+            VMEM(shape, BF16),
+            SMEM(table.shape, jnp.int32),
+            pltpu.SemaphoreType.DMA((groups + 1,)),
         ],
         compiler_params=limit(8),
         cost_estimate=cost(10**9, 2 * 10**6),

time: 35.9 us -> 35.2 us (0.981)
  Pallas kernels: 15.2 us -> 14.5 us
    pallas_call x1, Pallas kernels: 1.9 us -> 1.46 us  [dress(): pl.pallas_call(partial(dress_kernel, groups, slots, taus, rows, count), i...]
  transfers between devices with their start and end apart: 9 -> 9, of which waited for: 6 -> 6; matrix products, arithmetic and copies ran while one was open for 0% -> 0% of each run, Pallas kernels for 29% -> 30%
where the time goes in v8:
time: 35.2 us; the launch traced here: 35.1 us
  Pallas kernels  14.5 us (41%)
  starting transfers between devices  11.3 us (32%)
  waiting for transfers between devices  9.14 us (26%)
    pallas_call x1, Pallas kernels, gram(): pl.pallas_call(partial(gram_kernel, count, tiles, planes, lx, groups, slo...  8.41 us
    ppermute x3, starting transfers between devices, fast_shards(): lax.ppermute(own, 'tm', [(i, i ^ step) for i in range(groups)])  4.45 us
    pallas_call x2, Pallas kernels, rim_plane(): pl.pallas_call(partial(rim_kernel, tiles, planes, 0 if leads else chunks,...  4.09 us
    ppermute x3, waiting for transfers between devices, fast_shards(): lax.ppermute(own, 'tm', [(i, i ^ step) for i in range(groups)])  4.03 us
    ppermute x3, waiting for transfers between devices, fast_shards(): lax.ppermute(parts[step], 'space', [(i, i ^ step * cores) for i in range(...  3.61 us
    ppermute x3, starting transfers between devices, fast_shards(): lax.ppermute(parts[step], 'space', [(i, i ^ step * cores) for i in range(...  3.55 us
    ppermute x1, starting transfers between devices, fast_shards(): halos.append(lax.ppermute(rim, 'space', up))  2.64 us
    ppermute x1, waiting for transfers between devices, fast_shards(): got = lax.ppermute(send, 'space', [(i, i ^ 1) for i in range(space_size)])  1.5 us
  transfers between devices with their start and end apart: 9, of which 6 were waited for; matrix products, arithmetic and copies ran while one was open for 0% of the time, Pallas kernels for 30%

profile of v8, /device:TPU:0, one launch (start us, length us, event | category | flops | bytes accessed | tf_op | source)
XLA Modules:
  0.0 35.1 jit_solution(5856630496649731014)
XLA Ops:
  0.0 2.1 %rim.1 = (bf16[2,6,128,128]{3,2,1,0:T(8,128)(2,1)S(1)}, bf16[6144,128]{1,0:T(8,128)(2,1)S(1)}, f32[4,27,8,128]{3,2,1,0:T(8,128)S(1)}) custom-call(bf16[12288,128]{1,0:T(8,128)(2,1)} %bitcast.21, f32[864,128]{1,0:T(8,128)} %bitcast.23), custom_call_target="tpu_custom_call" | custom-call | flops 100000000 | bytes 2000000 | tf_op jit(solution)/shard_map/rim/pallas_call | solution.py:130
  2.1 0.5 %collective-permute-start = (bf16[2,6,128,128]{3,2,1,0:T(8,128)(2,1)S(1)}, bf16[2,6,128,128]{3,2,1,0:T(8,128)(2,1)S(1)}, u32[]{:S(2)}, u32[]{:S(2)}) collective-permute-start(bf16[2,6,128,128]{3,2,1,0:T(8,128)(2,1)S(1)} %get-tuple-element.25), channel_id=1, source_target_pairs={{0,1},{1,2},{2,3},{3,4},{4,5},{5,6},{6,7},{7,0},{8,9},{9,10},{10,1... | collective-permute-start | bytes 1179656 | tf_op jit(solution)/shard_map/ppermute | solution.py:579
  2.6 0.0 copy-start.1
  2.6 0.0 copy-start.5
  2.6 2.0 %rest.1 = (bf16[2,6,128,128]{3,2,1,0:T(8,128)(2,1)S(1)}, bf16[6144,128]{1,0:T(8,128)(2,1)S(1)}, f32[864,128]{1,0:T(8,128)S(1)}) custom-call(bf16[12288,128]{1,0:T(8,128)(2,1)} %bitcast.22, f32[864,128]{1,0:T(8,128)} %bitcast.24, f32[4,27,8,128]{3,2,1,0:T(8,128)S(1)} %get-tuple-element.21.refs_0_), custom_call_target="tpu_custom_call" | custom-call | flops 100000000 | bytes 2000000 | tf_op jit(solution)/shard_map/rest/pallas_call | solution.py:130
  4.7 2.6 %collective-permute-start.1 = (bf16[2,6,128,128]{3,2,1,0:T(8,128)(2,1)S(1)}, bf16[2,6,128,128]{3,2,1,0:T(8,128)(2,1)S(1)}, u32[]{:S(2)}, u32[]{:S(2)}) collective-permute-start(bf16[2,6,128,128]{3,2,1,0:T(8,128)(2,1)S(1)} %get-tuple-element.26), channel_id=1, source_target_pairs={{0,1},{1,2},{2,3},{3,4},{4,5},{5,6},{6,7},{7,0},{8,9},{9,10},{10,1... | collective-permute-start | bytes 1179656 | tf_op jit(solution)/shard_map/ppermute | solution.py:581
  7.3 0.0 copy-done.1
  7.3 0.0 copy-done.2
  7.3 0.0 copy-done.3
  7.3 0.0 copy-done.4
  7.3 0.0 copy-done.5
  7.3 8.4 %gram.1 = (f32[4,2,128,128]{3,2,1,0:T(8,128)S(1)}, bf16[2,6,256,128]{3,2,1,0:T(8,128)(2,1)S(1)}, s32[1,128]{1,0:T(1,128)S(1)}) custom-call(bf16[6144,128]{1,0:T(8,128)(2,1)S(1)} %get-tuple-element.20.low_ref, bf16[6144,128]{1,0:T(8,128)(2,1)S(1)} %get-tuple-element.22.high_ref, f32[864,128]{1,0:T(8,128)S(1)} %get-tuple-element.23.u_ref, f32[64]{0:T(128)S(1)} %copy-done.5, ...), custom_call_target="tpu_custom_call" | custom-call | flops 8000000000 | bytes 5000000 | tf_op jit(solution)/shard_map/gram/pallas_call | solution.py:382
  15.8 0.0 collective-permute-done.low_ref
  15.8 0.0 collective-permute-done.1.high_ref
  15.8 0.0 copy-start
  15.8 0.5 %edge.1 = (f32[4,4,2,16,128]{4,3,2,1,0:T(8,128)S(1)}, f32[4,4,2,16,128]{4,3,2,1,0:T(8,128)S(1)}) custom-call(bf16[2,6,128,128]{3,2,1,0:T(8,128)(2,1)S(1)} %collective-permute-done.low_ref, bf16[2,6,128,128]{3,2,1,0:T(8,128)(2,1)S(1)} %collective-permute-done.1.high_ref, bf16[2,6,256,128]{3,2,1,0:T(8,128)(2,1)S(1)} %get-tuple-element.27.lhs_ref, ...), custom_call_target="tpu_custom_call" | custom-call | flops 1000000000 | bytes 3000000 | tf_op jit(solution)/shard_map/edge/pallas_call | solution.py:432
  16.3 0.1 collective-permute-start.2
  16.4 1.5 %collective-permute-done.2.got_ref = f32[4,4,2,16,128]{4,3,2,1,0:T(8,128)S(1)} collective-permute-done((f32[4,4,2,16,128]{4,3,2,1,0:T(8,128)S(1)}, f32[4,4,2,16,128]{4,3,2,1,0:T(8,128)S(1)}, u32[]{:S(2)}, u32[]{:S(2)}) %collective-permute-start.2) | collective-permute-done | bytes 262176 | tf_op jit(solution)/shard_map/ppermute | solution.py:587
  17.9 1.7 %collective-permute-start.3 = (bf16[5,2,16,128]{3,2,1,0:T(8,128)(2,1)S(1)}, bf16[5,2,16,128]{3,2,1,0:T(8,128)(2,1)S(1)}, u32[]{:S(2)}, u32[]{:S(2)}) collective-permute-start(bf16[5,2,16,128]{3,2,1,0:T(8,128)(2,1)S(1)} %get-tuple-element.32), channel_id=1, source_target_pairs={{0,6},{1,7},{2,4},{3,5},{4,2},{5,3},{6,0},{7,1},{8,14},{9,15},{10,... | collective-permute-start | bytes 122888 | tf_op jit(solution)/shard_map/ppermute | solution.py:593
  19.7 1.4 %collective-permute-start.4 = (bf16[5,2,16,128]{3,2,1,0:T(8,128)(2,1)S(1)}, bf16[5,2,16,128]{3,2,1,0:T(8,128)(2,1)S(1)}, u32[]{:S(2)}, u32[]{:S(2)}) collective-permute-start(bf16[5,2,16,128]{3,2,1,0:T(8,128)(2,1)S(1)} %get-tuple-element.33), channel_id=1, source_target_pairs={{0,2},{1,3},{2,0},{3,1},{4,6},{5,7},{6,4},{7,5},{8,10},{9,11},{10,... | collective-permute-start | bytes 122888 | tf_op jit(solution)/shard_map/ppermute | solution.py:593
  21.1 0.4 %collective-permute-start.5 = (bf16[5,2,16,128]{3,2,1,0:T(8,128)(2,1)S(1)}, bf16[5,2,16,128]{3,2,1,0:T(8,128)(2,1)S(1)}, u32[]{:S(2)}, u32[]{:S(2)}) collective-permute-start(bf16[5,2,16,128]{3,2,1,0:T(8,128)(2,1)S(1)} %get-tuple-element.34), channel_id=1, source_target_pairs={{0,4},{1,5},{2,6},{3,7},{4,0},{5,1},{6,2},{7,3},{8,12},{9,13},{10,... | collective-permute-start | bytes 122888 | tf_op jit(solution)/shard_map/ppermute | solution.py:593
  21.5 1.5 %collective-permute-done.3.refs_0_ = bf16[5,2,16,128]{3,2,1,0:T(8,128)(2,1)S(1)} collective-permute-done((bf16[5,2,16,128]{3,2,1,0:T(8,128)(2,1)S(1)}, bf16[5,2,16,128]{3,2,1,0:T(8,128)(2,1)S(1)}, u32[]{:S(2)}, u32[]{:S(2)}) %collective-permute-start.3) | collective-permute-done | bytes 40992 | tf_op jit(solution)/shard_map/ppermute | solution.py:593
  23.0 0.7 %collective-permute-done.4.refs_1_ = bf16[5,2,16,128]{3,2,1,0:T(8,128)(2,1)S(1)} collective-permute-done((bf16[5,2,16,128]{3,2,1,0:T(8,128)(2,1)S(1)}, bf16[5,2,16,128]{3,2,1,0:T(8,128)(2,1)S(1)}, u32[]{:S(2)}, u32[]{:S(2)}) %collective-permute-start.4) | collective-permute-done | bytes 40992 | tf_op jit(solution)/shard_map/ppermute | solution.py:593
  23.7 1.4 %collective-permute-done.5.refs_2_ = bf16[5,2,16,128]{3,2,1,0:T(8,128)(2,1)S(1)} collective-permute-done((bf16[5,2,16,128]{3,2,1,0:T(8,128)(2,1)S(1)}, bf16[5,2,16,128]{3,2,1,0:T(8,128)(2,1)S(1)}, u32[]{:S(2)}, u32[]{:S(2)}) %collective-permute-start.5) | collective-permute-done | bytes 40992 | tf_op jit(solution)/shard_map/ppermute | solution.py:593
  25.1 3.7 %collective-permute-start.8 = (bf16[4,2,16,128]{3,2,1,0:T(8,128)(2,1)S(1)}, bf16[4,2,16,128]{3,2,1,0:T(8,128)(2,1)S(1)}, u32[]{:S(2)}, u32[]{:S(2)}) collective-permute-start(bf16[4,2,16,128]{3,2,1,0:T(8,128)(2,1)S(1)} %total.1.refs_0_), channel_id=1, source_target_pairs={{0,24},{8,16},{16,8},{24,0},{1,25},{9,17},{17,9},{25,1},{2,26},{10... | collective-permute-start | bytes 98312 | tf_op jit(solution)/shard_map/ppermute | solution.py:598
  28.8 0.0 collective-permute-start.7
  28.8 0.8 %collective-permute-start.6 = (bf16[4,2,16,128]{3,2,1,0:T(8,128)(2,1)S(1)}, bf16[4,2,16,128]{3,2,1,0:T(8,128)(2,1)S(1)}, u32[]{:S(2)}, u32[]{:S(2)}) collective-permute-start(bf16[4,2,16,128]{3,2,1,0:T(8,128)(2,1)S(1)} %total.1.refs_0_), channel_id=1, source_target_pairs={{0,8},{8,0},{16,24},{24,16},{1,9},{9,1},{17,25},{25,17},{2,10},{10... | collective-permute-start | bytes 98312 | tf_op jit(solution)/shard_map/ppermute | solution.py:598
  29.6 1.3 %collective-permute-done.8.refs_3_ = bf16[4,2,16,128]{3,2,1,0:T(8,128)(2,1)S(1)} collective-permute-done((bf16[4,2,16,128]{3,2,1,0:T(8,128)(2,1)S(1)}, bf16[4,2,16,128]{3,2,1,0:T(8,128)(2,1)S(1)}, u32[]{:S(2)}, u32[]{:S(2)}) %collective-permute-start.8) | collective-permute-done | bytes 32800 | tf_op jit(solution)/shard_map/ppermute | solution.py:598
  30.9 2.7 %collective-permute-done.7.refs_2_ = bf16[4,2,16,128]{3,2,1,0:T(8,128)(2,1)S(1)} collective-permute-done((bf16[4,2,16,128]{3,2,1,0:T(8,128)(2,1)S(1)}, bf16[4,2,16,128]{3,2,1,0:T(8,128)(2,1)S(1)}, u32[]{:S(2)}, u32[]{:S(2)}) %collective-permute-start.7) | collective-permute-done | bytes 32800 | tf_op jit(solution)/shard_map/ppermute | solution.py:598
  33.6 0.0 collective-permute-done.6.refs_1_
  33.6 0.0 copy-done
  33.6 1.5 %dress.1 = bf16[4,18,2,16,128]{4,3,2,1,0:T(8,128)(2,1)} custom-call(s32[1,128]{1,0:T(1,128)S(1)} %get-tuple-element.24.table_any, bf16[8,2,128,128]{3,2,1,0:T(8,128)(2,1)S(1)} %bitcast.16, bf16[4,2,16,128]{3,2,1,0:T(8,128)(2,1)S(1)} %total.1.refs_0_, bf16[4,2,16,128]{3,2,1,0:T(8,128)(2,1)S(1)} %collective-permute-done.6.refs_1_, ...), custom_call_target="tpu_custom_call" | custom-call | flops 1000000000 | bytes 2000000 | tf_op jit(solution)/shard_map/dress/pallas_call | solution.py:533
  (5 shorter events, 0.1 us)
Async XLA Ops:
  2.1 13.7 %collective-permute-start = (bf16[2,6,128,128]{3,2,1,0:T(8,128)(2,1)S(1)}, bf16[2,6,128,128]{3,2,1,0:T(8,128)(2,1)S(1)}, u32[]{:S(2)}, u32[]{:S(2)}) collective-permute-start(bf16[2,6,128,128]{3,2,1,0:T(8,128)(2,1)S(1)} %get-tuple-element.25), channel_id=1, source_target_pairs={{0,1},{1,2},{2,3},{3,4},{4,5},{5,6},{6,7},{7,0},{8,9},{9,10},{10,1... | collective-permute-start | bytes 1179656 | tf_op jit(solution)/shard_map/ppermute | solution.py:579
  2.6 4.7 %copy-start.1 = (s32[96,1]{0,1:T(1,128)S(1)}, s32[96,1]{0,1:T(1,128)}, u32[]{:S(2)}) copy-start(s32[96,1]{0,1:T(1,128)} %param.11) | copy-start | bytes 1156
  2.6 4.7 %copy-start.2 = (s32[96]{0:T(128)S(1)}, s32[96]{0:T(128)}, u32[]{:S(2)}) copy-start(s32[96]{0:T(128)} %param.12) | copy-start | bytes 1156
  2.6 4.7 %copy-start.3 = (s32[96]{0:T(128)S(1)}, s32[96]{0:T(128)}, u32[]{:S(2)}) copy-start(s32[96]{0:T(128)} %param.13) | copy-start | bytes 1156
  2.6 4.7 %copy-start.4 = (s32[96]{0:T(128)S(1)}, s32[96]{0:T(128)}, u32[]{:S(2)}) copy-start(s32[96]{0:T(128)} %param.14) | copy-start | bytes 1156
  2.6 4.7 %copy-start.5 = (f32[64]{0:T(128)S(1)}, f32[64]{0:T(128)}, u32[]{:S(2)}) copy-start(f32[64]{0:T(128)} %constant.2.clone.phase_ref) | copy-start | bytes 772
  4.7 11.1 %collective-permute-start.1 = (bf16[2,6,128,128]{3,2,1,0:T(8,128)(2,1)S(1)}, bf16[2,6,128,128]{3,2,1,0:T(8,128)(2,1)S(1)}, u32[]{:S(2)}, u32[]{:S(2)}) collective-permute-start(bf16[2,6,128,128]{3,2,1,0:T(8,128)(2,1)S(1)} %get-tuple-element.26), channel_id=1, source_target_pairs={{0,1},{1,2},{2,3},{3,4},{4,5},{5,6},{6,7},{7,0},{8,9},{9,10},{10,1... | collective-permute-start | bytes 1179656 | tf_op jit(solution)/shard_map/ppermute | solution.py:581
  15.8 17.8 %copy-start = (bf16[2,4,2,128,128]{4,3,2,1,0:T(8,128)(2,1)S(1)}, bf16[2,4,2,128,128]{4,3,2,1,0:T(8,128)(2,1)}, u32[]{:S(2)}) copy-start(bf16[2,4,2,128,128]{4,3,2,1,0:T(8,128)(2,1)} %param.10) | copy-start | bytes 1572868
  16.3 1.6 %collective-permute-start.2 = (f32[4,4,2,16,128]{4,3,2,1,0:T(8,128)S(1)}, f32[4,4,2,16,128]{4,3,2,1,0:T(8,128)S(1)}, u32[]{:S(2)}, u32[]{:S(2)}) collective-permute-start(f32[4,4,2,16,128]{4,3,2,1,0:T(8,128)S(1)} %get-tuple-element.30), channel_id=1, source_target_pairs={{0,1},{1,0},{2,3},{3,2},{4,5},{5,4},{6,7},{7,6},{8,9},{9,8},{10,11... | collective-permute-start | bytes 786440 | tf_op jit(solution)/shard_map/ppermute | solution.py:587
  17.9 5.0 %collective-permute-start.3 = (bf16[5,2,16,128]{3,2,1,0:T(8,128)(2,1)S(1)}, bf16[5,2,16,128]{3,2,1,0:T(8,128)(2,1)S(1)}, u32[]{:S(2)}, u32[]{:S(2)}) collective-permute-start(bf16[5,2,16,128]{3,2,1,0:T(8,128)(2,1)S(1)} %get-tuple-element.32), channel_id=1, source_target_pairs={{0,6},{1,7},{2,4},{3,5},{4,2},{5,3},{6,0},{7,1},{8,14},{9,15},{10,... | collective-permute-start | bytes 122888 | tf_op jit(solution)/shard_map/ppermute | solution.py:593
  19.7 4.0 %collective-permute-start.4 = (bf16[5,2,16,128]{3,2,1,0:T(8,128)(2,1)S(1)}, bf16[5,2,16,128]{3,2,1,0:T(8,128)(2,1)S(1)}, u32[]{:S(2)}, u32[]{:S(2)}) collective-permute-start(bf16[5,2,16,128]{3,2,1,0:T(8,128)(2,1)S(1)} %get-tuple-element.33), channel_id=1, source_target_pairs={{0,2},{1,3},{2,0},{3,1},{4,6},{5,7},{6,4},{7,5},{8,10},{9,11},{10,... | collective-permute-start | bytes 122888 | tf_op jit(solution)/shard_map/ppermute | solution.py:593
  21.1 4.0 %collective-permute-start.5 = (bf16[5,2,16,128]{3,2,1,0:T(8,128)(2,1)S(1)}, bf16[5,2,16,128]{3,2,1,0:T(8,128)(2,1)S(1)}, u32[]{:S(2)}, u32[]{:S(2)}) collective-permute-start(bf16[5,2,16,128]{3,2,1,0:T(8,128)(2,1)S(1)} %get-tuple-element.34), channel_id=1, source_target_pairs={{0,4},{1,5},{2,6},{3,7},{4,0},{5,1},{6,2},{7,3},{8,12},{9,13},{10,... | collective-permute-start | bytes 122888 | tf_op jit(solution)/shard_map/ppermute | solution.py:593
  25.1 5.8 %collective-permute-start.8 = (bf16[4,2,16,128]{3,2,1,0:T(8,128)(2,1)S(1)}, bf16[4,2,16,128]{3,2,1,0:T(8,128)(2,1)S(1)}, u32[]{:S(2)}, u32[]{:S(2)}) collective-permute-start(bf16[4,2,16,128]{3,2,1,0:T(8,128)(2,1)S(1)} %total.1.refs_0_), channel_id=1, source_target_pairs={{0,24},{8,16},{16,8},{24,0},{1,25},{9,17},{17,9},{25,1},{2,26},{10... | collective-permute-start | bytes 98312 | tf_op jit(solution)/shard_map/ppermute | solution.py:598
  28.8 4.8 %collective-permute-start.7 = (bf16[4,2,16,128]{3,2,1,0:T(8,128)(2,1)S(1)}, bf16[4,2,16,128]{3,2,1,0:T(8,128)(2,1)S(1)}, u32[]{:S(2)}, u32[]{:S(2)}) collective-permute-start(bf16[4,2,16,128]{3,2,1,0:T(8,128)(2,1)S(1)} %total.1.refs_0_), channel_id=1, source_target_pairs={{0,16},{8,24},{16,0},{24,8},{1,17},{9,25},{17,1},{25,9},{2,18},{10... | collective-permute-start | bytes 98312 | tf_op jit(solution)/shard_map/ppermute | solution.py:598
  28.8 4.8 %collective-permute-start.6 = (bf16[4,2,16,128]{3,2,1,0:T(8,128)(2,1)S(1)}, bf16[4,2,16,128]{3,2,1,0:T(8,128)(2,1)S(1)}, u32[]{:S(2)}, u32[]{:S(2)}) collective-permute-start(bf16[4,2,16,128]{3,2,1,0:T(8,128)(2,1)S(1)} %total.1.refs_0_), channel_id=1, source_target_pairs={{0,8},{8,0},{16,24},{24,16},{1,9},{9,1},{17,25},{25,17},{2,10},{10... | collective-permute-start | bytes 98312 | tf_op jit(solution)/shard_map/ppermute | solution.py:598
